TPU v7x, 32 devices: a whole 2x2x4 slice. The times are simulated.
32 devices in a mesh: fsdp: 4 (over z), ctx: 2 (over core), tp: 4 (over y, x).
Axes of the slice: x: 2, y: 2, z: 4, core: 2. Of those that a mesh axis runs over, the one named last changes fastest.
Arguments:
- characters: bfloat16 [8192, 16, 256], P(('fsdp', 'ctx', 'tp')), may hold values from -6 to 6
- counts: int32 [8192], P(('fsdp', 'ctx', 'tp')), may hold values from 1 to 16, as said below
- words_in: bfloat16 [8192, 512], P(('fsdp', 'ctx', 'tp')), may hold values from -6 to 6
- cotangent: bfloat16 [8192, 512], P(('fsdp', 'ctx', 'tp')), may hold values from -6 to 6
- char_prenorm: bfloat16 [256], P('fsdp'), may hold values from 0.099609375 to 1.8984375
- char_qkv: bfloat16 [256, 768], P('fsdp'), may hold values from -0.5 to 0.5
- char_out: bfloat16 [256, 256], P('fsdp'), may hold values from -0.375 to 0.375
- char_midnorm: bfloat16 [256], P('fsdp'), may hold values from 0.099609375 to 1.8984375
- char_up: bfloat16 [256, 1024], P('fsdp'), may hold values from -0.375 to 0.375
- char_down: bfloat16 [1024, 256], P('fsdp'), may hold values from -0.1875 to 0.1875
- pool_query: bfloat16 [256], P('fsdp'), may hold values from -0.375 to 0.375
- char_proj: bfloat16 [256, 512], P('fsdp'), may hold values from -0.375 to 0.375
- word_prenorm: bfloat16 [512], P('fsdp'), may hold values from 0.099609375 to 1.8984375
- word_qkv: bfloat16 [512, 3, 512], P('fsdp', None, 'tp'), may hold values from -0.375 to 0.375
- word_out: bfloat16 [512, 512], P('tp', 'fsdp'), may hold values from -0.5 to 0.5
- word_midnorm: bfloat16 [512], P('fsdp'), may hold values from 0.099609375 to 1.8984375
- word_up: bfloat16 [512, 2048], P('fsdp', 'tp'), may hold values from -0.25 to 0.25
- word_down: bfloat16 [2048, 512], P('tp', 'fsdp'), may hold values from -0.125 to 0.125
Outputs:
- block_out: bfloat16 [8192, 512], P(('fsdp', 'ctx', 'tp'))
- chars_grad: float32 [8192, 16, 256], P(('fsdp', 'ctx', 'tp'))
- words_grad: float32 [8192, 512], P(('fsdp', 'ctx', 'tp'))
- branch_rms: float32 [3, 8192], P(None, ('fsdp', 'ctx', 'tp'))
- char_prenorm_grad: float32 [256], P('fsdp')
- char_qkv_grad: float32 [256, 768], P('fsdp')
- char_out_grad: float32 [256, 256], P('fsdp')
- char_midnorm_grad: float32 [256], P('fsdp')
- char_up_grad: float32 [256, 1024], P('fsdp')
- char_down_grad: float32 [1024, 256], P('fsdp')
- pool_query_grad: float32 [256], P('fsdp')
- char_proj_grad: float32 [256, 512], P('fsdp')
- word_prenorm_grad: float32 [512], P('fsdp')
- word_qkv_grad: float32 [512, 3, 512], P('fsdp', None, 'tp')
- word_out_grad: float32 [512, 512], P('tp', 'fsdp')
- word_midnorm_grad: float32 [512], P('fsdp')
- word_up_grad: float32 [512, 2048], P('fsdp', 'tp')
- word_down_grad: float32 [2048, 512], P('tp', 'fsdp')
Inputs may be any that keep to these rules, and one draw needn't show every extreme that they name: `counts`: the number of real characters of each word; slots from it to 15 are padding.
All inputs are finite; a program needn't handle non-finite values.
Results may differ from a plain program's by a relative error of at most 0.03.
The roundings to bfloat16 on the way count: a program that leaves them out, or rounds other values in their place, can miss the bound.
Values may be sent and summed in bfloat16 or wider, within the bound.
A program may use at most 256 MiB of HBM per device.

v0:
```python
import math

import jax
import jax.numpy as jnp
from jax import lax
from jax.sharding import PartitionSpec as P

CHEADS = 4
HEADS = 8
BLOCK = 256


EPSILON = 1e-05
MASKED = -1e30


def layer_norm(row_values, gain_vec):
    centered = row_values - jnp.mean(row_values, axis=-1, keepdims=True)
    spread = jnp.mean(centered * centered, axis=-1, keepdims=True)
    return centered * lax.rsqrt(spread + EPSILON) * gain_vec


def pool_words(states, query_vec, present):
    logits = jnp.sum(states * query_vec, axis=-1)
    logits = jnp.where(present, logits, MASKED)
    weights = jax.nn.softmax(logits, axis=-1)
    return jnp.sum(weights[:, :, None] * states, axis=1)


def multiply(left_side, right_side):
    return jnp.dot(left_side, right_side, preferred_element_type=jnp.float32)


def outer_accum(left_side, right_side):
    return lax.dot_general(
        left_side, right_side, (((0,), (0,)), ((), ())), preferred_element_type=jnp.float32
    )


def back_project(left_side, right_side):
    return lax.dot_general(
        left_side, right_side, (((1,), (1,)), ((), ())), preferred_element_type=jnp.float32
    )


def root_mean(row_values):
    return jnp.sqrt(jnp.mean(row_values * row_values, axis=-1))


def rows_over_tp(row_values):
    return lax.all_gather(row_values, "tp", axis=0, tiled=True)


def grads_over_tp(row_values):
    return lax.all_gather(row_values, "tp", axis=0, tiled=True)


def partial_heads(low_rows, weight, local_rows):

    def rows_term(first_row, row_count):
        return multiply(low_rows, weight)

    return lax.psum_scatter(
        rows_term(jnp.int32(0), local_rows * lax.axis_size("tp")),
        "tp",
        scatter_dimension=0,
        tiled=True,
    )


def partial_inputs(low_rows, weight, local_rows):

    def rows_term(first_row, row_count):
        return back_project(low_rows, weight)

    return lax.psum_scatter(
        rows_term(jnp.int32(0), local_rows * lax.axis_size("tp")),
        "tp",
        scatter_dimension=0,
        tiled=True,
    )


def char_scores(packed, present, score_scale):
    scores = (
        jnp.einsum(
            "wqhe,wkhe->whqk", packed[:, :, 0], packed[:, :, 1], preferred_element_type=jnp.float32
        )
        * score_scale
    )
    scores = jnp.where(present[:, None, None, :], scores, MASKED)
    return jax.nn.softmax(scores, axis=-1)


def char_attend(packed, present, score_scale):
    attention = char_scores(packed, present, score_scale)
    return jnp.einsum(
        "whqk,wkhe->wqhe",
        attention.astype(jnp.bfloat16),
        packed[:, :, 2],
        preferred_element_type=jnp.float32,
    )


def char_attend_back(packed, present, score_scale, grad_low):
    attention = char_scores(packed, present, score_scale)
    grad_attention = jnp.einsum(
        "wqhe,wkhe->whqk", grad_low, packed[:, :, 2], preferred_element_type=jnp.float32
    )
    grad_value = jnp.einsum(
        "whqk,wqhe->wkhe",
        attention.astype(jnp.bfloat16),
        grad_low,
        preferred_element_type=jnp.float32,
    )
    shared = jnp.sum(attention * grad_attention, axis=-1, keepdims=True)
    grad_scores = (attention * (grad_attention - shared) * score_scale).astype(jnp.bfloat16)
    grad_query = jnp.einsum(
        "whqk,wkhe->wqhe", grad_scores, packed[:, :, 1], preferred_element_type=jnp.float32
    )
    grad_key = jnp.einsum(
        "whqk,wqhe->wkhe", grad_scores, packed[:, :, 0], preferred_element_type=jnp.float32
    )
    return jnp.stack([grad_query, grad_key, grad_value], axis=2)


def word_scores(query_blk, query_pos, key_rows, key_block, score_scale):
    scores = (
        jnp.einsum("qhe,khe->hqk", query_blk, key_rows, preferred_element_type=jnp.float32)
        * score_scale
    )
    allowed = key_block[None, :] <= (query_pos // BLOCK)[:, None]
    return jnp.where(allowed[None], scores, MASKED)


def local(
    characters,
    counts,
    words_in,
    cotangent,
    char_prenorm,
    char_qkv,
    char_out,
    char_midnorm,
    char_up,
    char_down,
    pool_query,
    char_proj,
    word_prenorm,
    word_qkv,
    word_out,
    word_midnorm,
    word_up,
    word_down,
):
    bfloat = jnp.bfloat16
    single = jnp.float32
    (
        char_prenorm,
        char_qkv,
        char_out,
        char_midnorm,
        char_up,
        char_down,
        pool_query,
        char_proj,
        word_prenorm,
        word_midnorm,
        word_qkv,
        word_up,
    ) = (
        lax.all_gather(char_prenorm, "fsdp", axis=0, tiled=True),
        lax.all_gather(char_qkv, "fsdp", axis=0, tiled=True),
        lax.all_gather(char_out, "fsdp", axis=0, tiled=True),
        lax.all_gather(char_midnorm, "fsdp", axis=0, tiled=True),
        lax.all_gather(char_up, "fsdp", axis=0, tiled=True),
        lax.all_gather(char_down, "fsdp", axis=0, tiled=True),
        lax.all_gather(pool_query, "fsdp", axis=0, tiled=True),
        lax.all_gather(char_proj, "fsdp", axis=0, tiled=True),
        lax.all_gather(word_prenorm, "fsdp", axis=0, tiled=True),
        lax.all_gather(word_midnorm, "fsdp", axis=0, tiled=True),
        lax.all_gather(word_qkv, "fsdp", axis=0, tiled=True),
        lax.all_gather(word_up, "fsdp", axis=0, tiled=True),
    )
    word_out, word_down = (
        lax.all_gather(word_out, "fsdp", axis=1, tiled=True),
        lax.all_gather(word_down, "fsdp", axis=1, tiled=True),
    )
    word_count, char_len, char_dim = characters.shape
    char_rows = word_count * char_len
    char_head = char_dim // CHEADS
    char_scale = char_head ** (-0.5)
    present = jnp.arange(char_len, dtype=jnp.int32)[None, :] < counts[:, None]
    embedded = characters.astype(single).reshape(char_rows, char_dim)
    gain_first = char_prenorm.astype(single)
    normed = layer_norm(embedded, gain_first).astype(bfloat)
    packed = (
        multiply(normed, char_qkv)
        .astype(bfloat)
        .reshape(word_count, char_len, 3, CHEADS, char_head)
    )
    char_mixed = char_attend(packed, present, char_scale)
    char_mixed_low = char_mixed.astype(bfloat).reshape(char_rows, char_dim)
    after_attn = embedded + multiply(char_mixed_low, char_out)
    gain_second = char_midnorm.astype(single)
    middle = layer_norm(after_attn, gain_second).astype(bfloat)
    char_hidden = multiply(middle, char_up)
    char_upper = jax.nn.gelu(char_hidden).astype(bfloat)
    after_mlp = after_attn + multiply(char_upper, char_down)
    states = after_mlp.reshape(word_count, char_len, char_dim)
    pool_vector = pool_query.astype(single)
    pooled = pool_words(states, pool_vector, present)
    pooled_low = pooled.astype(bfloat)
    start_rows = words_in.astype(single) + multiply(pooled_low, char_proj)
    local_rows, model_width = start_rows.shape
    ctx_rows = local_rows * lax.axis_size("tp")
    head_size = model_width // HEADS
    local_width = word_qkv.shape[2]
    heads_local = local_width // head_size
    word_scale = head_size ** (-0.5)
    gain_word_first = word_prenorm.astype(single)
    normed_first = layer_norm(start_rows, gain_word_first).astype(bfloat)
    gathered_first = rows_over_tp(normed_first)
    qkv_matrix = word_qkv.reshape(model_width, 3 * local_width)
    packed_word = (
        multiply(gathered_first, qkv_matrix)
        .astype(bfloat)
        .reshape(ctx_rows, 3, heads_local, head_size)
    )
    key_rows, value_rows = (
        lax.all_gather(packed_word[:, 1], "ctx", axis=0, tiled=True),
        lax.all_gather(packed_word[:, 2], "ctx", axis=0, tiled=True),
    )
    block_rows = math.gcd(ctx_rows, 512)
    block_count = ctx_rows // block_rows
    query_blocks = packed_word[:, 0].reshape(block_count, block_rows, heads_local, head_size)
    positions = lax.axis_index("ctx") * ctx_rows + jnp.arange(ctx_rows, dtype=jnp.int32)
    position_blocks = positions.reshape(block_count, block_rows)
    key_block = jnp.arange(key_rows.shape[0], dtype=jnp.int32) // BLOCK

    def attend_block(inputs_blk):
        query_blk, query_pos = inputs_blk
        scores = word_scores(query_blk, query_pos, key_rows, key_block, word_scale)
        row_top = jnp.max(scores, axis=-1, keepdims=True)
        exponent = jnp.exp(scores - row_top)
        row_total = jnp.sum(exponent, axis=-1, keepdims=True)
        attention = exponent / row_total
        log_total = (row_top + jnp.log(row_total))[..., 0]
        mixed_blk = jnp.einsum(
            "hqk,khe->qhe", attention.astype(bfloat), value_rows, preferred_element_type=single
        )
        return (mixed_blk, log_total)

    word_mixed, log_totals = lax.map(attend_block, (query_blocks, position_blocks))
    word_mixed_low = word_mixed.astype(bfloat).reshape(ctx_rows, local_width)
    attn_out = partial_heads(word_mixed_low, word_out, local_rows)
    after_word_attn = start_rows + attn_out
    gain_word_second = word_midnorm.astype(single)
    normed_second = layer_norm(after_word_attn, gain_word_second).astype(bfloat)
    gathered_second = rows_over_tp(normed_second)
    word_hidden = multiply(gathered_second, word_up)
    word_upper = jax.nn.gelu(word_hidden).astype(bfloat)
    mlp_out = partial_heads(word_upper, word_down, local_rows)
    final_rows = after_word_attn + mlp_out
    branch_rms = jnp.stack([root_mean(attn_out), root_mean(mlp_out), root_mean(final_rows)])
    grad_final = cotangent.astype(single)
    grad_mlp_rows = grads_over_tp(cotangent)
    word_down_grad = outer_accum(word_upper, grad_mlp_rows)
    grad_upper = back_project(grad_mlp_rows, word_down)
    grad_hidden = jax.vjp(jax.nn.gelu, word_hidden)[1](grad_upper)[0].astype(bfloat)
    word_up_grad = outer_accum(gathered_second, grad_hidden)
    grad_normed_second = partial_inputs(grad_hidden, word_up, local_rows)
    grad_after_ln, word_midnorm_grad = jax.vjp(layer_norm, after_word_attn, gain_word_second)[1](
        grad_normed_second
    )
    grad_after_attn = grad_final + grad_after_ln
    grad_attn_rows = grads_over_tp(grad_after_attn.astype(bfloat))
    word_out_grad = outer_accum(word_mixed_low, grad_attn_rows)
    grad_mixed = (
        back_project(grad_attn_rows, word_out)
        .astype(bfloat)
        .reshape(block_count, block_rows, heads_local, head_size)
    )

    def attend_back(sums_carry, inputs_blk):
        key_sum, value_sum = sums_carry
        query_blk, query_pos, log_total, grad_blk = inputs_blk
        scores = word_scores(query_blk, query_pos, key_rows, key_block, word_scale)
        attention = jnp.exp(scores - log_total[..., None])
        grad_attention = jnp.einsum(
            "qhe,khe->hqk", grad_blk, value_rows, preferred_element_type=single
        )
        value_part = jnp.einsum(
            "hqk,qhe->khe", attention.astype(bfloat), grad_blk, preferred_element_type=single
        )
        shared = jnp.sum(attention * grad_attention, axis=-1, keepdims=True)
        grad_scores = (attention * (grad_attention - shared) * word_scale).astype(bfloat)
        query_part = jnp.einsum(
            "hqk,khe->qhe", grad_scores, key_rows, preferred_element_type=single
        )
        key_part = jnp.einsum("hqk,qhe->khe", grad_scores, query_blk, preferred_element_type=single)
        return ((key_sum + key_part, value_sum + value_part), query_part)

    zero_keys = jnp.zeros(key_rows.shape, single)
    (key_grads, value_grads), query_grads = lax.scan(
        attend_back, (zero_keys, zero_keys), (query_blocks, position_blocks, log_totals, grad_mixed)
    )
    own_keys, own_values = (
        lax.psum_scatter(key_grads, "ctx", scatter_dimension=0, tiled=True),
        lax.psum_scatter(value_grads, "ctx", scatter_dimension=0, tiled=True),
    )
    grad_packed = (
        jnp.stack(
            [query_grads.reshape(ctx_rows, heads_local, head_size), own_keys, own_values], axis=1
        )
        .astype(bfloat)
        .reshape(ctx_rows, 3 * local_width)
    )
    word_qkv_grad = outer_accum(gathered_first, grad_packed).reshape(model_width, 3, local_width)
    grad_normed_first = partial_inputs(grad_packed, qkv_matrix, local_rows)
    grad_start_ln, word_prenorm_grad = jax.vjp(layer_norm, start_rows, gain_word_first)[1](
        grad_normed_first
    )
    grad_start = grad_after_attn + grad_start_ln
    grad_proj = grad_start.astype(bfloat)
    char_proj_grad = outer_accum(pooled_low, grad_proj)
    grad_pooled = back_project(grad_proj, char_proj)
    pool_pull = jax.vjp(
        lambda state_rows, vector: pool_words(state_rows, vector, present), states, pool_vector
    )[1]
    grad_states, pool_query_grad = pool_pull(grad_pooled)
    grad_after_mlp = grad_states.reshape(char_rows, char_dim)
    grad_down_low = grad_after_mlp.astype(bfloat)
    char_down_grad = outer_accum(char_upper, grad_down_low)
    grad_char_upper = back_project(grad_down_low, char_down)
    grad_char_hidden = jax.vjp(jax.nn.gelu, char_hidden)[1](grad_char_upper)[0].astype(bfloat)
    char_up_grad = outer_accum(middle, grad_char_hidden)
    grad_middle = back_project(grad_char_hidden, char_up)
    grad_mid_ln, char_midnorm_grad = jax.vjp(layer_norm, after_attn, gain_second)[1](grad_middle)
    grad_char_attn = grad_after_mlp + grad_mid_ln
    grad_char_low = grad_char_attn.astype(bfloat)
    char_out_grad = outer_accum(char_mixed_low, grad_char_low)
    grad_char_mixed = (
        back_project(grad_char_low, char_out)
        .astype(bfloat)
        .reshape(word_count, char_len, CHEADS, char_head)
    )
    grad_char_packed = (
        char_attend_back(packed, present, char_scale, grad_char_mixed)
        .astype(bfloat)
        .reshape(char_rows, 3 * char_dim)
    )
    char_qkv_grad = outer_accum(normed, grad_char_packed)
    grad_normed = back_project(grad_char_packed, char_qkv)
    grad_embed_ln, char_prenorm_grad = jax.vjp(layer_norm, embedded, gain_first)[1](grad_normed)
    chars_grad = (grad_char_attn + grad_embed_ln).reshape(word_count, char_len, char_dim)
    (
        char_prenorm_grad,
        char_qkv_grad,
        char_out_grad,
        char_midnorm_grad,
        char_up_grad,
        char_down_grad,
        pool_query_grad,
        char_proj_grad,
        word_prenorm_grad,
        word_midnorm_grad,
    ) = (
        lax.psum(char_prenorm_grad.astype(jnp.bfloat16), ("ctx", "tp")).astype(jnp.float32),
        lax.psum(char_qkv_grad.astype(jnp.bfloat16), ("ctx", "tp")).astype(jnp.float32),
        lax.psum(char_out_grad.astype(jnp.bfloat16), ("ctx", "tp")).astype(jnp.float32),
        lax.psum(char_midnorm_grad.astype(jnp.bfloat16), ("ctx", "tp")).astype(jnp.float32),
        lax.psum(char_up_grad.astype(jnp.bfloat16), ("ctx", "tp")).astype(jnp.float32),
        lax.psum(char_down_grad.astype(jnp.bfloat16), ("ctx", "tp")).astype(jnp.float32),
        lax.psum(pool_query_grad.astype(jnp.bfloat16), ("ctx", "tp")).astype(jnp.float32),
        lax.psum(char_proj_grad.astype(jnp.bfloat16), ("ctx", "tp")).astype(jnp.float32),
        lax.psum(word_prenorm_grad.astype(jnp.bfloat16), ("ctx", "tp")).astype(jnp.float32),
        lax.psum(word_midnorm_grad.astype(jnp.bfloat16), ("ctx", "tp")).astype(jnp.float32),
    )
    word_qkv_grad, word_up_grad, word_out_grad, word_down_grad = (
        lax.psum(word_qkv_grad.astype(jnp.bfloat16), "ctx").astype(jnp.float32),
        lax.psum(word_up_grad.astype(jnp.bfloat16), "ctx").astype(jnp.float32),
        lax.psum(word_out_grad.astype(jnp.bfloat16), "ctx").astype(jnp.float32),
        lax.psum(word_down_grad.astype(jnp.bfloat16), "ctx").astype(jnp.float32),
    )
    (
        char_prenorm_grad,
        char_qkv_grad,
        char_out_grad,
        char_midnorm_grad,
        char_up_grad,
        char_down_grad,
        pool_query_grad,
        char_proj_grad,
        word_prenorm_grad,
        word_midnorm_grad,
        word_qkv_grad,
        word_up_grad,
    ) = (
        lax.psum_scatter(
            char_prenorm_grad.astype(jnp.bfloat16), "fsdp", scatter_dimension=0, tiled=True
        ).astype(jnp.float32),
        lax.psum_scatter(
            char_qkv_grad.astype(jnp.bfloat16), "fsdp", scatter_dimension=0, tiled=True
        ).astype(jnp.float32),
        lax.psum_scatter(
            char_out_grad.astype(jnp.bfloat16), "fsdp", scatter_dimension=0, tiled=True
        ).astype(jnp.float32),
        lax.psum_scatter(
            char_midnorm_grad.astype(jnp.bfloat16), "fsdp", scatter_dimension=0, tiled=True
        ).astype(jnp.float32),
        lax.psum_scatter(
            char_up_grad.astype(jnp.bfloat16), "fsdp", scatter_dimension=0, tiled=True
        ).astype(jnp.float32),
        lax.psum_scatter(
            char_down_grad.astype(jnp.bfloat16), "fsdp", scatter_dimension=0, tiled=True
        ).astype(jnp.float32),
        lax.psum_scatter(
            pool_query_grad.astype(jnp.bfloat16), "fsdp", scatter_dimension=0, tiled=True
        ).astype(jnp.float32),
        lax.psum_scatter(
            char_proj_grad.astype(jnp.bfloat16), "fsdp", scatter_dimension=0, tiled=True
        ).astype(jnp.float32),
        lax.psum_scatter(
            word_prenorm_grad.astype(jnp.bfloat16), "fsdp", scatter_dimension=0, tiled=True
        ).astype(jnp.float32),
        lax.psum_scatter(
            word_midnorm_grad.astype(jnp.bfloat16), "fsdp", scatter_dimension=0, tiled=True
        ).astype(jnp.float32),
        lax.psum_scatter(
            word_qkv_grad.astype(jnp.bfloat16), "fsdp", scatter_dimension=0, tiled=True
        ).astype(jnp.float32),
        lax.psum_scatter(
            word_up_grad.astype(jnp.bfloat16), "fsdp", scatter_dimension=0, tiled=True
        ).astype(jnp.float32),
    )
    word_out_grad, word_down_grad = (
        lax.psum_scatter(
            word_out_grad.astype(jnp.bfloat16), "fsdp", scatter_dimension=1, tiled=True
        ).astype(jnp.float32),
        lax.psum_scatter(
            word_down_grad.astype(jnp.bfloat16), "fsdp", scatter_dimension=1, tiled=True
        ).astype(jnp.float32),
    )
    return (
        final_rows.astype(bfloat),
        chars_grad,
        grad_start,
        branch_rms,
        char_prenorm_grad,
        char_qkv_grad,
        char_out_grad,
        char_midnorm_grad,
        char_up_grad,
        char_down_grad,
        pool_query_grad,
        char_proj_grad,
        word_prenorm_grad,
        word_qkv_grad,
        word_out_grad,
        word_midnorm_grad,
        word_up_grad,
        word_down_grad,
    )


def solution(mesh):
    return jax.shard_map(
        local,
        mesh=mesh,
        in_specs=(
            P(("fsdp", "ctx", "tp"), None, None),
            P(("fsdp", "ctx", "tp")),
            P(("fsdp", "ctx", "tp"), None),
            P(("fsdp", "ctx", "tp"), None),
            P("fsdp"),
            P("fsdp", None),
            P("fsdp", None),
            P("fsdp"),
            P("fsdp", None),
            P("fsdp", None),
            P("fsdp"),
            P("fsdp", None),
            P("fsdp"),
            P("fsdp", None, "tp"),
            P("tp", "fsdp"),
            P("fsdp"),
            P("fsdp", "tp"),
            P("tp", "fsdp"),
        ),
        out_specs=(
            P(("fsdp", "ctx", "tp"), None),
            P(("fsdp", "ctx", "tp"), None, None),
            P(("fsdp", "ctx", "tp"), None),
            P(None, ("fsdp", "ctx", "tp")),
            P("fsdp"),
            P("fsdp", None),
            P("fsdp", None),
            P("fsdp"),
            P("fsdp", None),
            P("fsdp", None),
            P("fsdp"),
            P("fsdp", None),
            P("fsdp"),
            P("fsdp", None, "tp"),
            P("tp", "fsdp"),
            P("fsdp"),
            P("fsdp", "tp"),
            P("tp", "fsdp"),
        ),
        check_vma=False,
    )
```

profile of v0, /device:TPU:0, one launch (start us, length us, event | category | flops | bytes accessed | tf_op | source)
XLA Modules:
  0.0 1017.3 jit_solution(2496783421401721926)
XLA Ops:
  14.5 13.4 %all-reduce.11 = (bf16[256]{0:T(256)(128)(2,1)S(1)}, bf16[256]{0:T(256)(128)(2,1)S(1)}, bf16[256]{0:T(256)(128)(2,1)S(1)}) all-reduce(bf16[256]{0:T(256)(128)(2,1)S(1)} %dynamic-update-slice, bf16[256]{0:T(256)(128)(2,1)S(1)} %dynamic-update-slice.1, bf16[256]{0:T(256)(128)(2,1)S(1)} %dynamic-update-slice.2), channel_id=1, replica_groups=mesh['fsdp'=4,'ctx'=2,'tp'=4] {'fsdp'}, use_global_device_ids=true, to_apply=%add | all-reduce | flops 768 | bytes 3072
  29.6 7.5 all-gather.2
  38.4 13.4 %all_gather.62 = bf16[256,256]{1,0:T(8,128)(2,1)S(1)} all-gather(bf16[64,256]{1,0:T(8,128)(2,1)S(1)} %copy-done.74), channel_id=1, replica_groups=mesh['fsdp'=4,'ctx'=2,'tp'=4] {'fsdp'}, dimensions={0}, use_global_device_ids=true | all-gather | bytes 163840 | tf_op jit(solution)/shard_map/all_gather | solution.py:174
  52.6 14.3 %all_gather.67 = bf16[256,512]{1,0:T(8,128)(2,1)S(1)} all-gather(bf16[64,512]{1,0:T(8,128)(2,1)S(1)} %copy-done.69), channel_id=1, replica_groups=mesh['fsdp'=4,'ctx'=2,'tp'=4] {'fsdp'}, dimensions={0}, use_global_device_ids=true | all-gather | bytes 327680 | tf_op jit(solution)/shard_map/all_gather | solution.py:179
  66.9 15.4 %all_gather.61 = bf16[256,768]{1,0:T(8,128)(2,1)S(1)} all-gather(bf16[64,768]{1,0:T(8,128)(2,1)S(1)} %copy-done.68), channel_id=1, replica_groups=mesh['fsdp'=4,'ctx'=2,'tp'=4] {'fsdp'}, dimensions={0}, use_global_device_ids=true | all-gather | bytes 491520 | tf_op jit(solution)/shard_map/all_gather | solution.py:173
  82.3 16.0 %all_gather.64 = bf16[256,1024]{1,0:T(8,128)(2,1)S(1)} all-gather(bf16[64,1024]{1,0:T(8,128)(2,1)S(1)} %copy-done.63), channel_id=1, replica_groups=mesh['fsdp'=4,'ctx'=2,'tp'=4] {'fsdp'}, dimensions={0}, use_global_device_ids=true | all-gather | bytes 655360 | tf_op jit(solution)/shard_map/all_gather | solution.py:176
  98.3 15.4 %all_gather.65 = bf16[1024,256]{1,0:T(8,128)(2,1)S(1)} all-gather(bf16[256,256]{1,0:T(8,128)(2,1)} %param.31), channel_id=1, replica_groups=mesh['fsdp'=4,'ctx'=2,'tp'=4] {'fsdp'}, dimensions={0}, use_global_device_ids=true | all-gather | bytes 655360 | tf_op jit(solution)/shard_map/all_gather | solution.py:177
  115.6 4.4 convolution_convert_fusion
  120.0 18.6 %reshape.554 = bf16[256,16,3,4,64]{4,3,2,1,0:T(4,128)(2,1)} reshape(bf16[4096,768]{1,0:T(8,128)(2,1)} %convolution_convert_fusion) | data formatting | bytes 12582912 | tf_op jit(solution)/shard_map/reshape | solution.py:200
  138.6 8.5 fusion.165
  147.1 6.1 fusion.118
  153.2 12.6 %fusion.168 = (f32[256,4,16]{2,1,0:T(4,128)S(1)}, f32[256,4,16,16]{2,3,1,0:T(8,128)}) fusion(f32[256,4,16,16]{2,3,1,0:T(8,128)} %fusion.118, pred[256,16]{1,0:T(8,128)(4,1)S(1)} %copy-done.66), kind=kOutput, calls=%fused_computation.258 | output fusion | flops 1572879 | bytes 2166784 | tf_op jit(solution)/shard_map/sub | solution.py:92
  166.7 4.8 convert_bitcast_fusion
  171.5 4.2 copy.83
  175.7 7.0 reshape.555
  188.9 7.9 multiply_reduce_fusion.8
  202.4 12.3 %all_gather.73 = bf16[128,512]{1,0:T(8,128)(2,1)S(1)} all-gather(bf16[128,128]{1,0:T(8,128)(2,1)S(1)} %copy-done.75), channel_id=1, replica_groups=mesh['fsdp'=4,'ctx'=2,'tp'=4] {'fsdp'}, dimensions={1}, use_global_device_ids=true | all-gather | bytes 163840 | tf_op jit(solution)/shard_map/all_gather | solution.py:186
  214.7 13.3 %all_gather.70 = bf16[512,3,128]{0,2,1:T(8,128)(2,1)S(1)} all-gather(bf16[128,3,128]{0,2,1:T(8,128)(2,1)S(1)} %copy.84), channel_id=1, replica_groups=mesh['fsdp'=4,'ctx'=2,'tp'=4] {'fsdp'}, dimensions={0}, use_global_device_ids=true | all-gather | bytes 491520 | tf_op jit(solution)/shard_map/all_gather | solution.py:182
  235.8 19.2 %while.32 = (s32[]{:T(128)}, bf16[2,512,2,64]{1,3,2,0:T(8,128)(2,1)}, f32[2,2,512]{2,1,0:T(2,128)S(1)}, s32[2,512]{1,0:T(2,128)S(1)}, bf16[2,512,2,64]{1,3,2,0:T...) while((s32[]{:T(128)}, ...), condition=%wide.region_15.16_spmd.clone, body=%wide.region_12.15_spmd.clone.sunk | while | flops 563108352 | bytes 32958628 | solution.py:254
  259.6 10.8 %all-gather.3 = bf16[4,1,128]{2,1,0:T(2,128)(2,1)S(1)} all-gather(bf16[1,1,128]{2,1,0:T(2,128)(2,1)S(1)} %bitcast.256), channel_id=1, replica_groups=mesh['fsdp'=4,'ctx'=2,'tp'=4] {'fsdp'}, dimensions={0}, use_global_device_ids=true | all-gather | bytes 1280 | tf_op jit(solution)/shard_map/all_gather | solution.py:181
  270.4 23.7 %reduce-scatter.20.cloned.1.call-done = f32[256,512]{1,0:T(8,128)} async-done(((f32[1024,512]{1,0:T(8,128)}), f32[256,512]{1,0:T(8,128)}) %reduce-scatter.20.cloned.1.call-update) | async-done | bytes 524304 | tf_op jit(solution)/shard_map/reduce_scatter | solution.py:63
  297.2 15.6 %all_gather.76 = bf16[512,512]{1,0:T(8,128)(2,1)S(1)} all-gather(bf16[128,512]{1,0:T(8,128)(2,1)S(1)} %copy-done.64), channel_id=1, replica_groups=mesh['fsdp'=4,'ctx'=2,'tp'=4] {'fsdp'}, dimensions={0}, use_global_device_ids=true | all-gather | bytes 655360 | tf_op jit(solution)/shard_map/all_gather | solution.py:183
  312.8 15.2 %all_gather.77 = bf16[512,512]{1,0:T(8,128)(2,1)S(1)} all-gather(bf16[512,128]{1,0:T(8,128)(2,1)S(1)} %copy-done.65), channel_id=1, replica_groups=mesh['fsdp'=4,'ctx'=2,'tp'=4] {'fsdp'}, dimensions={1}, use_global_device_ids=true | all-gather | bytes 655360 | tf_op jit(solution)/shard_map/all_gather | solution.py:187
  331.4 20.5 %all-gather.11.cloned.1.call-done = bf16[1024,512]{1,0:T(8,128)(2,1)} async-done(((bf16[256,512]{1,0:T(8,128)(2,1)}), bf16[1024,512]{1,0:T(8,128)(2,1)}) %all-gather.11.cloned.1.call-update) | async-done | bytes 1048592 | tf_op jit(solution)/shard_map/all_gather | solution.py:51
  351.9 5.0 fusion.130
  363.9 31.5 %reduce-scatter.24.cloned.1.call-done = f32[256,512]{1,0:T(8,128)} async-done(((f32[1024,512]{1,0:T(8,128)}), f32[256,512]{1,0:T(8,128)}) %reduce-scatter.24.cloned.1.call-update) | async-done | bytes 524304 | tf_op jit(solution)/shard_map/reduce_scatter | solution.py:76
  395.4 38.1 %reduce-scatter.22.cloned.1.call-done = f32[256,512]{1,0:T(8,128)} async-done(((f32[1024,512]{1,0:T(8,128)}), f32[256,512]{1,0:T(8,128)}) %reduce-scatter.22.cloned.1.call-update) | async-done | bytes 524304 | tf_op jit(solution)/shard_map/reduce_scatter | solution.py:63
  439.0 26.7 %all-gather.15.cloned.1.call-done = bf16[1024,512]{1,0:T(8,128)(2,1)} async-done(((bf16[256,512]{1,0:T(8,128)(2,1)}), bf16[1024,512]{1,0:T(8,128)(2,1)}) %all-gather.15.cloned.1.call-update) | async-done | bytes 1048592 | tf_op jit(solution)/shard_map/all_gather | solution.py:55
  469.1 95.2 %while.33 = (s32[]{:T(128)}, f32[2048,2,64]{0,2,1:T(8,128)}, f32[2048,2,64]{0,2,1:T(8,128)}, bf16[2,512,2,64]{1,0,3,2:T(2,128)(2,1)}, bf16[2,512,2,64]{1,3,2,0:T...) while((s32[]{:T(128)}, f32[2048,2,64]{0,2,1:T(8,128)}, ...), condition=%wide.region_25.26_spmd.clone, body=%wide.region_23.25_spmd.clone.sunk | while | flops 1398830592 | bytes 129681656 | solution.py:305
  476.9 5.4 fusion.260
  482.4 13.5 %fusion.264 = bf16[1,512,2,64]{1,3,2,0:T(8,128)(2,1)S(1)} fusion(bf16[2048,2,64]{0,2,1:T(8,128)(2,1)S(1)} %get-tuple-element.646, f32[2,512,2048]{2,1,0:T(8,128)} %fusion.260, f32[2,512,2048]{2,1,0:T(8,128)} %copy-done, f32[2,512]{1,0:T(2,128)S(1)} %dynamic-slice_bitcast_fusion.2, pred[512,2048]{1,0:T(8,128)(4,1)S(1)} %broadcast_compare_fusion.5), kind=kOutput, calls=%fused_computation.56.clone.1 | convolution fusion | flops 291507200 | bytes 18485248 | tf_op jit(solution)/shard_map/while/body/eval_jaxpr/hqk,khe->qhe/dot_general | solution.py:298
  495.9 15.1 %fusion.262 = f32[2048,2,64]{0,2,1:T(8,128)} fusion(f32[2,512,2048]{2,1,0:T(8,128)} %fusion.260, f32[2,512,2048]{2,1,0:T(8,128)} %copy-done, f32[2,512]{1,0:T(2,128)S(1)} %dynamic-slice_bitcast_fusion.2, pred[512,2048]{1,0:T(8,128)(4,1)S(1)} %broadcast_compare_fusion.5, f32[2048,2,64]{0,2,1:T(8,128)} %get-tuple-element.629, pred[]{:T(512)S(6)} %compare.27, ...), kind=kOutput, calls=%fused_computation.54.clone.1 | convolution fusion | flops 292031488 | bytes 37888004 | tf_op jit(solution)/shard_map/while/body/eval_jaxpr/hqk,qhe->khe/dot_general | solution.py:301
  511.2 5.3 dynamic_update_slice.30
  524.4 5.4 fusion.260
  529.8 13.5 %fusion.264 = bf16[1,512,2,64]{1,3,2,0:T(8,128)(2,1)S(1)} fusion(bf16[2048,2,64]{0,2,1:T(8,128)(2,1)S(1)} %get-tuple-element.646, f32[2,512,2048]{2,1,0:T(8,128)} %fusion.260, f32[2,512,2048]{2,1,0:T(8,128)} %copy-done, f32[2,512]{1,0:T(2,128)S(1)} %dynamic-slice_bitcast_fusion.2, pred[512,2048]{1,0:T(8,128)(4,1)S(1)} %broadcast_compare_fusion.5), kind=kOutput, calls=%fused_computation.56.clone.1 | convolution fusion | flops 291507200 | bytes 18485248 | tf_op jit(solution)/shard_map/while/body/eval_jaxpr/hqk,khe->qhe/dot_general | solution.py:298
  543.4 15.4 %fusion.262 = f32[2048,2,64]{0,2,1:T(8,128)} fusion(f32[2,512,2048]{2,1,0:T(8,128)} %fusion.260, f32[2,512,2048]{2,1,0:T(8,128)} %copy-done, f32[2,512]{1,0:T(2,128)S(1)} %dynamic-slice_bitcast_fusion.2, pred[512,2048]{1,0:T(8,128)(4,1)S(1)} %broadcast_compare_fusion.5, f32[2048,2,64]{0,2,1:T(8,128)} %get-tuple-element.629, pred[]{:T(512)S(6)} %compare.27, ...), kind=kOutput, calls=%fused_computation.54.clone.1 | convolution fusion | flops 292031488 | bytes 37888004 | tf_op jit(solution)/shard_map/while/body/eval_jaxpr/hqk,qhe->khe/dot_general | solution.py:301
  559.0 5.3 dynamic_update_slice.30
  573.0 12.0 %reduce-scatter.28.cloned.1.call-done = f32[1024,2,64]{0,2,1:T(8,128)} async-done(((f32[2048,2,64]{0,2,1:T(8,128)}), f32[1024,2,64]{0,2,1:T(8,128)}) %reduce-scatter.28.cloned.1.call-update) | async-done | bytes 524304 | tf_op jit(solution)/shard_map/reduce_scatter | solution.py:310
  602.0 8.0 reduce-scatter.48.cloned.1.call-done
  611.7 21.2 %reduce-scatter.44.cloned.1.call-done = bf16[128,512]{1,0:T(8,128)(2,1)} async-done(((bf16[512,512]{1,0:T(8,128)(2,1)}), bf16[128,512]{1,0:T(8,128)(2,1)}) %reduce-scatter.44.cloned.1.call-update) | async-done | bytes 131088 | tf_op jit(solution)/shard_map/reduce_scatter | solution.py:433
  632.9 21.1 %reduce-scatter.42.cloned.1.call-done = bf16[128,3,128]{2,0,1:T(8,128)(2,1)} async-done(((bf16[512,3,128]{2,0,1:T(8,128)(2,1)}), bf16[128,3,128]{2,0,1:T(8,128)(2,1)}) %reduce-scatter.42.cloned.1.call-update) | async-done | bytes 98320 | tf_op jit(solution)/shard_map/reduce_scatter | solution.py:430
  654.0 36.4 %reduce-scatter.30.cloned.1.call-done = f32[256,512]{1,0:T(8,128)} async-done(((f32[1024,512]{1,0:T(8,128)}), f32[256,512]{1,0:T(8,128)}) %reduce-scatter.30.cloned.1.call-update) | async-done | bytes 524304 | tf_op jit(solution)/shard_map/reduce_scatter | solution.py:76
  698.9 14.7 %fusion.104 = bf16[4096,1024]{1,0:T(8,128)(2,1)S(1)} fusion(f32[4096,1024]{1,0:T(8,128)} %copy-done.9, bf16[4096,256]{1,0:T(8,128)(2,1)S(1)} %fusion.111, bf16[1024,256]{1,0:T(8,128)(2,1)S(1)} %copy-done.46), kind=kOutput, calls=%fused_computation.105 | convolution fusion | flops 2231369728 | bytes 27787264 | tf_op jit(solution)/shard_map/dot_general | solution.py:41
  727.9 9.3 fusion.115
  737.2 7.7 fusion.120
  744.9 17.5 %fusion.119 = bf16[256,4,64,16]{2,3,1,0:T(8,128)(2,1)} fusion(bf16[256,16,1,4,64]{4,3,2,1,0:T(4,128)(2,1)} %copy-done.13, f32[256,4,16,16]{2,3,1,0:T(8,128)} %fusion.115, f32[256,4,16,16]{2,3,1,0:T(8,128)} %get-tuple-element.470, f32[256,4,16]{2,1,0:T(4,128)S(1)} %copy-done.112), kind=kOutput, calls=%fused_computation.153 | convolution fusion | flops 35405840 | bytes 6356992 | tf_op jit(solution)/shard_map/whqk,wkhe->wqhe/dot_general | solution.py:118
  762.4 17.1 %fusion.117 = bf16[256,4,64,16]{2,3,1,0:T(8,128)(2,1)} fusion(bf16[256,16,1,4,64]{4,3,2,1,0:T(4,128)(2,1)} %copy-done.12, f32[256,4,16,16]{2,3,1,0:T(8,128)} %fusion.115, f32[256,4,16,16]{2,3,1,0:T(8,128)} %get-tuple-element.470, f32[256,4,16]{2,1,0:T(4,128)S(1)} %copy-done.112), kind=kOutput, calls=%fused_computation.151 | convolution fusion | flops 35405840 | bytes 6356992 | tf_op jit(solution)/shard_map/whqk,wqhe->wkhe/dot_general | solution.py:121
  779.5 5.0 copy.96
  784.5 5.9 copy.94
  790.4 6.1 copy.93
  796.5 5.5 maximum_convert_fusion
  802.0 20.2 %copy.97 = bf16[256,16,3,4,64]{4,3,2,1,0:T(4,128)(2,1)} copy(bf16[256,16,3,4,64]{0,4,3,2,1:T(8,128)(2,1)} %maximum_convert_fusion) | data formatting | bytes 12582912 | tf_op jit(solution)/shard_map/convert_element_type | solution.py:350
  822.2 18.6 %convert_element_type.291 = bf16[4096,768]{1,0:T(8,128)(2,1)} reshape(bf16[256,16,3,4,64]{4,3,2,1,0:T(4,128)(2,1)} %copy.97) | data formatting | bytes 12582912 | tf_op jit(solution)/shard_map/convert_element_type | solution.py:350
  841.9 5.4 convolution_convert_fusion.8
  847.4 11.5 %convolution_convert_fusion.3 = bf16[1024,256]{1,0:T(8,128)(2,1)} fusion(bf16[4096,256]{1,0:T(8,128)(2,1)} %copy-done.33, f32[4096,1024]{1,0:T(8,128)} %copy-done.9), kind=kOutput, calls=%fused_computation.172 | convolution fusion | flops 2185494528 | bytes 19398656 | tf_op jit(solution)/shard_map/dot_general | solution.py:35
  869.3 8.9 convolution_convert_fusion.4
  878.6 6.8 multiply_reduce_fusion.5
  887.0 4.5 multiply_reduce_fusion.4
  891.4 12.0 %all-reduce.10 = (bf16[256]{0:T(256)(128)(2,1)S(1)}, bf16[256]{0:T(256)(128)(2,1)S(1)}, bf16[256]{0:T(256)(128)(2,1)S(1)}, bf16[512]{0:T(512)(128)(2,1)S(1)}, bf16[512]{0:T(512)(128)(2,1)S(1)}) all-reduce(bf16[256]{0:T(256)(128)(2,1)S(1)} %get-tuple-element.380, ...), channel_id=10, replica_groups=mesh['fsdp'=4,'ctx'=2,'tp'=4] {'fsdp'}, use_global_device_ids=true, to_apply=%region_43.44.clone | all-reduce | flops 1792 | bytes 7168
  905.0 22.3 %reduce-scatter.36.cloned.1.call-done = bf16[64,1024]{1,0:T(8,128)(2,1)} async-done(((bf16[256,1024]{1,0:T(8,128)(2,1)}), bf16[64,1024]{1,0:T(8,128)(2,1)}) %reduce-scatter.36.cloned.1.call-update) | async-done | bytes 131088 | tf_op jit(solution)/shard_map/reduce_scatter | solution.py:412
  927.4 9.3 add_add_fusion.2
  936.7 10.8 %reduce-scatter.34.cloned.1.call-done = bf16[64,256]{1,0:T(8,128)(2,1)} async-done(((bf16[256,256]{1,0:T(8,128)(2,1)}), bf16[64,256]{1,0:T(8,128)(2,1)}) %reduce-scatter.34.cloned.1.call-update) | async-done | bytes 32784 | tf_op jit(solution)/shard_map/reduce_scatter | solution.py:406
  947.5 28.2 %all-reduce.8 = (bf16[64]{0:T(256)(128)(2,1)S(1)}, bf16[64,256]{1,0:T(8,128)(2,1)S(1)}, bf16[64]{0:T(256)(128)(2,1)S(1)}, bf16[64]{0:T(256)(128)(2,1)S(1)}, bf16...) all-reduce(bf16[64]{0:T(256)(128)(2,1)S(1)} %dynamic-slice.4, ...), channel_id=1, replica_groups=mesh['fsdp'=4,'ctx'=2,'tp'=4] {'ctx','tp'}, use_global_device_ids=true, to_apply=%region_42.43 | all-reduce | flops 16832 | bytes 67328 | tf_op jit(solution)/shard_map/psum | solution.py:369
  978.9 24.9 %all-reduce.16.cloned.1.call-done = (bf16[64,768]{1,0:T(8,128)(2,1)}, bf16[64,1024]{1,0:T(8,128)(2,1)}, bf16[256,256]{1,0:T(8,128)(2,1)}, bf16[64,512]{1,0:T(8,128)(2,1)}) async-done(((bf16[64,768]{1,0:T(8,128)(2,1)}, bf16[64,1024]{1,0:T(8,128)(2,1)}, bf16[256,256]{1,0:T(8,128)(2,1)}, bf16[64,512]{1,0:T(8,128)(2,1)}), (bf16[64,768]{1,0:T(8,128)(2,1)}, bf16[64,1024]{1,0:T(8,128)(2,1)}, ...) | async-done | bytes 426000 | tf_op jit(solution)/shard_map/psum | solution.py:370
  (452 shorter events, 166.2 us)
Async XLA Ops:
  7.2 106.4 %copy-start.1 = (bf16[256,16,256]{2,1,0:T(8,128)(2,1)S(1)}, bf16[256,16,256]{2,1,0:T(8,128)(2,1)}, u32[]{:S(2)}) copy-start(bf16[256,16,256]{2,1,0:T(8,128)(2,1)} %param.22) | copy-start | bytes 6291460
  7.2 22.3 %copy-start.105 = (bf16[128]{0:T(256)(128)(2,1)S(1)}, bf16[128]{0:T(256)(128)(2,1)}, u32[]{:S(2)}) copy-start(bf16[128]{0:T(256)(128)(2,1)} %param.34) | copy-start | bytes 772
  7.3 30.4 %copy-start.80 = (s32[256]{0:T(256)S(1)}, s32[256]{0:T(256)}, u32[]{:S(2)}) copy-start(s32[256]{0:T(256)} %param.23) | copy-start | bytes 3076
  7.3 31.1 %copy-start.74 = (bf16[64,256]{1,0:T(8,128)(2,1)S(1)}, bf16[64,256]{1,0:T(8,128)(2,1)}, u32[]{:S(2)}) copy-start(bf16[64,256]{1,0:T(8,128)(2,1)} %param.28) | copy-start | bytes 98308
  7.3 45.3 %copy-start.69 = (bf16[64,512]{1,0:T(8,128)(2,1)S(1)}, bf16[64,512]{1,0:T(8,128)(2,1)}, u32[]{:S(2)}) copy-start(bf16[64,512]{1,0:T(8,128)(2,1)} %param.33) | copy-start | bytes 196612
  7.3 59.6 %copy-start.68 = (bf16[64,768]{1,0:T(8,128)(2,1)S(1)}, bf16[64,768]{1,0:T(8,128)(2,1)}, u32[]{:S(2)}) copy-start(bf16[64,768]{1,0:T(8,128)(2,1)} %param.27) | copy-start | bytes 294916
  7.3 75.0 %copy-start.63 = (bf16[64,1024]{1,0:T(8,128)(2,1)S(1)}, bf16[64,1024]{1,0:T(8,128)(2,1)}, u32[]{:S(2)}) copy-start(bf16[64,1024]{1,0:T(8,128)(2,1)} %param.30) | copy-start | bytes 393220
  7.3 221.3 %all-gather.9.cloned.1.call-start = ((), (), s32[]{:S(2)}) async-start(), calls=%async_computation.15 | async-start | bytes 1310720 | tf_op jit(solution)/shard_map/all_gather | solution.py:51
  9.8 57.0 %copy-start.31 = (f32[256,16]{1,0:T(8,128)}, f32[256,16]{1,0:T(8,128)S(1)}, u32[]{:S(2)}) copy-start(f32[256,16]{1,0:T(8,128)S(1)} %broadcast_multiply_fusion) | copy-start | bytes 49156
  9.9 105.6 %copy-start.49 = (f32[4096]{0:T(1024)}, f32[4096]{0:T(1024)S(1)}, u32[]{:S(2)}) copy-start(f32[4096]{0:T(1024)S(1)} %div.186) | copy-start | bytes 49156
  51.7 130.9 %copy-start.37 = (bf16[256,256]{1,0:T(8,128)(2,1)}, bf16[256,256]{1,0:T(8,128)(2,1)S(1)}, u32[]{:S(2)}) copy-start(bf16[256,256]{1,0:T(8,128)(2,1)S(1)} %all_gather.62) | copy-start | bytes 393220
  52.5 14.3 %copy-start.61 = (f32[4096]{0:T(1024)}, f32[4096]{0:T(1024)S(1)}, u32[]{:S(2)}) copy-start(f32[4096]{0:T(1024)S(1)} %add.229) | copy-start | bytes 49156
  52.6 61.1 %copy-start.51 = (f32[4096]{0:T(1024)}, f32[4096]{0:T(1024)S(1)}, u32[]{:S(2)}) copy-start(f32[4096]{0:T(1024)S(1)} %rsqrt.47) | copy-start | bytes 49156
  66.9 133.8 %copy-start.27 = (bf16[256,512]{1,0:T(8,128)(2,1)}, bf16[256,512]{1,0:T(8,128)(2,1)S(1)}, u32[]{:S(2)}) copy-start(bf16[256,512]{1,0:T(8,128)(2,1)S(1)} %all_gather.67) | copy-start | bytes 786436
  82.3 33.3 %copy-start.34 = (bf16[256,768]{1,0:T(8,128)(2,1)}, bf16[256,768]{1,0:T(8,128)(2,1)S(1)}, u32[]{:S(2)}) copy-start(bf16[256,768]{1,0:T(8,128)(2,1)S(1)} %all_gather.61) | copy-start | bytes 1179652
  98.3 88.1 %copy-start.29 = (bf16[256,1024]{1,0:T(8,128)(2,1)}, bf16[256,1024]{1,0:T(8,128)(2,1)S(1)}, u32[]{:S(2)}) copy-start(bf16[256,1024]{1,0:T(8,128)(2,1)S(1)} %all_gather.64) | copy-start | bytes 1572868
  113.6 75.2 %copy-start.45 = (bf16[1024,256]{1,0:T(8,128)(2,1)}, bf16[1024,256]{1,0:T(8,128)(2,1)S(1)}, u32[]{:S(2)}) copy-start(bf16[1024,256]{1,0:T(8,128)(2,1)S(1)} %all_gather.65) | copy-start | bytes 1572868
  147.1 18.8 %copy-start.14 = (bf16[256,16,1,4,64]{4,3,2,1,0:T(4,128)(2,1)}, bf16[256,16,1,4,64]{4,3,2,1,0:T(4,128)(2,1)S(1)}, u32[]{:S(2)}) copy-start(bf16[256,16,1,4,64]{4,3,2,1,0:T(4,128)(2,1)S(1)} %get-tuple-element.455) | copy-start | bytes 6291460
  196.9 31.1 %copy-start.70 = (f32[4096]{0:T(1024)}, f32[4096]{0:T(1024)S(1)}, u32[]{:S(2)}) copy-start(f32[4096]{0:T(1024)S(1)} %get-tuple-element.473) | copy-start | bytes 49156
  197.0 31.0 %copy-start.20 = (f32[256,16]{1,0:T(8,128)}, f32[256,16]{1,0:T(8,128)S(1)}, u32[]{:S(2)}) copy-start(f32[256,16]{1,0:T(8,128)S(1)} %reduce_sum.318) | copy-start | bytes 49156
  197.2 30.8 %copy-start.78 = (f32[256]{0:T(256)}, f32[256]{0:T(256)S(1)}, u32[]{:S(2)}) copy-start(f32[256]{0:T(256)S(1)} %fusion.146) | copy-start | bytes 3076
  200.7 14.0 %copy-start.39 = (bf16[256,256]{1,0:T(8,128)(2,1)}, bf16[256,256]{1,0:T(8,128)(2,1)S(1)}, u32[]{:S(2)}) copy-start(bf16[256,256]{1,0:T(8,128)(2,1)S(1)} %multiply_reduce_fusion.7) | copy-start | bytes 393220
  201.1 27.5 %copy-start.83 = (f32[256]{0:T(256)}, f32[256]{0:T(256)S(1)}, u32[]{:S(2)}) copy-start(f32[256]{0:T(256)S(1)} %broadcast_multiply_fusion.3) | copy-start | bytes 3076
  201.3 27.3 %copy-start.89 = (f32[256]{0:T(256)}, f32[256]{0:T(256)S(1)}, u32[]{:S(2)}) copy-start(f32[256]{0:T(256)S(1)} %fusion.149) | copy-start | bytes 3076
  202.2 92.0 %reduce-scatter.20.cloned.1.call-start = ((), (), s32[]{:S(2)}) async-start(), calls=%async_computation.16 | async-start | bytes 2621440 | tf_op jit(solution)/shard_map/reduce_scatter | solution.py:63
  256.2 41.0 %copy-start.64 = (bf16[128,512]{1,0:T(8,128)(2,1)S(1)}, bf16[128,512]{1,0:T(8,128)(2,1)}, u32[]{:S(2)}) copy-start(bf16[128,512]{1,0:T(8,128)(2,1)} %param.38) | copy-start | bytes 393220
  257.0 55.9 %copy-start.65 = (bf16[512,128]{1,0:T(8,128)(2,1)S(1)}, bf16[512,128]{1,0:T(8,128)(2,1)}, u32[]{:S(2)}) copy-start(bf16[512,128]{1,0:T(8,128)(2,1)} %param.39) | copy-start | bytes 393220
  258.8 69.3 %all-gather.13.cloned.1.call-start = ((), (), s32[]{:S(2)}) async-start(), calls=%async_computation.19 | async-start | bytes 1310720 | tf_op jit(solution)/shard_map/all_gather | solution.py:55
  259.6 92.4 %all-gather.11.cloned.1.call-start = ((), (), s32[]{:S(2)}) async-start(), calls=%async_computation.17 | async-start | bytes 1310720 | tf_op jit(solution)/shard_map/all_gather | solution.py:51
  297.1 98.3 %reduce-scatter.24.cloned.1.call-start = ((), (), s32[]{:S(2)}) async-start(), calls=%async_computation.20 | async-start | bytes 2621440 | tf_op jit(solution)/shard_map/reduce_scatter | solution.py:76
  360.1 73.4 %reduce-scatter.22.cloned.1.call-start = ((), (), s32[]{:S(2)}) async-start(), calls=%async_computation.18 | async-start | bytes 2621440 | tf_op jit(solution)/shard_map/reduce_scatter | solution.py:63
  360.1 73.4 %copy-start.77 = (f32[256]{0:T(256)S(1)}, f32[256]{0:T(256)}, u32[]{:S(2)}) copy-start(f32[256]{0:T(256)} %copy-done.76) | copy-start | bytes 3076
  360.1 73.4 %copy-start.86 = (f32[256]{0:T(256)S(1)}, f32[256]{0:T(256)}, u32[]{:S(2)}) copy-start(f32[256]{0:T(256)} %copy-done.85) | copy-start | bytes 3076
  360.1 76.1 %copy-start.99 = (f32[256]{0:T(256)S(1)}, f32[256]{0:T(256)}, u32[]{:S(2)}) copy-start(f32[256]{0:T(256)} %copy-done.98) | copy-start | bytes 3076
  363.9 74.2 %copy-start.23 = (bf16[256,512]{1,0:T(8,128)(2,1)S(1)}, bf16[256,512]{1,0:T(8,128)(2,1)}, u32[]{:S(2)}) copy-start(bf16[256,512]{1,0:T(8,128)(2,1)} %param.25) | copy-start | bytes 786436
  363.9 101.8 %all-gather.15.cloned.1.call-start = ((), (), s32[]{:S(2)}) async-start(), calls=%async_computation.21 | async-start | bytes 1310720 | tf_op jit(solution)/shard_map/all_gather | solution.py:55
  439.0 134.1 %reduce-scatter.26.cloned.1.call-start = ((), (), s32[]{:S(2)}) async-start(), calls=%async_computation.22 | async-start | bytes 1572864 | tf_op jit(solution)/shard_map/reduce_scatter | solution.py:309
  564.3 20.7 %reduce-scatter.28.cloned.1.call-start = ((), (), s32[]{:S(2)}) async-start(), calls=%async_computation.23 | async-start | bytes 1572864 | tf_op jit(solution)/shard_map/reduce_scatter | solution.py:310
  565.1 44.9 %reduce-scatter.48.cloned.1.call-start = ((), (), s32[]{:S(2)}) async-start(), calls=%async_computation.33 | async-start | bytes 655360
  569.1 63.8 %reduce-scatter.44.cloned.1.call-start = ((), (), s32[]{:S(2)}) async-start(), calls=%async_computation.31 | async-start | bytes 655360 | tf_op jit(solution)/shard_map/reduce_scatter | solution.py:433
  572.0 82.0 %reduce-scatter.42.cloned.1.call-start = ((), (), s32[]{:S(2)}) async-start(), calls=%async_computation.30 | async-start | bytes 491520 | tf_op jit(solution)/shard_map/reduce_scatter | solution.py:430
  590.1 100.4 %reduce-scatter.30.cloned.1.call-start = ((), (), s32[]{:S(2)}) async-start(), calls=%async_computation.24 | async-start | bytes 2621440 | tf_op jit(solution)/shard_map/reduce_scatter | solution.py:76
  593.5 96.9 %copy-start.73 = (f32[4,1,128]{2,1,0:T(1,128)S(1)}, f32[4,1,128]{2,1,0:T(1,128)}, u32[]{:S(2)}) copy-start(f32[4,1,128]{2,1,0:T(1,128)} %convert_element_type.322) | copy-start | bytes 6148
  593.5 96.9 %copy-start.84 = (f32[256]{0:T(256)S(1)}, f32[256]{0:T(256)}, u32[]{:S(2)}) copy-start(f32[256]{0:T(256)} %copy-done.83) | copy-start | bytes 3076
  593.6 266.0 %reduce-scatter.46.cloned.1.call-start = ((), (), s32[]{:S(2)}) async-start(), calls=%async_computation.32 | async-start | bytes 163840
  597.5 97.0 %copy-start.24 = (bf16[256,512]{1,0:T(8,128)(2,1)S(1)}, bf16[256,512]{1,0:T(8,128)(2,1)}, u32[]{:S(2)}) copy-start(bf16[256,512]{1,0:T(8,128)(2,1)} %param.25) | copy-start | bytes 786436
  597.5 97.0 %copy-start.96 = (f32[256]{0:T(256)S(1)}, f32[256]{0:T(256)}, u32[]{:S(2)}) copy-start(f32[256]{0:T(256)} %copy-done.95) | copy-start | bytes 3076
  597.5 97.2 %copy-start.28 = (bf16[256,512]{1,0:T(8,128)(2,1)S(1)}, bf16[256,512]{1,0:T(8,128)(2,1)}, u32[]{:S(2)}) copy-start(bf16[256,512]{1,0:T(8,128)(2,1)} %copy-done.27) | copy-start | bytes 786436
  598.7 265.8 %all-reduce.18.cloned.1.call-start = ((), (), s32[]{:S(2)}) async-start(), calls=%async_computation.35 | async-start | bytes 720896 | tf_op jit(solution)/shard_map/psum | solution.py:381
  654.0 249.9 %reduce-scatter.40.cloned.1.call-start = ((), (), s32[]{:S(2)}) async-start(), calls=%async_computation.29 | async-start | bytes 327680 | tf_op jit(solution)/shard_map/reduce_scatter | solution.py:421
  694.7 146.1 %copy-start.18 = (f32[256,512]{1,0:T(8,128)}, f32[256,512]{1,0:T(8,128)S(1)}, u32[]{:S(2)}) copy-start(f32[256,512]{1,0:T(8,128)S(1)} %add_add_fusion.6) | copy-start | bytes 1572868
  698.9 14.7 %copy-start.5 = (f32[4096,256]{1,0:T(8,128)S(1)}, f32[4096,256]{1,0:T(8,128)}, u32[]{:S(2)}) copy-start(f32[4096,256]{1,0:T(8,128)} %copy-done.4) | copy-start | bytes 12582916
  698.9 14.7 %copy-start.30 = (bf16[256,1024]{1,0:T(8,128)(2,1)S(1)}, bf16[256,1024]{1,0:T(8,128)(2,1)}, u32[]{:S(2)}) copy-start(bf16[256,1024]{1,0:T(8,128)(2,1)} %copy-done.29) | copy-start | bytes 1572868
  698.9 14.7 %copy-start.48 = (f32[4096]{0:T(1024)S(1)}, f32[4096]{0:T(1024)}, u32[]{:S(2)}) copy-start(f32[4096]{0:T(1024)} %copy-done.47) | copy-start | bytes 49156
  698.9 14.8 %copy-start.54 = (f32[4096]{0:T(1024)S(1)}, f32[4096]{0:T(1024)}, u32[]{:S(2)}) copy-start(f32[4096]{0:T(1024)} %copy-done.53) | copy-start | bytes 49156
  698.9 14.7 %copy-start.94 = (f32[256]{0:T(256)S(1)}, f32[256]{0:T(256)}, u32[]{:S(2)}) copy-start(f32[256]{0:T(256)} %convert_element_type.265) | copy-start | bytes 3076
  822.2 18.6 %copy-start.40 = (bf16[256,256]{1,0:T(8,128)(2,1)S(1)}, bf16[256,256]{1,0:T(8,128)(2,1)}, u32[]{:S(2)}) copy-start(bf16[256,256]{1,0:T(8,128)(2,1)} %copy-done.39) | copy-start | bytes 393220
  822.2 19.6 %copy-start.10 = (bf16[256,16,256]{2,1,0:T(8,128)(2,1)S(1)}, bf16[256,16,256]{2,1,0:T(8,128)(2,1)}, u32[]{:S(2)}) copy-start(bf16[256,16,256]{2,1,0:T(8,128)(2,1)} %multiply_convert_fusion.3) | copy-start | bytes 6291460
  841.8 62.1 %reduce-scatter.32.cloned.1.call-start = ((), (), s32[]{:S(2)}) async-start(), calls=%async_computation.25 | async-start | bytes 491520 | tf_op jit(solution)/shard_map/reduce_scatter | solution.py:403
  847.3 11.6 %copy-start.101 = (f32[256]{0:T(256)S(1)}, f32[256]{0:T(256)}, u32[]{:S(2)}) copy-start(f32[256]{0:T(256)} %get-tuple-element.386) | copy-start | bytes 3076
  847.3 57.7 %reduce-scatter.38.cloned.1.call-start = ((), (), s32[]{:S(2)}) async-start(), calls=%async_computation.28 | async-start | bytes 655360 | tf_op jit(solution)/shard_map/reduce_scatter | solution.py:415
  858.9 68.5 %reduce-scatter.36.cloned.1.call-start = ((), (), s32[]{:S(2)}) async-start(), calls=%async_computation.27 | async-start | bytes 655360 | tf_op jit(solution)/shard_map/reduce_scatter | solution.py:412
  878.3 69.2 %reduce-scatter.34.cloned.1.call-start = ((), (), s32[]{:S(2)}) async-start(), calls=%async_computation.26 | async-start | bytes 163840 | tf_op jit(solution)/shard_map/reduce_scatter | solution.py:406
  886.9 117.0 %all-reduce.16.cloned.1.call-start = ((), (), s32[]{:S(2)}) async-start(), calls=%async_computation.34 | async-start | bytes 851968 | tf_op jit(solution)/shard_map/psum | solution.py:370
  (75 other events, 321.8 us)
Sparse Core Ops, SparseCore 0:
  202.3 26.2 all-gather.8
  258.9 35.1 reduce-scatter.19
  296.2 26.6 all-gather.12
  325.3 26.6 all-gather.10
  360.2 35.1 reduce-scatter.23
  398.2 35.1 reduce-scatter.21
  439.1 26.6 all-gather.14
  564.5 8.5 reduce-scatter.25
  575.3 9.6 reduce-scatter.27
  587.2 22.7 reduce-scatter.47
  613.0 19.8 reduce-scatter.43
  635.1 18.8 reduce-scatter.41
  656.9 33.4 reduce-scatter.29
  693.2 19.1 reduce-scatter.45
  715.4 16.7 all-reduce.17
  841.9 19.6 reduce-scatter.39
  863.9 18.8 reduce-scatter.31
  884.9 20.0 reduce-scatter.37
  907.3 19.9 reduce-scatter.35
  930.0 17.4 reduce-scatter.33
  951.4 52.3 all-reduce.15
where the time goes:
time: 1020 us
  waiting for transfers between devices  301 us (30%)
  matrix products  258 us (25%)
  blocking collectives  211 us (21%)
  local copies, waits for them, and re-layouts  131 us (13%)
  other arithmetic  96.4 us (9%)
  between operations  18.3 us (2%)
    reduce_scatter x2, waiting for transfers between devices, partial_inputs(): lax.psum_scatter(rows_term(jnp.int32(0), local_rows * lax.axis_size('tp')...  67.9 us
    reduce_scatter x2, waiting for transfers between devices, partial_heads(): lax.psum_scatter(rows_term(jnp.int32(0), local_rows * lax.axis_size('tp')...  61.8 us
    convert_element_type x2, local copies, waits for them, and re-layouts, local(): grad_char_packed = char_attend_back(packed, present, char_scale, grad_cha...  38.8 us
    dot_general x9, matrix products, outer_accum(): lax.dot_general(left_side, right_side, (((0,), (0,)), ((), ())), preferre...  37 us
    dot_general x9, matrix products, back_project(): lax.dot_general(left_side, right_side, (((1,), (1,)), ((), ())), preferre...  36.7 us
    dot_general x2, matrix products, attend_back(): jnp.einsum('hqk,qhe->khe', grad_scores, query_blk, preferred_element_type...  30.5 us
    dot_general x9, matrix products, multiply(): return jnp.dot(left_side, right_side, preferred_element_type=jnp.float32)  29.8 us
    psum x1, blocking collectives, local(): lax.psum(char_prenorm_grad.astype(jnp.bfloat16), ('ctx', 'tp'))  28.2 us
  transfers between devices with their start and end apart: 21, of which 16 were waited for; matrix products, arithmetic and copies ran while one was open for 24% of the time, Pallas kernels for 0%

commit v1 on v0

v1 whole, which is shorter than its diff:
```python
import functools

import jax
import jax.numpy as jnp
from jax import lax
from jax.experimental import pallas as pl
from jax.experimental.pallas import tpu as pltpu
from jax.sharding import PartitionSpec as P

CHEADS = 4
HEADS = 8
HEAD = 64
EPSILON = 1e-05
MASKED = -1e30
CGELU = 0.7978845608028654
AGELU = 0.044715
ROWS = 512
GROUP = 128
F32 = jnp.float32
BF16 = jnp.bfloat16
VMEM_LIMIT = 66_000_000


def mm(a, b):
    return lax.dot_general(a, b, (((1,), (0,)), ((), ())), preferred_element_type=F32)


def mm_nt(a, b):
    return lax.dot_general(a, b, (((1,), (1,)), ((), ())), preferred_element_type=F32)


def mm_tn(a, b):
    return lax.dot_general(a, b, (((0,), (0,)), ((), ())), preferred_element_type=F32)


def ln_parts(x):
    c = x - jnp.mean(x, axis=-1, keepdims=True)
    r = lax.rsqrt(jnp.mean(c * c, axis=-1, keepdims=True) + EPSILON)
    return c * r, r


def ln_back(xhat, r, gain, g):
    gg = g * gain
    a = jnp.mean(gg, axis=-1, keepdims=True)
    b = jnp.mean(gg * xhat, axis=-1, keepdims=True)
    return r * (gg - a - xhat * b)


def gelu_both(x):
    x2 = x * x
    y = (CGELU * AGELU) * x2 + CGELU
    hp = 0.5 * jnp.tanh(x * y) + 0.5
    g = x * hp
    d = hp + (g - g * hp) * (6.0 * y - 4.0 * CGELU)
    return g, d


def pair_masks(rows):
    lane = lax.broadcasted_iota(jnp.int32, (rows, 128), 1)
    return lane < HEAD


def split_heads(x, low_lanes):
    zero = jnp.zeros_like(x)
    return jnp.where(low_lanes, x, zero), jnp.where(low_lanes, zero, x)


def stack_heads(x, low_lanes):
    a, b = split_heads(x, low_lanes)
    return jnp.concatenate([a, b], axis=0)


def word_of_lane(width):
    return (lax.broadcasted_iota(jnp.int32, (16, width), 1) % GROUP) // 16


def compress(blocks, lane_word):
    out = blocks[0:16, :]
    for w in range(1, GROUP // 16):
        out = jnp.where(lane_word == w, blocks[16 * w : 16 * w + 16, :], out)
    return out


def expand(dense, lane_word):
    zero = jnp.zeros_like(dense)
    return jnp.concatenate(
        [jnp.where(lane_word == w, dense, zero) for w in range(GROUP // 16)], axis=0
    )


def pool_weights(am, q_row, cnt_col):
    words = am.shape[0] // 16
    am3 = am.reshape(words, 16, am.shape[1])
    logits = jnp.sum(am * q_row, axis=-1, keepdims=True)
    slot = (lax.broadcasted_iota(jnp.int32, (am.shape[0], 1), 0) % 16).astype(F32)
    logits = jnp.where(slot < cnt_col, logits, MASKED).reshape(words, 16, 1)
    e = jnp.exp(logits - jnp.max(logits, axis=1, keepdims=True))
    w = e / jnp.sum(e, axis=1, keepdims=True)
    return am3, w


def count_column(cnt_row):
    return jnp.transpose(jnp.broadcast_to(cnt_row, (GROUP, GROUP)))[:, 0:1]


def char_fwd_tile(x, cnt, weights):
    g1, wqkv, wout, g2, wup, wdown, pq = weights
    rows = x.shape[0]
    groups = rows // GROUP
    xf = x.astype(F32)
    xhat, _ = ln_parts(xf)
    normed = (xhat * g1).astype(BF16)
    packed = mm(normed, wqkv).astype(BF16)
    low = pair_masks(GROUP)
    lw = word_of_lane(2 * GROUP)
    slot = lax.broadcasted_iota(jnp.int32, (16, 2 * GROUP), 0).astype(F32)
    probs, mixed, cols = [], [], []
    for g in range(groups):
        r = slice(g * GROUP, (g + 1) * GROUP)
        cnt_row = cnt[g : g + 1, :]
        cols.append(count_column(cnt_row))
        cnt2 = jnp.concatenate([cnt_row, cnt_row], axis=1)
        valid = slot < cnt2
        pg, mg = [], []
        for p in range(CHEADS // 2):
            q = packed[r, 128 * p : 128 * p + 128] * BF16(0.125)
            k = packed[r, 256 + 128 * p : 384 + 128 * p]
            v = packed[r, 512 + 128 * p : 640 + 128 * p]
            st = mm_nt(k, stack_heads(q, low))
            s = jnp.where(valid, compress(st, lw), MASKED)
            e = jnp.exp(s - jnp.max(s, axis=0, keepdims=True))
            pr = e / jnp.sum(e, axis=0, keepdims=True)
            pt = expand(pr.astype(BF16), lw)
            o = mm_tn(pt, v)
            pg.append(pr)
            mg.append(jnp.where(low, o[:GROUP], o[GROUP:]))
        probs.append(jnp.concatenate(pg, axis=1))
        mixed.append(jnp.concatenate(mg, axis=1))
    probs = jnp.concatenate(probs, axis=0)
    mixed = jnp.concatenate(mixed, axis=0).astype(BF16)
    aa = xf + mm(mixed, wout)
    ahat, _ = ln_parts(aa)
    middle = (ahat * g2).astype(BF16)
    upper, dgelu = gelu_both(mm(middle, wup))
    upper = upper.astype(BF16)
    am = aa + mm(upper, wdown)
    am3, w = pool_weights(am, pq, jnp.concatenate(cols, axis=0))
    pooled = jnp.sum(w * am3, axis=1)
    return packed, probs, mixed, aa, upper, dgelu.astype(BF16), am, pooled.astype(BF16)


def char_fwd_kernel(x, cnt, g1, wqkv, wout, g2, wup, wdown, pq, *outs):
    weights = (g1[...].astype(F32), wqkv[...], wout[...], g2[...].astype(F32), wup[...], wdown[...], pq[...].astype(F32))
    for ref, val in zip(outs, char_fwd_tile(x[...], cnt[0], weights)):
        ref[...] = val


def full_spec(shape):
    return pl.BlockSpec(shape, lambda i: (0,) * len(shape))


def rows_spec(rows, width):
    return pl.BlockSpec((rows, width), lambda i: (i, 0))


def char_forward(x, cnt, weights):
    total = x.shape[0]
    tiles = total // ROWS
    widths = [(ROWS, 768, BF16), (ROWS // 8, 512, F32), (ROWS, 256, BF16), (ROWS, 256, F32), (ROWS, 1024, BF16), (ROWS, 1024, BF16), (ROWS, 256, F32), (ROWS // 16, 256, BF16)]
    return pl.pallas_call(
        char_fwd_kernel,
        grid=(tiles,),
        in_specs=[rows_spec(ROWS, 256), pl.BlockSpec((1, ROWS // GROUP, GROUP), lambda i: (i, 0, 0))] + [full_spec(w.shape) for w in weights],
        out_specs=[rows_spec(r, w) for r, w, _ in widths],
        out_shape=[jax.ShapeDtypeStruct((r * tiles, w), d) for r, w, d in widths],
        compiler_params=pltpu.CompilerParams(vmem_limit_bytes=VMEM_LIMIT, dimension_semantics=("arbitrary",)),
        name="char_forward",
    )(x, cnt, *weights)


def char_bwd_tile(x, cnt, packed, probs, mixed, aa, upper, dgelu, am, gpool_ref, base, weights):
    g1, wqkv, wout, g2, wup, wdown, pq = weights
    rows = x.shape[0]
    groups = rows // GROUP
    words = rows // 16
    low = pair_masks(GROUP)
    lw = word_of_lane(2 * GROUP)
    cols = jnp.concatenate([count_column(cnt[g : g + 1, :]) for g in range(groups)], axis=0)
    am3, w = pool_weights(am, pq, cols)
    gp = jnp.concatenate(
        [jnp.broadcast_to(gpool_ref[pl.ds(base + i, 1), :], (16, 256)) for i in range(words)], axis=0
    )
    dw = jnp.sum(gp * am, axis=-1, keepdims=True).reshape(words, 16, 1)
    dlog = (w * (dw - jnp.sum(w * dw, axis=1, keepdims=True))).reshape(rows, 1)
    gm = w.reshape(rows, 1) * gp + dlog * pq
    d_pq = jnp.sum(dlog * am, axis=0, keepdims=True)
    gdl = gm.astype(BF16)
    d_down_t = mm_tn(gdl, upper)
    ghid = (dgelu.astype(F32) * mm_nt(gdl, wdown)).astype(BF16)
    ahat, ar = ln_parts(aa)
    middle = (ahat * g2).astype(BF16)
    d_up = mm_tn(middle, ghid)
    gmid = mm_nt(ghid, wup)
    gca = gm + ln_back(ahat, ar, g2, gmid)
    d_g2 = jnp.sum(gmid * ahat, axis=0, keepdims=True)
    gcl = gca.astype(BF16)
    d_out = mm_tn(mixed, gcl)
    gcm = mm_nt(gcl, wout).astype(BF16)
    dqkv = []
    for g in range(groups):
        r = slice(g * GROUP, (g + 1) * GROUP)
        dq_g, dk_g, dv_g = [], [], []
        for p in range(CHEADS // 2):
            q = packed[r, 128 * p : 128 * p + 128] * BF16(0.125)
            k = packed[r, 256 + 128 * p : 384 + 128 * p]
            v = packed[r, 512 + 128 * p : 640 + 128 * p]
            do = stack_heads(gcm[r, 128 * p : 128 * p + 128], low)
            pr = probs[16 * g : 16 * g + 16, 256 * p : 256 * p + 256]
            dp = compress(mm_nt(v, do), lw)
            ds = (pr * (dp - jnp.sum(pr * dp, axis=0, keepdims=True))).astype(BF16)
            dst = expand(ds, lw)
            pt = expand(pr.astype(BF16), lw)
            dv_g.append(mm(pt, do))
            dk_g.append(mm(dst, stack_heads(q, low)))
            o = mm_tn(dst, k)
            dq_g.append(jnp.where(low, o[:GROUP], o[GROUP:]) * 0.125)
        dqkv.append(jnp.concatenate(dq_g + dk_g + dv_g, axis=1))
    dqkv = jnp.concatenate(dqkv, axis=0).astype(BF16)
    xf = x.astype(F32)
    xhat, xr = ln_parts(xf)
    normed = (xhat * g1).astype(BF16)
    d_qkv = mm_tn(normed, dqkv)
    gn = mm_nt(dqkv, wqkv)
    d_g1 = jnp.sum(gn * xhat, axis=0, keepdims=True)
    cg = gca + ln_back(xhat, xr, g1, gn)
    return cg, (d_g1, d_qkv, d_out, d_g2, d_up, d_down_t, d_pq)


def char_bwd_kernel(x, cnt, packed, probs, mixed, aa, upper, dgelu, am, gpool, g1, wqkv, wout, g2, wup, wdown, pq, cg, *accs):
    weights = (g1[...].astype(F32), wqkv[...], wout[...], g2[...].astype(F32), wup[...], wdown[...], pq[...].astype(F32))
    step = pl.program_id(0)

    @pl.when(step == 0)
    def _():
        for acc in accs:
            acc[...] = jnp.zeros_like(acc)

    out, sums = char_bwd_tile(
        x[...], cnt[0], packed[...], probs[...], mixed[...], aa[...], upper[...], dgelu[...], am[...],
        gpool, step * (ROWS // 16), weights,
    )
    cg[...] = out
    for acc, val in zip(accs, sums):
        acc[...] += val


def char_backward(x, cnt, saved, gpool, weights):
    total = x.shape[0]
    tiles = total // ROWS
    widths = [(ROWS, 768), (ROWS // 8, 512), (ROWS, 256), (ROWS, 256), (ROWS, 1024), (ROWS, 1024), (ROWS, 256)]
    acc_shapes = [(1, 256), (256, 768), (256, 256), (1, 256), (256, 1024), (256, 1024), (1, 256)]
    return pl.pallas_call(
        char_bwd_kernel,
        grid=(tiles,),
        in_specs=[rows_spec(ROWS, 256), pl.BlockSpec((1, ROWS // GROUP, GROUP), lambda i: (i, 0, 0))]
        + [rows_spec(r, w) for r, w in widths]
        + [full_spec(gpool.shape)]
        + [full_spec(w.shape) for w in weights],
        out_specs=[rows_spec(ROWS, 256)] + [full_spec(s) for s in acc_shapes],
        out_shape=[jax.ShapeDtypeStruct((total, 256), F32)] + [jax.ShapeDtypeStruct(s, F32) for s in acc_shapes],
        compiler_params=pltpu.CompilerParams(vmem_limit_bytes=VMEM_LIMIT, dimension_semantics=("arbitrary",)),
        name="char_backward",
    )(x, cnt, *saved, gpool, *weights)


def word_kernel(
    axes, nblk,
    xall, start, cot, wq, wk, wv, wout, g2, wup, wdown,
    block_out, rms, gaa, dx, d_q, d_k, d_v, d_out, d_g2, d_up, d_down,
    kk, vv, kt, vt, ss, ee, qm, dom, mx, ll, ot, dqt, wkt, wvt, dk_acc, dv_acc, dlt, dk_sum, dv_sum, dx_own,
):
    own = axes()
    blk = start.shape[0]
    low = pair_masks(blk)

    def rows(j):
        return pl.ds(pl.multiple_of(j * blk, blk), blk)

    wkt[...] = jnp.transpose(wk[...])
    wvt[...] = jnp.transpose(wv[...])
    xown = xall[rows(own), :]
    q = mm(xown, wq[...]).astype(BF16) * BF16(0.125)
    for p in range(HEADS // 2):
        a, b = split_heads(q[:, 128 * p : 128 * p + 128], low)
        qm[2 * p] = a
        qm[2 * p + 1] = b
    mx[...] = jnp.full(mx.shape, MASKED, F32)
    ll[...] = jnp.zeros(ll.shape, F32)
    ot[...] = jnp.zeros(ot.shape, F32)
    dqt[...] = jnp.zeros(dqt.shape, F32)
    dk_sum[...] = jnp.zeros(dk_sum.shape, F32)
    dv_sum[...] = jnp.zeros(dv_sum.shape, F32)
    dx[...] = jnp.zeros(dx.shape, BF16)

    half = HEADS // 2

    def scores_of(j, heads):
        for h in heads:
            p = h // 2
            s = mm_nt(kk[j, :, 128 * p : 128 * p + 128], qm[h])
            ss[j, h % half] = s
            mx[h] = jnp.maximum(mx[h], jnp.max(s.reshape(blk // 8, 8, blk), axis=0))

    def mix_of(j, heads):
        for h in heads:
            e = jnp.exp(ss[j, h % half] - mx[h, 0:1, :])
            ll[h] += jnp.sum(e.reshape(blk // 8, 8, blk), axis=0)
            eb = e.astype(BF16)
            ee[j, h] = eb
            ot[64 * h : 64 * h + 64, :] += mm(vt[j, 64 * h : 64 * h + 64, :], eb)

    def top_of(heads):
        for h in heads:
            mx[h] = jnp.broadcast_to(jnp.max(mx[h], axis=0, keepdims=True), (8, blk))

    first, second = range(half), range(half, HEADS)

    @pl.loop(0, own + 1)
    def _(j):
        xj = xall[rows(j), :]
        kk[j] = mm(xj, wk[...]).astype(BF16)
        vv[j] = mm(xj, wv[...]).astype(BF16)
        kt[j] = mm_nt(wkt[...], xj).astype(BF16)
        vt[j] = mm_nt(wvt[...], xj).astype(BF16)
        scores_of(j, first)

    top_of(first)

    @pl.loop(0, own + 1)
    def _(j):
        mix_of(j, first)
        scores_of(j, second)

    top_of(second)

    @pl.loop(0, own + 1)
    def _(j):
        mix_of(j, second)

    for h in range(HEADS):
        linv = 1.0 / jnp.sum(ll[h], axis=0, keepdims=True)
        ll[h] = jnp.broadcast_to(linv, (8, blk))
        ot[64 * h : 64 * h + 64, :] = ot[64 * h : 64 * h + 64, :] * linv
    mixed_t = ot[...].astype(BF16)
    attn = mm(jnp.transpose(mixed_t), wout[...])
    awa = start[...] + attn
    ahat, ar = ln_parts(awa)
    g2v = g2[...].astype(F32)
    n2 = (ahat * g2v).astype(BF16)
    upper, dgelu = gelu_both(mm(n2, wup[...]))
    upper = upper.astype(BF16)
    mlp = mm(upper, wdown[...])
    final = awa + mlp
    block_out[...] = final.astype(BF16)
    lane = lax.broadcasted_iota(jnp.int32, (blk, 128), 1)
    cols = [jnp.sqrt(jnp.mean(v * v, axis=-1, keepdims=True)) for v in (attn, mlp, final)]
    rms[...] = jnp.transpose(jnp.where(lane == 0, cols[0], jnp.where(lane == 1, cols[1], cols[2])))[0:8, :]
    cotv = cot[...]
    d_down[...] = mm_tn(upper, cotv).astype(BF16)
    ghid = (dgelu * mm_nt(cotv, wdown[...])).astype(BF16)
    d_up[...] = mm_tn(n2, ghid).astype(BF16)
    gn2 = mm_nt(ghid, wup[...])
    d_g2[...] = jnp.sum(gn2 * ahat, axis=0, keepdims=True)
    ga = cotv.astype(F32) + ln_back(ahat, ar, g2v, gn2)
    gaa[...] = ga
    gal = ga.astype(BF16)
    d_out[...] = mm(mixed_t, gal).astype(BF16)
    do_t = mm_nt(wout[...], gal).astype(BF16)
    do_s = []
    for h in range(HEADS):
        r = slice(64 * h, 64 * h + 64)
        d = do_t[r, :].astype(F32)
        linv = ll[h, 0:1, :]
        dlt[h] = jnp.broadcast_to(jnp.sum(d * ot[r, :], axis=0, keepdims=True) * linv, (8, blk))
        do_s.append((d * linv).astype(BF16))
    do = jnp.transpose(jnp.concatenate(do_s, axis=0))
    for p in range(HEADS // 2):
        a, b = split_heads(do[:, 128 * p : 128 * p + 128], low)
        dom[2 * p] = a
        dom[2 * p + 1] = b

    def back_of(j, _):
        for p in range(HEADS // 2):
            c = slice(128 * p, 128 * p + 128)
            vp = vv[j, :, c]
            dk = None
            for h in (2 * p, 2 * p + 1):
                e = ee[j, h]
                dp = mm_nt(vp, dom[h])
                ds = (e.astype(F32) * (dp - dlt[h, 0:1, :])).astype(BF16)
                dvh = mm(e, dom[h])
                dkh = mm(ds, qm[h])
                dk, dv = (dkh, dvh) if dk is None else (dk + dkh, dv + dvh)
                dqt[64 * h : 64 * h + 64, :] += mm(kt[j, 64 * h : 64 * h + 64, :], ds)
            dk_acc[:, c] = dk.astype(BF16)
            dv_acc[:, c] = dv.astype(BF16)
        dk = dk_acc[...]
        dv = dv_acc[...]
        xj = xall[rows(j), :]
        dxj = mm_nt(dk, wk[...]) + mm_nt(dv, wv[...])
        dx[rows(j), :] = dxj.astype(BF16)
        dx_own[...] = dxj
        xt = jnp.transpose(xj)
        dk_sum[...] += mm(xt, dk)
        dv_sum[...] += mm(xt, dv)
        return 0

    lax.fori_loop(0, own + 1, back_of, 0)
    dq = jnp.transpose((dqt[...] * 0.125).astype(BF16))
    d_q[...] = mm_tn(xown, dq).astype(BF16)
    d_k[...] = dk_sum[...].astype(BF16)
    d_v[...] = dv_sum[...].astype(BF16)
    dx[rows(own), :] = (dx_own[...] + mm_nt(dq, wq[...])).astype(BF16)


def word_section(xall, start, cot, wq, wk, wv, wout, g2, wup, wdown):
    blk, width = start.shape
    nblk = xall.shape[0] // blk
    ff = wup.shape[1]

    def axes():
        return lax.axis_index("ctx") * lax.axis_size("tp") + lax.axis_index("tp")

    out_shapes = [((blk, width), BF16), ((8, blk), F32), ((blk, width), F32), ((nblk * blk, width), BF16)]
    out_shapes += [((width, width), BF16)] * 4 + [((1, width), F32), ((width, ff), BF16), ((ff, width), BF16)]
    vm = pl.BlockSpec(memory_space=pltpu.VMEM)
    return pl.pallas_call(
        functools.partial(word_kernel, axes, nblk),
        in_specs=[vm] * 10,
        out_specs=[vm] * len(out_shapes),
        out_shape=[jax.ShapeDtypeStruct(s, d) for s, d in out_shapes],
        scratch_shapes=[
            pltpu.VMEM((nblk, blk, width), BF16),
            pltpu.VMEM((nblk, blk, width), BF16),
            pltpu.VMEM((nblk, width, blk), BF16),
            pltpu.VMEM((nblk, width, blk), BF16),
            pltpu.VMEM((nblk, HEADS // 2, blk, blk), F32),
            pltpu.VMEM((nblk, HEADS, blk, blk), BF16),
            pltpu.VMEM((HEADS, blk, 128), BF16),
            pltpu.VMEM((HEADS, blk, 128), BF16),
            pltpu.VMEM((HEADS, 8, blk), F32),
            pltpu.VMEM((HEADS, 8, blk), F32),
            pltpu.VMEM((width, blk), F32),
            pltpu.VMEM((width, blk), F32),
            pltpu.VMEM((width, width), BF16),
            pltpu.VMEM((width, width), BF16),
            pltpu.VMEM((blk, width), BF16),
            pltpu.VMEM((blk, width), BF16),
            pltpu.VMEM((HEADS, 8, blk), F32),
            pltpu.VMEM((width, width), F32),
            pltpu.VMEM((width, width), F32),
            pltpu.VMEM((blk, width), F32),
        ],
        compiler_params=pltpu.CompilerParams(vmem_limit_bytes=VMEM_LIMIT),
        name="word_section",
    )(xall, start, cot, wq, wk, wv, wout, g2, wup, wdown)


def gather(x, name, axis):
    return lax.all_gather(x, name, axis=axis, tiled=True)


def scatter(x, name, axis):
    return lax.psum_scatter(x, name, scatter_dimension=axis, tiled=True)


def local(characters, counts, words_in, cotangent, char_prenorm, char_qkv, char_out, char_midnorm, char_up, char_down,
          pool_query, char_proj, word_prenorm, word_qkv, word_out, word_midnorm, word_up, word_down):
    words, slots, cdim = characters.shape
    x = characters.reshape(words * slots, cdim)
    cnt = jnp.repeat(counts.astype(F32), slots).reshape(words * slots // ROWS, ROWS // GROUP, GROUP)
    names = (char_prenorm, char_qkv, char_out, char_midnorm, char_up, char_down, pool_query)
    weights = [gather(w, "fsdp", 0) for w in names]
    weights = [w.reshape(1, -1) if w.ndim == 1 else w for w in weights]
    proj = gather(char_proj, "fsdp", 0)
    g_word1 = gather(word_prenorm, "fsdp", 0).astype(F32)
    g_word2 = gather(word_midnorm, "fsdp", 0).reshape(1, -1)
    wqkv = gather(gather(jnp.moveaxis(word_qkv, 1, 0), "fsdp", 1), "tp", 2)
    wout = gather(gather(word_out, "fsdp", 1), "tp", 0)
    wup = gather(gather(word_up, "fsdp", 0), "tp", 1)
    wdown = gather(gather(word_down, "fsdp", 1), "tp", 0)

    *saved, pooled_low = char_forward(x, cnt, weights)
    start = words_in.astype(F32) + mm(pooled_low, proj)
    shat, sr = ln_parts(start)
    normed_first = (shat * g_word1).astype(BF16)
    xall = gather(normed_first, ("ctx", "tp"), 0)
    (block_out, rms, gaa, dx, d_q, d_k, d_v, d_wout, d_g2w, d_wup, d_wdown) = word_section(
        xall, start, cotangent, wqkv[0], wqkv[1], wqkv[2], wout, g_word2, wup, wdown
    )
    gnf = scatter(dx.astype(BF16), ("ctx", "tp"), 0).astype(F32)
    words_grad = gaa + ln_back(shat, sr, g_word1, gnf)
    d_g1w = jnp.sum(gnf * shat, axis=0)
    gproj = words_grad.astype(BF16)
    d_proj = mm_tn(pooled_low, gproj)
    gpool = mm_nt(gproj, proj)
    cg, d_g1, d_qkv, d_out, d_g2, d_up, d_down_t, d_pq = char_backward(x, cnt, saved, gpool, weights)

    def reduce_char(g):
        g = lax.psum(g.astype(BF16), ("ctx", "tp"))
        return scatter(g, "fsdp", 0).astype(F32)

    def reduce_word(g, tp_axis, fsdp_axis):
        g = scatter(g.astype(BF16), "tp", tp_axis)
        g = lax.psum(g, "ctx")
        return scatter(g, "fsdp", fsdp_axis).astype(F32)

    d_wqkv = reduce_word(jnp.stack([d_q, d_k, d_v], axis=0), 2, 1)
    return (
        block_out,
        cg.reshape(words, slots, cdim),
        words_grad,
        rms[:3],
        reduce_char(d_g1[0]),
        reduce_char(d_qkv),
        reduce_char(d_out),
        reduce_char(d_g2[0]),
        reduce_char(d_up),
        reduce_char(d_down_t.T),
        reduce_char(d_pq[0]),
        reduce_char(d_proj),
        reduce_char(d_g1w),
        jnp.moveaxis(d_wqkv, 0, 1),
        reduce_word(d_wout, 0, 1),
        reduce_char(d_g2w[0]),
        reduce_word(d_wup, 1, 0),
        reduce_word(d_wdown, 0, 1),
    )


def solution(mesh):
    rows = ("fsdp", "ctx", "tp")
    v, m = P("fsdp"), P("fsdp", None)
    return jax.shard_map(
        local,
        mesh=mesh,
        in_specs=(
            P(rows, None, None), P(rows), P(rows, None), P(rows, None),
            v, m, m, v, m, m, v, m, v, P("fsdp", None, "tp"), P("tp", "fsdp"), v, P("fsdp", "tp"), P("tp", "fsdp"),
        ),
        out_specs=(
            P(rows, None), P(rows, None, None), P(rows, None), P(None, rows),
            v, m, m, v, m, m, v, m, v, P("fsdp", None, "tp"), P("tp", "fsdp"), v, P("fsdp", "tp"), P("tp", "fsdp"),
        ),
        check_vma=False,
    )
```

time: 1020 us -> 730 us (0.72)
  matrix products: 258 us -> 3.13 us
  local copies, waits for them, and re-layouts: 131 us -> 23.2 us
  Pallas kernels: 0 us -> 93.3 us
  other arithmetic: 96.4 us -> 24 us
  waiting for transfers between devices: 301 us -> 351 us
    dot_general x47 -> x3, matrix products: 258 us -> 3.13 us  [the longest x1 1.21 us: mm(): lax.dot_general(a, b, (((1,), (0,)), ((), ())), preferred_element_type=F32)]
    pallas_call x0 -> x3, Pallas kernels: none -> 93.3 us  [the longest x1 44.1 us: char_backward(): pl.pallas_call(char_bwd_kernel, grid=(tiles,), in_specs=[rows_spec(ROWS,...]
    unnamed x23, waiting for transfers between devices: 9.47 us -> 73.5 us
    all_gather x4, waiting for transfers between devices: 47.8 us -> 0.02 us  [gather(): return lax.all_gather(x, name, axis=axis, tiled=True)]
    convert_element_type x4 -> x0, local copies, waits for them, and re-layouts: 44.2 us -> none  [the longest x2 38.8 us: local(): grad_char_packed = char_attend_back(packed, present, char_scale, grad_cha...]
    reduce_sum x19 -> x2, other arithmetic: 34.1 us -> 1.46 us  [the longest x1 1.27 us: local(): d_g1w = jnp.sum(gnf * shat, axis=0)]
    reshape x4 -> x3, local copies, waits for them, and re-layouts: 29.4 us -> 1.7 us  [local(): weights = [w.reshape(1, -1) if w.ndim == 1 else w for w in weights]]
    reduce_scatter x13 -> x11, waiting for transfers between devices: 219 us -> 237 us  [scatter(): return lax.psum_scatter(x, name, scatter_dimension=axis, tiled=True)]
  transfers between devices with their start and end apart: 21 -> 20, of which waited for: 16 -> 15; matrix products, arithmetic and copies ran while one was open for 24% -> 6% of each run, Pallas kernels for 0% -> 10%
where the time goes in v1:
time: 730 us; the launch traced here: 729 us
  waiting for transfers between devices  351 us (48%)
  blocking collectives  217 us (30%)
  Pallas kernels  93.3 us (13%)
  other arithmetic  24 us (3%)
  local copies, waits for them, and re-layouts  23.2 us (3%)
  between operations  16.8 us (2%)
    reduce_scatter x11, waiting for transfers between devices, scatter(): return lax.psum_scatter(x, name, scatter_dimension=axis, tiled=True)  237 us
    all_gather x12, blocking collectives, gather(): return lax.all_gather(x, name, axis=axis, tiled=True)  166 us
    unnamed x23, waiting for transfers between devices  73.5 us
    pallas_call x1, Pallas kernels, char_backward(): pl.pallas_call(char_bwd_kernel, grid=(tiles,), in_specs=[rows_spec(ROWS,...  44.1 us
    pallas_call x1, Pallas kernels, char_forward(): pl.pallas_call(char_fwd_kernel, grid=(tiles,), in_specs=[rows_spec(ROWS,...  31.6 us
    psum x1, blocking collectives, reduce_char(): g = lax.psum(g.astype(BF16), ('ctx', 'tp'))  28.4 us
    psum x1, waiting for transfers between devices, reduce_char(): g = lax.psum(g.astype(BF16), ('ctx', 'tp'))  24.8 us
    unnamed x2, blocking collectives  18.5 us
  transfers between devices with their start and end apart: 20, of which 15 were waited for; matrix products, arithmetic and copies ran while one was open for 6% of the time, Pallas kernels for 10%

profile of v1, /device:TPU:0, one launch (start us, length us, event | category | flops | bytes accessed | tf_op | source)
XLA Modules:
  0.0 728.8 jit_solution(13957279227434476592)
XLA Ops:
  7.3 18.4 %all_gather.67 = bf16[3,512,128]{2,1,0:T(8,128)(2,1)} all-gather(bf16[3,128,128]{2,1,0:T(8,128)(2,1)} %bitcast.47), channel_id=1, replica_groups=mesh['fsdp'=4,'ctx'=2,'tp'=4] {'fsdp'}, dimensions={1}, use_global_device_ids=true | all-gather | bytes 491520 | tf_op jit(solution)/shard_map/all_gather | solution.py:470
  25.8 16.6 %all_gather.72 = bf16[512,512]{1,0:T(8,128)(2,1)} all-gather(bf16[128,512]{1,0:T(8,128)(2,1)} %param.34), channel_id=1, replica_groups=mesh['fsdp'=4,'ctx'=2,'tp'=4] {'fsdp'}, dimensions={0}, use_global_device_ids=true | all-gather | bytes 655360 | tf_op jit(solution)/shard_map/all_gather | solution.py:470
  42.5 15.3 %all_gather.74 = bf16[512,512]{1,0:T(8,128)(2,1)} all-gather(bf16[512,128]{1,0:T(8,128)(2,1)S(1)} %copy-done.11), channel_id=1, replica_groups=mesh['fsdp'=4,'ctx'=2,'tp'=4] {'fsdp'}, dimensions={1}, use_global_device_ids=true | all-gather | bytes 655360 | tf_op jit(solution)/shard_map/all_gather | solution.py:470
  59.9 9.6 %all-reduce.11 = (bf16[256]{0:T(256)(128)(2,1)S(1)}, bf16[256]{0:T(256)(128)(2,1)S(1)}, bf16[256]{0:T(256)(128)(2,1)S(1)}) all-reduce(bf16[256]{0:T(256)(128)(2,1)S(1)} %dynamic-update-slice, bf16[256]{0:T(256)(128)(2,1)S(1)} %dynamic-update-slice.1, bf16[256]{0:T(256)(128)(2,1)S(1)} %dynamic-update-slice.2), channel_id=1, replica_groups=mesh['fsdp'=4,'ctx'=2,'tp'=4] {'fsdp'}, use_global_device_ids=true, to_apply=%add | all-reduce | flops 768 | bytes 3072
  71.4 0.7 broadcast_in_dim.15.cnt
  72.1 8.3 %all-gather = bf16[4,1,128]{2,1,0:T(2,128)(2,1)S(1)} all-gather(bf16[1,1,128]{2,1,0:T(2,128)(2,1)S(1)} %bitcast.53), channel_id=1, replica_groups=mesh['fsdp'=4,'ctx'=2,'tp'=4] {'fsdp'}, dimensions={0}, use_global_device_ids=true | all-gather | bytes 1280 | tf_op jit(solution)/shard_map/all_gather | solution.py:470
  80.4 14.3 %all_gather.59.wout = bf16[256,256]{1,0:T(8,128)(2,1)} all-gather(bf16[64,256]{1,0:T(8,128)(2,1)S(1)} %copy-done.16), channel_id=1, replica_groups=mesh['fsdp'=4,'ctx'=2,'tp'=4] {'fsdp'}, dimensions={0}, use_global_device_ids=true | all-gather | bytes 163840 | tf_op jit(solution)/shard_map/all_gather | solution.py:470
  94.7 15.1 %all_gather.58.wqkv = bf16[256,768]{1,0:T(8,128)(2,1)} all-gather(bf16[64,768]{1,0:T(8,128)(2,1)S(1)} %copy-done.14), channel_id=1, replica_groups=mesh['fsdp'=4,'ctx'=2,'tp'=4] {'fsdp'}, dimensions={0}, use_global_device_ids=true | all-gather | bytes 491520 | tf_op jit(solution)/shard_map/all_gather | solution.py:470
  109.9 16.8 %all_gather.61.wup = bf16[256,1024]{1,0:T(8,128)(2,1)} all-gather(bf16[64,1024]{1,0:T(8,128)(2,1)S(1)} %copy-done.12), channel_id=1, replica_groups=mesh['fsdp'=4,'ctx'=2,'tp'=4] {'fsdp'}, dimensions={0}, use_global_device_ids=true | all-gather | bytes 655360 | tf_op jit(solution)/shard_map/all_gather | solution.py:470
  126.6 15.5 %all_gather.62.wdown = bf16[1024,256]{1,0:T(8,128)(2,1)} all-gather(bf16[256,256]{1,0:T(8,128)(2,1)S(1)} %copy-done.13), channel_id=1, replica_groups=mesh['fsdp'=4,'ctx'=2,'tp'=4] {'fsdp'}, dimensions={0}, use_global_device_ids=true | all-gather | bytes 655360 | tf_op jit(solution)/shard_map/all_gather | solution.py:470
  142.2 31.6 %char_forward.1 = (bf16[4096,768]{1,0:T(8,128)(2,1)}, f32[512,512]{1,0:T(8,128)}, bf16[4096,256]{1,0:T(8,128)(2,1)}, f32[4096,256]{1,0:T(8,128)}, bf16[4096,1024...) custom-call(bf16[4096,256]{1,0:T(8,128)(2,1)} %bitcast.37, ...), custom_call_target="tpu_custom_call" | custom-call | tf_op jit(solution)/shard_map/char_forward/pallas_call | solution.py:170
  173.8 14.4 %all_gather.64 = bf16[256,512]{1,0:T(8,128)(2,1)S(1)} all-gather(bf16[64,512]{1,0:T(8,128)(2,1)S(1)} %copy-done.15), channel_id=1, replica_groups=mesh['fsdp'=4,'ctx'=2,'tp'=4] {'fsdp'}, dimensions={0}, use_global_device_ids=true | all-gather | bytes 327680 | tf_op jit(solution)/shard_map/all_gather | solution.py:470
  188.2 1.2 fusion.12
  189.7 0.9 multiply_convert_fusion
  190.6 8.7 %all-gather.1 = bf16[4,1,128]{2,1,0:T(2,128)(2,1)} all-gather(bf16[1,1,128]{2,1,0:T(2,128)(2,1)S(1)} %bitcast.54), channel_id=1, replica_groups=mesh['fsdp'=4,'ctx'=2,'tp'=4] {'fsdp'}, dimensions={0}, use_global_device_ids=true | all-gather | bytes 1280 | tf_op jit(solution)/shard_map/all_gather | solution.py:470
  199.3 12.2 %all_gather.69 = bf16[128,512]{1,0:T(8,128)(2,1)S(1)} all-gather(bf16[128,128]{1,0:T(8,128)(2,1)S(1)} %copy-done.17), channel_id=1, replica_groups=mesh['fsdp'=4,'ctx'=2,'tp'=4] {'fsdp'}, dimensions={1}, use_global_device_ids=true | all-gather | bytes 163840 | tf_op jit(solution)/shard_map/all_gather | solution.py:470
  211.5 10.8 %all_gather.70.wout = bf16[512,512]{1,0:T(8,128)(2,1)} all-gather(bf16[128,512]{1,0:T(8,128)(2,1)S(1)} %all_gather.69), channel_id=1, replica_groups=mesh['fsdp'=4,'ctx'=2,'tp'=4] {'tp'}, dimensions={0}, use_global_device_ids=true | all-gather | bytes 655360 | tf_op jit(solution)/shard_map/all_gather | solution.py:470
  222.3 2.5 slice_bitcast_fusion
  224.9 17.6 %word_section.1 = (bf16[256,512]{1,0:T(8,128)(2,1)}, f32[8,256]{1,0:T(8,128)}, f32[256,512]{1,0:T(8,128)}, bf16[2048,512]{1,0:T(8,128)(2,1)}, bf16[512,512]{1,0:...) custom-call(bf16[2048,512]{1,0:T(8,128)(2,1)} %all-gather.7.cloned.1, ...), custom_call_target="tpu_custom_call" | custom-call | tf_op jit(solution)/shard_map/word_section/pallas_call | solution.py:437
  243.2 0.7 reduce-scatter.27.cloned.1.call-update
  244.0 1.3 pad_maximum_fusion
  245.3 3.2 copy.38
  248.5 1.7 copy.44
  250.2 0.7 reduce-scatter.25.cloned.1.call-update
  251.0 56.0 %reduce-scatter.21.cloned.1.call-done = bf16[256,512]{1,0:T(8,128)(2,1)} async-done(((bf16[2048,512]{1,0:T(8,128)(2,1)}), bf16[256,512]{1,0:T(8,128)(2,1)}) %reduce-scatter.21.cloned.1.call-update) | async-done | bytes 262160 | tf_op jit(solution)/shard_map/reduce_scatter | solution.py:474
  307.0 1.3 fusion.7
  308.3 1.2 fusion.5
  309.5 1.0 convolution_convert_fusion
  310.7 1.0 fusion.9.gpool
  311.7 44.1 %char_backward.1 = (f32[4096,256]{1,0:T(8,128)}, f32[1,256]{1,0:T(1,128)}, f32[256,768]{1,0:T(8,128)}, f32[256,256]{1,0:T(8,128)}, f32[1,256]{1,0:T(1,128)}, /*i...) custom-call(bf16[4096,256]{1,0:T(8,128)(2,1)} %bitcast.38, f32[8,4,128]{2,1,0:T(4,128)} %broadcast_in_dim.15.cnt, ...), custom_call_target="tpu_custom_call" | custom-call | tf_op jit(solution)/shard_map/char_backward/pallas_call | solution.py:262
  355.8 2.1 convert_element_type.112
  357.9 2.2 convert_element_type.119
  360.2 0.9 convert_bitcast_fusion
  361.1 1.7 copy.40
  362.9 10.0 %reduce-scatter.27.cloned.1.call-done = bf16[512,512]{1,0:T(8,128)(2,1)} async-done(((bf16[2048,512]{1,0:T(8,128)(2,1)}), bf16[512,512]{1,0:T(8,128)(2,1)}) %reduce-scatter.27.cloned.1.call-update) | async-done | bytes 524304 | tf_op jit(solution)/shard_map/reduce_scatter | solution.py:474
  372.9 2.0 copy.42
  375.1 32.1 %reduce-scatter.43.cloned.1.call-done = bf16[128,1536]{1,0:T(8,128)(2,1)} async-done(((bf16[512,1536]{1,0:T(8,128)(2,1)}), bf16[128,1536]{1,0:T(8,128)(2,1)}) %reduce-scatter.43.cloned.1.call-update) | async-done | bytes 393232
  407.2 1.7 reshape.109
  408.8 1.1 copy.39
  410.0 35.6 %reduce-scatter.25.cloned.1.call-done = bf16[512,512]{1,0:T(8,128)(2,1)} async-done(((bf16[512,2048]{1,0:T(8,128)(2,1)}), bf16[512,512]{1,0:T(8,128)(2,1)}) %reduce-scatter.25.cloned.1.call-update) | async-done | bytes 524304 | tf_op jit(solution)/shard_map/reduce_scatter | solution.py:474
  445.7 0.7 convert_element_type.114
  446.4 21.5 %reduce-scatter.37.cloned.1.call-done = bf16[64,512]{1,0:T(8,128)(2,1)} async-done(((bf16[256,512]{1,0:T(8,128)(2,1)}), bf16[64,512]{1,0:T(8,128)(2,1)}) %reduce-scatter.37.cloned.1.call-update) | async-done | bytes 65552 | tf_op jit(solution)/shard_map/reduce_scatter | solution.py:474
  468.0 21.2 %reduce-scatter.29.cloned.1.call-done = bf16[64,768]{1,0:T(8,128)(2,1)} async-done(((bf16[256,768]{1,0:T(8,128)(2,1)}), bf16[64,768]{1,0:T(8,128)(2,1)}) %reduce-scatter.29.cloned.1.call-update) | async-done | bytes 98320 | tf_op jit(solution)/shard_map/reduce_scatter | solution.py:474
  489.2 22.0 %reduce-scatter.33.cloned.1.call-done = bf16[64,1024]{1,0:T(8,128)(2,1)} async-done(((bf16[256,1024]{1,0:T(8,128)(2,1)}), bf16[64,1024]{1,0:T(8,128)(2,1)}) %reduce-scatter.33.cloned.1.call-update) | async-done | bytes 131088 | tf_op jit(solution)/shard_map/reduce_scatter | solution.py:474
  511.2 22.2 %reduce-scatter.35.cloned.1.call-done = bf16[256,256]{0,1:T(8,128)(2,1)} async-done(((bf16[1024,256]{0,1:T(8,128)(2,1)}), bf16[256,256]{0,1:T(8,128)(2,1)}) %reduce-scatter.35.cloned.1.call-update) | async-done | bytes 131088 | tf_op jit(solution)/shard_map/reduce_scatter | solution.py:474
  535.4 18.2 %reduce-scatter.45.cloned.1.call-done = bf16[128,128]{1,0:T(8,128)(2,1)} async-done(((bf16[512,128]{1,0:T(8,128)(2,1)}), bf16[128,128]{1,0:T(8,128)(2,1)}) %reduce-scatter.45.cloned.1.call-update) | async-done | bytes 32784
  553.6 0.9 copy.41
  554.5 21.1 %reduce-scatter.47.cloned.1.call-done = bf16[128,512]{1,0:T(8,128)(2,1)} async-done(((bf16[512,512]{1,0:T(8,128)(2,1)}), bf16[128,512]{1,0:T(8,128)(2,1)}) %reduce-scatter.47.cloned.1.call-update) | async-done | bytes 131088
  575.6 1.7 copy.43
  577.3 19.5 %reduce-scatter.39.cloned.1.call-done = bf16[3,128,128]{2,1,0:T(8,128)(2,1)} async-done(((bf16[3,512,128]{2,1,0:T(8,128)(2,1)}), bf16[3,128,128]{2,1,0:T(8,128)(2,1)}) %reduce-scatter.39.cloned.1.call-update) | async-done | bytes 98320 | tf_op jit(solution)/shard_map/reduce_scatter | solution.py:474
  596.8 22.1 %reduce-scatter.41.cloned.1.call-done = bf16[128,512]{1,0:T(8,128)(2,1)} async-done(((bf16[512,512]{1,0:T(8,128)(2,1)}), bf16[128,512]{1,0:T(8,128)(2,1)}) %reduce-scatter.41.cloned.1.call-update) | async-done | bytes 131088 | tf_op jit(solution)/shard_map/reduce_scatter | solution.py:474
  618.9 3.4 psum.122
  623.0 8.9 %all-reduce.10 = (bf16[256]{0:T(256)(128)(2,1)S(1)}, bf16[256]{0:T(256)(128)(2,1)S(1)}, bf16[256]{0:T(256)(128)(2,1)S(1)}, bf16[512]{0:T(512)(128)(2,1)S(1)}, bf16[512]{0:T(512)(128)(2,1)S(1)}) all-reduce(bf16[256]{0:T(256)(128)(2,1)S(1)} %convert_reduce_fusion.3, ...), channel_id=3, replica_groups=mesh['fsdp'=4,'ctx'=2,'tp'=4] {'fsdp'}, use_global_device_ids=true, to_apply=%region_6.0.clone | all-reduce | flops 1792 | bytes 7168
  632.3 6.7 reduce-scatter.31.cloned.1.call-done
  639.0 28.4 %all-reduce.8 = (bf16[64]{0:T(256)(128)(2,1)S(1)}, bf16[64,256]{1,0:T(8,128)(2,1)S(1)}, bf16[64]{0:T(256)(128)(2,1)S(1)}, bf16[64]{0:T(256)(128)(2,1)S(1)}, bf16...) all-reduce(bf16[64]{0:T(256)(128)(2,1)S(1)} %dynamic-slice.4, ...), channel_id=1, replica_groups=mesh['fsdp'=4,'ctx'=2,'tp'=4] {'ctx','tp'}, use_global_device_ids=true, to_apply=%region_5.0 | all-reduce | flops 16832 | bytes 67328 | tf_op jit(solution)/shard_map/psum | solution.py:510
  670.5 24.8 %all-reduce.16.cloned.1.call-done = (bf16[256,256]{0,1:T(8,128)(2,1)}, bf16[64,768]{1,0:T(8,128)(2,1)}, bf16[64,1024]{1,0:T(8,128)(2,1)}, bf16[64,512]{1,0:T(8,128)(2,1)}) async-done(((bf16[256,256]{0,1:T(8,128)(2,1)}, bf16[64,768]{1,0:T(8,128)(2,1)}, bf16[64,1024]{1,0:T(8,128)(2,1)}, bf16[64,512]{1,0:T(8,128)(2,1)}), (bf16[256,256]{0,1:T(8,128)(2,1)}, bf16[64,768]{1,0:T(8,128)(2,1)}, ...) | async-done | bytes 426000 | tf_op jit(solution)/shard_map/psum | solution.py:510
  695.4 1.6 convert_element_type.120
  697.0 1.7 copy.37
  698.7 1.6 convert_element_type.113
  700.3 1.5 convert_element_type.128
  701.8 15.4 %all-reduce.18.cloned.1.call-done = (bf16[3,128,128]{2,1,0:T(8,128)(2,1)}, bf16[128,512]{1,0:T(8,128)(2,1)}, bf16[512,128]{1,0:T(8,128)(2,1)}) async-done(((bf16[3,128,128]{2,1,0:T(8,128)(2,1)}, bf16[128,512]{1,0:T(8,128)(2,1)}, bf16[512,128]{1,0:T(8,128)(2,1)}), (bf16[3,128,128]{2,1,0:T(8,128)(2,1)}, bf16[128,512]{1,0:T(8,128)(2,1)}, bf16[512,128]{1,0:T(8,128)(2,1)})) %all-reduce.18.cloned.1.call-update) | async-done | bytes 360464 | tf_op jit(solution)/shard_map/psum | solution.py:515
  717.2 1.6 convert_element_type.135
  718.8 1.6 convert_element_type.136
  720.4 1.6 convert_bitcast_fusion.1
  (138 shorter events, 10.3 us)
Async XLA Ops:
  7.2 50.7 %copy-start.18 = (u32[32]{0:T(128)S(1)}, u32[32]{0:T(128)}, u32[]{:S(2)}) copy-start(u32[32]{0:T(128)} %constant.12) | copy-start | bytes 388
  7.2 35.3 %copy-start.11 = (bf16[512,128]{1,0:T(8,128)(2,1)S(1)}, bf16[512,128]{1,0:T(8,128)(2,1)}, u32[]{:S(2)}) copy-start(bf16[512,128]{1,0:T(8,128)(2,1)} %param.35) | copy-start | bytes 393220
  7.2 51.9 %copy-start.27 = (bf16[64]{0:T(256)(128)(2,1)S(1)}, bf16[64]{0:T(256)(128)(2,1)}, u32[]{:S(2)}) copy-start(bf16[64]{0:T(256)(128)(2,1)} %param.22) | copy-start | bytes 388
  7.2 52.2 %copy-start.28 = (bf16[64]{0:T(256)(128)(2,1)S(1)}, bf16[64]{0:T(256)(128)(2,1)}, u32[]{:S(2)}) copy-start(bf16[64]{0:T(256)(128)(2,1)} %param.25) | copy-start | bytes 388
  7.2 52.4 %copy-start.29 = (bf16[64]{0:T(256)(128)(2,1)S(1)}, bf16[64]{0:T(256)(128)(2,1)}, u32[]{:S(2)}) copy-start(bf16[64]{0:T(256)(128)(2,1)} %param.28) | copy-start | bytes 388
  7.2 63.9 %copy-start.21 = (s32[256]{0:T(256)S(1)}, s32[256]{0:T(256)}, u32[]{:S(2)}) copy-start(s32[256]{0:T(256)} %param.19) | copy-start | bytes 3076
  7.3 64.8 %copy-start.22 = (bf16[128]{0:T(256)(128)(2,1)S(1)}, bf16[128]{0:T(256)(128)(2,1)}, u32[]{:S(2)}) copy-start(bf16[128]{0:T(256)(128)(2,1)} %param.30) | copy-start | bytes 772
  7.3 73.1 %copy-start.16 = (bf16[64,256]{1,0:T(8,128)(2,1)S(1)}, bf16[64,256]{1,0:T(8,128)(2,1)}, u32[]{:S(2)}) copy-start(bf16[64,256]{1,0:T(8,128)(2,1)} %param.24) | copy-start | bytes 98308
  7.3 87.4 %copy-start.14 = (bf16[64,768]{1,0:T(8,128)(2,1)S(1)}, bf16[64,768]{1,0:T(8,128)(2,1)}, u32[]{:S(2)}) copy-start(bf16[64,768]{1,0:T(8,128)(2,1)} %param.23) | copy-start | bytes 294916
  7.3 215.0 %all-gather.9.cloned.1.call-start = ((), (), s32[]{:S(2)}) async-start(), calls=%async_computation.15 | async-start | bytes 1966080 | tf_op jit(solution)/shard_map/all_gather | solution.py:470
  7.3 102.5 %copy-start.12 = (bf16[64,1024]{1,0:T(8,128)(2,1)S(1)}, bf16[64,1024]{1,0:T(8,128)(2,1)}, u32[]{:S(2)}) copy-start(bf16[64,1024]{1,0:T(8,128)(2,1)} %param.26) | copy-start | bytes 393220
  25.8 100.9 %copy-start.13 = (bf16[256,256]{1,0:T(8,128)(2,1)S(1)}, bf16[256,256]{1,0:T(8,128)(2,1)}, u32[]{:S(2)}) copy-start(bf16[256,256]{1,0:T(8,128)(2,1)} %param.27) | copy-start | bytes 393220
  25.8 199.1 %all-gather.11.cloned.1.call-start = ((), (), s32[]{:S(2)}) async-start(), calls=%async_computation.16 | async-start | bytes 2621440 | tf_op jit(solution)/shard_map/all_gather | solution.py:470
  42.4 182.4 %all-gather.13.cloned.1.call-start = ((), (), s32[]{:S(2)}) async-start(), calls=%async_computation.17 | async-start | bytes 2621440 | tf_op jit(solution)/shard_map/all_gather | solution.py:470
  57.8 167.1 %all-gather.7.cloned.1.call-start = ((), (), s32[]{:S(2)}) async-start(), calls=%async_computation.14 | async-start | bytes 2359296 | tf_op jit(solution)/shard_map/all_gather | solution.py:470
  126.6 47.1 %copy-start.15 = (bf16[64,512]{1,0:T(8,128)(2,1)S(1)}, bf16[64,512]{1,0:T(8,128)(2,1)}, u32[]{:S(2)}) copy-start(bf16[64,512]{1,0:T(8,128)(2,1)} %param.29) | copy-start | bytes 196612
  142.2 46.0 %copy-start.10 = (bf16[256,512]{1,0:T(8,128)(2,1)S(1)}, bf16[256,512]{1,0:T(8,128)(2,1)}, u32[]{:S(2)}) copy-start(bf16[256,512]{1,0:T(8,128)(2,1)} %param.20) | copy-start | bytes 786436
  173.8 16.8 %copy-start.23 = (bf16[128]{0:T(256)(128)(2,1)S(1)}, bf16[128]{0:T(256)(128)(2,1)}, u32[]{:S(2)}) copy-start(bf16[128]{0:T(256)(128)(2,1)} %param.33) | copy-start | bytes 772
  173.8 25.5 %copy-start.17 = (bf16[128,128]{1,0:T(8,128)(2,1)S(1)}, bf16[128,128]{1,0:T(8,128)(2,1)}, u32[]{:S(2)}) copy-start(bf16[128,128]{1,0:T(8,128)(2,1)} %param.32) | copy-start | bytes 98308
  189.4 35.4 %copy-start = (f32[256,512]{1,0:T(8,128)}, f32[256,512]{1,0:T(8,128)S(1)}, u32[]{:S(2)}) copy-start(f32[256,512]{1,0:T(8,128)S(1)} %get-tuple-element.138.start) | copy-start | bytes 1572868
  190.5 116.4 %reduce-scatter.21.cloned.1.call-start = ((), (), s32[]{:S(2)}) async-start(), calls=%async_computation.18 | async-start | bytes 2359296 | tf_op jit(solution)/shard_map/reduce_scatter | solution.py:474
  242.5 1.4 copy-start.5
  242.5 1.4 copy-start.6
  242.5 1.4 copy-start.7
  242.5 118.6 %reduce-scatter.23.cloned.1.call-start = ((), (), s32[]{:S(2)}) async-start(), calls=%async_computation.19 | async-start | bytes 655360 | tf_op jit(solution)/shard_map/reduce_scatter | solution.py:474
  243.1 129.8 %reduce-scatter.27.cloned.1.call-start = ((), (), s32[]{:S(2)}) async-start(), calls=%async_computation.21 | async-start | bytes 2621440 | tf_op jit(solution)/shard_map/reduce_scatter | solution.py:474
  243.9 163.3 %reduce-scatter.43.cloned.1.call-start = ((), (), s32[]{:S(2)}) async-start(), calls=%async_computation.29 | async-start | bytes 1966080
  250.2 56.8 %copy-start.1 = (f32[256,512]{1,0:T(8,128)S(1)}, f32[256,512]{1,0:T(8,128)}, u32[]{:S(2)}) copy-start(f32[256,512]{1,0:T(8,128)} %copy-done) | copy-start | bytes 1572868
  250.2 58.1 %copy-start.4 = (f32[256,512]{1,0:T(8,128)S(1)}, f32[256,512]{1,0:T(8,128)}, u32[]{:S(2)}) copy-start(f32[256,512]{1,0:T(8,128)} %get-tuple-element.54) | copy-start | bytes 1572868
  250.2 195.4 %reduce-scatter.25.cloned.1.call-start = ((), (), s32[]{:S(2)}) async-start(), calls=%async_computation.20 | async-start | bytes 2621440 | tf_op jit(solution)/shard_map/reduce_scatter | solution.py:474
  250.2 59.2 %copy-start.8 = (bf16[256,256]{1,0:T(8,128)(2,1)S(1)}, bf16[256,256]{1,0:T(8,128)(2,1)}, u32[]{:S(2)}) copy-start(bf16[256,256]{1,0:T(8,128)(2,1)} %get-tuple-element.45) | copy-start | bytes 393220
  250.9 217.0 %reduce-scatter.37.cloned.1.call-start = ((), (), s32[]{:S(2)}) async-start(), calls=%async_computation.26 | async-start | bytes 327680 | tf_op jit(solution)/shard_map/reduce_scatter | solution.py:474
  309.5 46.3 %copy-start.2 = (f32[256,512]{1,0:T(8,128)}, f32[256,512]{1,0:T(8,128)S(1)}, u32[]{:S(2)}) copy-start(f32[256,512]{1,0:T(8,128)S(1)} %fusion.5) | copy-start | bytes 1572868
  310.5 178.7 %reduce-scatter.29.cloned.1.call-start = ((), (), s32[]{:S(2)}) async-start(), calls=%async_computation.22 | async-start | bytes 491520 | tf_op jit(solution)/shard_map/reduce_scatter | solution.py:474
  355.8 4.4 copy-start.3
  357.9 153.4 %reduce-scatter.33.cloned.1.call-start = ((), (), s32[]{:S(2)}) async-start(), calls=%async_computation.24 | async-start | bytes 655360 | tf_op jit(solution)/shard_map/reduce_scatter | solution.py:474
  360.1 173.3 %reduce-scatter.35.cloned.1.call-start = ((), (), s32[]{:S(2)}) async-start(), calls=%async_computation.25 | async-start | bytes 655360 | tf_op jit(solution)/shard_map/reduce_scatter | solution.py:474
  361.0 192.6 %reduce-scatter.45.cloned.1.call-start = ((), (), s32[]{:S(2)}) async-start(), calls=%async_computation.30 | async-start | bytes 163840
  362.8 82.9 %copy-start.9 = (f32[256,256]{1,0:T(8,128)S(1)}, f32[256,256]{1,0:T(8,128)}, u32[]{:S(2)}) copy-start(f32[256,256]{1,0:T(8,128)} %get-tuple-element.60) | copy-start | bytes 786436
  362.8 212.8 %reduce-scatter.47.cloned.1.call-start = ((), (), s32[]{:S(2)}) async-start(), calls=%async_computation.31 | async-start | bytes 655360
  375.0 159.8 %copy-start.20 = (f32[8,256]{1,0:T(8,128)S(1)}, f32[8,256]{1,0:T(8,128)}, u32[]{:S(2)}) copy-start(f32[8,256]{1,0:T(8,128)} %get-tuple-element.57) | copy-start | bytes 24580
  375.0 160.4 %copy-start.19 = (f32[1,512]{1,0:T(1,128)S(1)}, f32[1,512]{1,0:T(1,128)}, u32[]{:S(2)}) copy-start(f32[1,512]{1,0:T(1,128)} %get-tuple-element.69) | copy-start | bytes 6148
  375.0 247.9 %copy-start.26 = (f32[1,256]{1,0:T(1,128)S(1)}, f32[1,256]{1,0:T(1,128)}, u32[]{:S(2)}) copy-start(f32[1,256]{1,0:T(1,128)} %get-tuple-element.64) | copy-start | bytes 3076
  375.0 247.9 %copy-start.25 = (f32[1,256]{1,0:T(1,128)S(1)}, f32[1,256]{1,0:T(1,128)}, u32[]{:S(2)}) copy-start(f32[1,256]{1,0:T(1,128)} %get-tuple-element.61) | copy-start | bytes 3076
  375.0 247.9 %copy-start.24 = (f32[1,256]{1,0:T(1,128)S(1)}, f32[1,256]{1,0:T(1,128)}, u32[]{:S(2)}) copy-start(f32[1,256]{1,0:T(1,128)} %get-tuple-element.58) | copy-start | bytes 3076
  375.0 221.7 %reduce-scatter.39.cloned.1.call-start = ((), (), s32[]{:S(2)}) async-start(), calls=%async_computation.27 | async-start | bytes 491520 | tf_op jit(solution)/shard_map/reduce_scatter | solution.py:474
  410.0 208.9 %reduce-scatter.41.cloned.1.call-start = ((), (), s32[]{:S(2)}) async-start(), calls=%async_computation.28 | async-start | bytes 655360 | tf_op jit(solution)/shard_map/reduce_scatter | solution.py:474
  445.6 193.4 %reduce-scatter.31.cloned.1.call-start = ((), (), s32[]{:S(2)}) async-start(), calls=%async_computation.23 | async-start | bytes 163840 | tf_op jit(solution)/shard_map/reduce_scatter | solution.py:474
  446.4 249.0 %all-reduce.16.cloned.1.call-start = ((), (), s32[]{:S(2)}) async-start(), calls=%async_computation.32 | async-start | bytes 851968 | tf_op jit(solution)/shard_map/psum | solution.py:510
  533.5 183.7 %all-reduce.18.cloned.1.call-start = ((), (), s32[]{:S(2)}) async-start(), calls=%async_computation.33 | async-start | bytes 720896 | tf_op jit(solution)/shard_map/psum | solution.py:515
Sparse Core Ops, SparseCore 0:
  25.9 30.6 all-gather.8
  58.4 35.1 all-gather.10
  95.4 35.3 all-gather.12
  190.7 26.7 all-gather.6
  242.7 64.2 reduce-scatter.20
  309.9 24.7 reduce-scatter.22
  337.7 35.1 reduce-scatter.26
  376.2 30.9 reduce-scatter.42
  410.4 35.1 reduce-scatter.24
  448.3 19.6 reduce-scatter.36
  470.3 18.8 reduce-scatter.28
  491.3 19.8 reduce-scatter.32
  513.5 19.8 reduce-scatter.34
  536.1 17.4 reduce-scatter.44
  555.8 19.7 reduce-scatter.46
  577.8 18.8 reduce-scatter.38
  598.9 19.9 reduce-scatter.40
  621.5 17.4 reduce-scatter.30
  642.9 52.3 all-reduce.15
  698.5 18.6 all-reduce.17

commit v2 on v1

--- a/solution.py
+++ b/solution.py
@@ -149,33 +149,12 @@
     return packed, probs, mixed, aa, upper, dgelu.astype(BF16), am, pooled.astype(BF16)
 
 
-def char_fwd_kernel(x, cnt, g1, wqkv, wout, g2, wup, wdown, pq, *outs):
-    weights = (g1[...].astype(F32), wqkv[...], wout[...], g2[...].astype(F32), wup[...], wdown[...], pq[...].astype(F32))
-    for ref, val in zip(outs, char_fwd_tile(x[...], cnt[0], weights)):
-        ref[...] = val
-
-
 def full_spec(shape):
     return pl.BlockSpec(shape, lambda i: (0,) * len(shape))
 
 
 def rows_spec(rows, width):
     return pl.BlockSpec((rows, width), lambda i: (i, 0))
-
-
-def char_forward(x, cnt, weights):
-    total = x.shape[0]
-    tiles = total // ROWS
-    widths = [(ROWS, 768, BF16), (ROWS // 8, 512, F32), (ROWS, 256, BF16), (ROWS, 256, F32), (ROWS, 1024, BF16), (ROWS, 1024, BF16), (ROWS, 256, F32), (ROWS // 16, 256, BF16)]
-    return pl.pallas_call(
-        char_fwd_kernel,
-        grid=(tiles,),
-        in_specs=[rows_spec(ROWS, 256), pl.BlockSpec((1, ROWS // GROUP, GROUP), lambda i: (i, 0, 0))] + [full_spec(w.shape) for w in weights],
-        out_specs=[rows_spec(r, w) for r, w, _ in widths],
-        out_shape=[jax.ShapeDtypeStruct((r * tiles, w), d) for r, w, d in widths],
-        compiler_params=pltpu.CompilerParams(vmem_limit_bytes=VMEM_LIMIT, dimension_semantics=("arbitrary",)),
-        name="char_forward",
-    )(x, cnt, *weights)
 
 
 def char_bwd_tile(x, cnt, packed, probs, mixed, aa, upper, dgelu, am, gpool_ref, base, weights):
@@ -236,8 +215,8 @@
     return cg, (d_g1, d_qkv, d_out, d_g2, d_up, d_down_t, d_pq)
 
 
-def char_bwd_kernel(x, cnt, packed, probs, mixed, aa, upper, dgelu, am, gpool, g1, wqkv, wout, g2, wup, wdown, pq, cg, *accs):
-    weights = (g1[...].astype(F32), wqkv[...], wout[...], g2[...].astype(F32), wup[...], wdown[...], pq[...].astype(F32))
+def char_bwd_kernel(x, cnt, packed, probs, mixed, aa, upper, dgelu, am, gpool, vec, qo, up, dn, cg, *accs):
+    weights = char_weights(vec, qo, up, dn)
     step = pl.program_id(0)
 
     @pl.when(step == 0)
@@ -273,22 +252,300 @@
     )(x, cnt, *saved, gpool, *weights)
 
 
+MESH = pl.DeviceIdType.MESH
+
+
+def remote(src, dst, sems, index, where):
+    return pltpu.make_async_remote_copy(
+        src_ref=src, dst_ref=dst,
+        send_sem=sems[0] if index is None else sems[0].at[index],
+        recv_sem=sems[1] if index is None else sems[1].at[index],
+        device_id=where, device_id_type=MESH,
+    )
+
+
+def span(start, size):
+    return pl.ds(pl.multiple_of(start, size), size)
+
+
+class Place:
+    def __init__(self):
+        self.f, self.c, self.t = lax.axis_index("fsdp"), lax.axis_index("ctx"), lax.axis_index("tp")
+        self.F, self.T = lax.axis_size("fsdp"), lax.axis_size("tp")
+
+    def fs(self, k):
+        return lax.rem(self.f + k + self.F, self.F)
+
+    def tp(self, k):
+        return lax.rem(self.t + k + self.T, self.T)
+
+    def peers(self):
+        out = [{"fsdp": self.fs(k)} for k in range(1, self.F)]
+        out += [{"tp": self.tp(k)} for k in range(1, self.T)]
+        return out + [{"ctx": 1 - self.c}]
+
+
+def greet(peers):
+    barrier = pltpu.get_barrier_semaphore()
+    for where in peers:
+        pl.semaphore_signal(barrier, inc=1, device_id=where, device_id_type=MESH)
+    pl.semaphore_wait(barrier, len(peers))
+
+
+class Piece:
+    def __init__(self, at, shard, whole, mine, landing, region, cores, planar, sems, local_sem, first):
+        self.at, self.shard, self.whole = at, shard, whole
+        self.mine, self.landing, self.region = mine, landing, region
+        self.cores, self.planar = cores, planar
+        self.sems, self.local_sem, self.first = sems, local_sem, first
+
+    @staticmethod
+    def slots(F, T):
+        return (F - 1) + (T - 1) + T
+
+    def local(self):
+        at = self.at
+        return pltpu.make_async_copy(self.shard.at[self.mine(at.c, at.t)], self.whole.at[self.landing(at.f, at.c, at.t)], self.local_sem)
+
+    def z(self, k, incoming=False):
+        at = self.at
+        f = at.fs(-k) if incoming else at.f
+        dst = self.whole.at[self.landing(f, at.c, at.t)]
+        src = dst if incoming else self.shard.at[self.mine(at.c, at.t)]
+        return remote(src, dst, self.sems, self.first + k - 1, {"fsdp": at.fs(k)})
+
+    def plane(self, k, incoming=False):
+        at = self.at
+        r = self.whole.at[self.region(at.c, at.tp(-k) if incoming else at.t)]
+        return remote(r, r, self.sems, self.first + at.F - 1 + k - 1, {"tp": at.tp(k)})
+
+    def side(self, k, incoming=False):
+        at = self.at
+        r = self.whole.at[self.region(1 - at.c if incoming else at.c, at.tp(-k))]
+        return remote(r, r, self.sems, self.first + at.F + at.T - 2 + k, {"ctx": 1 - at.c})
+
+    def begin(self):
+        self.local().start()
+        for k in range(1, self.at.F):
+            self.z(k).start()
+
+    def spread(self):
+        self.local().wait()
+        for k in range(1, self.at.F):
+            self.z(k, True).wait_recv()
+        if self.planar:
+            for k in range(1, self.at.T):
+                self.plane(k).start()
+            if self.cores:
+                self.side(0).start()
+
+    def pass_on(self):
+        if self.planar:
+            for k in range(1, self.at.T):
+                self.plane(k, True).wait_recv()
+                if self.cores:
+                    self.side(k).start()
+
+    def arrive(self):
+        if self.planar and self.cores:
+            for k in range(self.at.T):
+                self.side(k, True).wait_recv()
+
+    def drain(self):
+        for k in range(1, self.at.F):
+            self.z(k).wait_send()
+        if self.planar:
+            for k in range(1, self.at.T):
+                self.plane(k).wait_send()
+            if self.cores:
+                for k in range(self.at.T):
+                    self.side(k).wait_send()
+
+
+ALL = slice(None)
+
+
+def gather_pieces(at, shards, wholes, sems, local_sems):
+    F, T = at.F, at.T
+    qo, up, dn, pj, sm, w4, wu, wd = shards
+    rq, rd, rw = qo.shape[0], dn.shape[0], w4.shape[1]
+    cu = wu.shape[1]
+    lanes = lambda c, t: span(256 * t + 128 * c, 128)
+    table = [
+        (lambda c, t: (ALL, lanes(c, t)), lambda f, c, t: (span(f * rq, rq), lanes(c, t)), lambda c, t: (ALL, lanes(c, t)), True, True),
+        (lambda c, t: (ALL, lanes(c, t)), lambda f, c, t: (span(f * rq, rq), lanes(c, t)), lambda c, t: (ALL, lanes(c, t)), True, True),
+        (lambda c, t: (span(rd // T * t, rd // T), span(128 * c, 128)), lambda f, c, t: (f, span(rd // T * t, rd // T), span(128 * c, 128)), lambda c, t: (ALL, span(rd // T * t, rd // T), span(128 * c, 128)), True, True),
+        (lambda c, t: (ALL, span(128 * t, 128)), lambda f, c, t: (span(f * rq, rq), span(128 * t, 128)), lambda c, t: (ALL, span(128 * t, 128)), False, True),
+        (lambda c, t: (ALL, ALL), lambda f, c, t: (f,), lambda c, t: (ALL,), False, False),
+        (lambda c, t: (span(2 * c, 2),), lambda f, c, t: (span(2 * c, 2), span(f * rw, rw), span(128 * t, 128)), lambda c, t: (span(2 * c, 2), ALL, span(128 * t, 128)), True, True),
+        (lambda c, t: (ALL, span(cu // 2 * c, cu // 2)), lambda f, c, t: (span(f * rw, rw), span(cu * t + cu // 2 * c, cu // 2)), lambda c, t: (ALL, span(cu * t + cu // 2 * c, cu // 2)), True, True),
+        (lambda c, t: (span(cu // 2 * c, cu // 2), ALL), lambda f, c, t: (span(cu * t + cu // 2 * c, cu // 2), span(f * rw, rw)), lambda c, t: (span(cu * t + cu // 2 * c, cu // 2), ALL), True, True),
+    ]
+    slots = Piece.slots(F, T)
+    return [
+        Piece(at, shard, whole, mine, landing, region, cores, planar, sems, local_sems.at[i], i * slots)
+        for i, (shard, whole, (mine, landing, region, cores, planar)) in enumerate(zip(shards, wholes, table))
+    ]
+
+
+FWD_OUTS = [(ROWS, 768, BF16), (ROWS // 8, 512, F32), (ROWS, 256, BF16), (ROWS, 256, F32), (ROWS, 1024, BF16), (ROWS, 1024, BF16), (ROWS, 256, F32), (ROWS // 16, 256, BF16)]
+
+
+def char_weights(vec, qo, up, dn):
+    return (vec[0:1, :256], qo[:, :768], qo[:, 768:], vec[1:2, :256], up[...], dn[...], vec[2:3, :256])
+
+
+def char_fwd_kernel(x, cnt, vec, qo, up, dn, *outs):
+    for ref, val in zip(outs, char_fwd_tile(x[...], cnt[0], char_weights(vec, qo, up, dn))):
+        ref[...] = val
+
+
+def char_forward(x, cnt, *weights):
+    tiles = x.shape[0] // ROWS
+    return pl.pallas_call(
+        char_fwd_kernel,
+        grid=(tiles,),
+        in_specs=[rows_spec(ROWS, 256), pl.BlockSpec((1, ROWS // GROUP, GROUP), lambda i: (i, 0, 0))] + [full_spec(w.shape) for w in weights],
+        out_specs=[rows_spec(r, w) for r, w, _ in FWD_OUTS],
+        out_shape=[jax.ShapeDtypeStruct((r * tiles, w), d) for r, w, d in FWD_OUTS],
+        compiler_params=pltpu.CompilerParams(vmem_limit_bytes=VMEM_LIMIT, dimension_semantics=("arbitrary",)),
+        name="char_forward",
+    )(x, cnt, *weights)
+
+
+GATHERED = [((256, 1024), BF16), ((256, 1024), BF16), ((4, 256, 256), BF16), ((256, 512), BF16), ((4, 8, 128), F32), ((4, 512, 512), BF16), ((512, 2048), BF16), ((2048, 512), BF16)]
+
+
+def vectors(sm):
+    rows = []
+    for i, n in ((0, 64), (1, 64), (2, 64), (3, 128), (4, 128)):
+        v = jnp.concatenate([sm[f, i : i + 1, :n] for f in range(sm.shape[0])], axis=1)
+        rows.append(v if n == 128 else jnp.concatenate([v, jnp.zeros_like(v)], axis=1))
+    return jnp.concatenate(rows + [jnp.zeros((3, 512), F32)], axis=0)
+
+
+def gather_fwd_kernel(*refs):
+    n = len(GATHERED)
+    x, cnt = refs[:2]
+    shards = refs[2 : 2 + n]
+    outs = refs[2 + n : 2 + n + len(FWD_OUTS)]
+    full_out = refs[2 + n + len(FWD_OUTS) : 2 + 2 * n + len(FWD_OUTS)]
+    vec_out = refs[2 + 2 * n + len(FWD_OUTS)]
+    wholes = refs[3 + 2 * n + len(FWD_OUTS) : 3 + 3 * n + len(FWD_OUTS)]
+    vec, send, recv, local_sems = refs[3 + 3 * n + len(FWD_OUTS) :]
+    at = Place()
+    pieces = gather_pieces(at, shards, wholes, (send, recv), local_sems)
+    qo, up, dn, pj, sm, w4, wu, wd = pieces
+    step = pl.program_id(0)
+    last = pl.num_programs(0) - 1
+
+    @pl.when(step == 0)
+    def _():
+        greet(at.peers())
+        for p in pieces:
+            p.begin()
+        first = (qo, up, dn, sm)
+        for p in first:
+            p.spread()
+        for p in first:
+            p.pass_on()
+        for p in first:
+            p.arrive()
+        vec[...] = vectors(wholes[4])
+        vec_out[...] = vec[...]
+
+    @pl.when(step == 1)
+    def _():
+        for p in (pj, w4, wu, wd):
+            p.spread()
+
+    @pl.when(step == 4)
+    def _():
+        pj.pass_on()
+        w4.pass_on()
+
+    dn2 = wholes[2][...].reshape(1024, 256)
+    for ref, val in zip(outs, char_fwd_tile(x[...], cnt[0], char_weights(vec, wholes[0], wholes[1], dn2))):
+        ref[...] = val
+
+    @pl.when(step == last)
+    def _():
+        def out(i):
+            return pltpu.make_async_copy(wholes[i], full_out[i], local_sems.at[i])
+
+        for i in (0, 1, 2, 3):
+            out(i).start()
+        for p in (wu, wd):
+            p.pass_on()
+        for i, p in ((5, w4), (6, wu), (7, wd)):
+            p.arrive()
+            out(i).start()
+        for p in pieces:
+            p.drain()
+        for i in (0, 1, 2, 3, 5, 6, 7):
+            out(i).wait()
+
+
+def gather_forward(x, cnt, shards):
+    tiles = x.shape[0] // ROWS
+    any_ = pl.BlockSpec(memory_space=pl.ANY)
+    count = len(GATHERED) * Piece.slots(lax.axis_size("fsdp"), lax.axis_size("tp"))
+    return pl.pallas_call(
+        gather_fwd_kernel,
+        grid=(tiles,),
+        in_specs=[rows_spec(ROWS, 256), pl.BlockSpec((1, ROWS // GROUP, GROUP), lambda i: (i, 0, 0))] + [any_] * len(shards),
+        out_specs=[rows_spec(r, w) for r, w, _ in FWD_OUTS] + [any_] * len(GATHERED) + [full_spec((8, 512))],
+        out_shape=[jax.ShapeDtypeStruct((r * tiles, w), d) for r, w, d in FWD_OUTS] + [jax.ShapeDtypeStruct(sh, d) for sh, d in GATHERED] + [jax.ShapeDtypeStruct((8, 512), F32)],
+        scratch_shapes=[pltpu.VMEM(sh, d) for sh, d in GATHERED]
+        + [pltpu.VMEM((8, 512), F32), pltpu.SemaphoreType.DMA((count,)), pltpu.SemaphoreType.DMA((count,)), pltpu.SemaphoreType.DMA((len(GATHERED),))],
+        compiler_params=pltpu.CompilerParams(vmem_limit_bytes=VMEM_LIMIT, collective_id=0, has_side_effects=True, dimension_semantics=("arbitrary",)),
+        name="gather_forward",
+    )(x, cnt, *shards)
+
+
 def word_kernel(
-    axes, nblk,
-    xall, start, cot, wq, wk, wv, wout, g2, wup, wdown,
-    block_out, rms, gaa, dx, d_q, d_k, d_v, d_out, d_g2, d_up, d_down,
-    kk, vv, kt, vt, ss, ee, qm, dom, mx, ll, ot, dqt, wkt, wvt, dk_acc, dv_acc, dlt, dk_sum, dv_sum, dx_own,
+    pooled, proj, words_in, cot, vec, w4, wup, wdown,
+    block_out, rms, words_grad, gpool, d_proj, d_vec, d_w4, d_up, d_down,
+    xall, kk, vv, kt, vt, ss, ee, qm, dom, mx, ll, ot, dqt, wkt, wvt, wout, dk_acc, dv_acc, dlt, dk_sum, dv_sum,
+    dx, dx_in, dx_own, ag_send, ag_recv, rs_send, rs_recv,
 ):
-    own = axes()
-    blk = start.shape[0]
+    at = Place()
+    T = at.T
+    own = at.c * T + at.t
+    nblk, blk, width = xall.shape
+    half = HEADS // 2
     low = pair_masks(blk)
-
-    def rows(j):
-        return pl.ds(pl.multiple_of(j * blk, blk), blk)
-
+    first, second = range(half), range(half, HEADS)
+
+    start = words_in[...].astype(F32) + mm(pooled[...], proj[...])
+    shat, sr = ln_parts(start)
+    g1v = vec[3:4, :]
+    xall[own] = (shat * g1v).astype(BF16)
+    greet([{"ctx": i, "tp": at.tp(k)} for i in (at.c, 1 - at.c) for k in range(T) if k > 0] + [{"ctx": 1 - at.c}])
+
+    def row_copy(k, incoming=False):
+        r = xall.at[at.c * T + (at.tp(-k) if incoming else at.t)]
+        return remote(r, r, (ag_send, ag_recv), k - 1, {"tp": at.tp(k)})
+
+    def side_copy(k):
+        r = xall.at[at.tp(-k)]
+        return remote(r, r, (ag_send, ag_recv), T - 1 + k, {"ctx": 1 - at.c})
+
+    for k in range(1, T):
+
+        @pl.when((at.c == 0) | (at.t + k < T))
+        def _():
+            row_copy(k).start()
+
+    @pl.when(at.c == 0)
+    def _():
+        side_copy(0).start()
+
+    wq, wk, wv, wot = w4.at[0], w4.at[1], w4.at[2], w4.at[3]
     wkt[...] = jnp.transpose(wk[...])
     wvt[...] = jnp.transpose(wv[...])
-    xown = xall[rows(own), :]
+    wout[...] = jnp.transpose(wot[...])
+    xown = xall[own]
     q = mm(xown, wq[...]).astype(BF16) * BF16(0.125)
     for p in range(HEADS // 2):
         a, b = split_heads(q[:, 128 * p : 128 * p + 128], low)
@@ -300,9 +557,6 @@
     dqt[...] = jnp.zeros(dqt.shape, F32)
     dk_sum[...] = jnp.zeros(dk_sum.shape, F32)
     dv_sum[...] = jnp.zeros(dv_sum.shape, F32)
-    dx[...] = jnp.zeros(dx.shape, BF16)
-
-    half = HEADS // 2
 
     def scores_of(j, heads):
         for h in heads:
@@ -323,16 +577,40 @@
         for h in heads:
             mx[h] = jnp.broadcast_to(jnp.max(mx[h], axis=0, keepdims=True), (8, blk))
 
-    first, second = range(half), range(half, HEADS)
-
-    @pl.loop(0, own + 1)
-    def _(j):
-        xj = xall[rows(j), :]
-        kk[j] = mm(xj, wk[...]).astype(BF16)
-        vv[j] = mm(xj, wv[...]).astype(BF16)
-        kt[j] = mm_nt(wkt[...], xj).astype(BF16)
-        vt[j] = mm_nt(wvt[...], xj).astype(BF16)
-        scores_of(j, first)
+    @pl.when(at.c == 0)
+    def _():
+        for k in range(1, T):
+            row_copy(k, True).wait_recv()
+            side_copy(k).start()
+
+    @pl.loop(0, 2 * T)
+    def _(m):
+        k0 = m - 1
+        k1 = m - T
+        early = (m >= 1) & (m <= T)
+        late = (m > T) & (at.c == 1) & (at.t >= k1)
+
+        @pl.when(early & (at.c == 1))
+        def _():
+            r = xall.at[lax.rem(at.t - k0 + T, T)]
+            remote(r, r, (ag_send, ag_recv), T - 1 + k0, {"ctx": 1 - at.c}).wait_recv()
+
+        @pl.when(late)
+        def _():
+            r = xall.at[own - k1]
+            remote(r, r, (ag_send, ag_recv), k1 - 1, {"tp": at.t - k1}).wait_recv()
+
+        @pl.when((m == 0) | (early & ((at.c == 1) | ((m >= 2) & (at.t >= k0)))) | late)
+        def _():
+            is_early = early.astype(jnp.int32)
+            is_late = (m > T).astype(jnp.int32)
+            j = own + is_early * (lax.rem(at.t - k0 + T, T) - own) - is_late * k1
+            xj = xall[j]
+            kk[j] = mm(xj, wk[...]).astype(BF16)
+            vv[j] = mm(xj, wv[...]).astype(BF16)
+            kt[j] = mm_nt(wkt[...], xj).astype(BF16)
+            vt[j] = mm_nt(wvt[...], xj).astype(BF16)
+            scores_of(j, first)
 
     top_of(first)
 
@@ -352,10 +630,11 @@
         ll[h] = jnp.broadcast_to(linv, (8, blk))
         ot[64 * h : 64 * h + 64, :] = ot[64 * h : 64 * h + 64, :] * linv
     mixed_t = ot[...].astype(BF16)
-    attn = mm(jnp.transpose(mixed_t), wout[...])
-    awa = start[...] + attn
+    mixed = jnp.transpose(mixed_t)
+    attn = mm(mixed, wout[...])
+    awa = start + attn
     ahat, ar = ln_parts(awa)
-    g2v = g2[...].astype(F32)
+    g2v = vec[4:5, :]
     n2 = (ahat * g2v).astype(BF16)
     upper, dgelu = gelu_both(mm(n2, wup[...]))
     upper = upper.astype(BF16)
@@ -364,17 +643,22 @@
     block_out[...] = final.astype(BF16)
     lane = lax.broadcasted_iota(jnp.int32, (blk, 128), 1)
     cols = [jnp.sqrt(jnp.mean(v * v, axis=-1, keepdims=True)) for v in (attn, mlp, final)]
-    rms[...] = jnp.transpose(jnp.where(lane == 0, cols[0], jnp.where(lane == 1, cols[1], cols[2])))[0:8, :]
+    rms[...] = jnp.transpose(jnp.where(lane == 0, cols[0], jnp.where(lane == 1, cols[1], cols[2])))[0:3, :]
     cotv = cot[...]
-    d_down[...] = mm_tn(upper, cotv).astype(BF16)
+    ff = wup.shape[1]
+    cu = ff // T // 2
+    gdown = mm_tn(upper, cotv).astype(BF16)
     ghid = (dgelu * mm_nt(cotv, wdown[...])).astype(BF16)
-    d_up[...] = mm_tn(n2, ghid).astype(BF16)
+    gup = mm_tn(n2, ghid).astype(BF16)
+    for c in range(2):
+        for t in range(T):
+            d_down[c, cu * t : cu * t + cu, :] = gdown[cu * (2 * t + c) : cu * (2 * t + c) + cu, :]
+            d_up[c, :, cu * t : cu * t + cu] = gup[:, cu * (2 * t + c) : cu * (2 * t + c) + cu]
     gn2 = mm_nt(ghid, wup[...])
-    d_g2[...] = jnp.sum(gn2 * ahat, axis=0, keepdims=True)
+    d_g2 = jnp.sum(gn2 * ahat, axis=0, keepdims=True)
     ga = cotv.astype(F32) + ln_back(ahat, ar, g2v, gn2)
-    gaa[...] = ga
     gal = ga.astype(BF16)
-    d_out[...] = mm(mixed_t, gal).astype(BF16)
+    d_w4[3] = mm_tn(gal, mixed).astype(BF16)
     do_t = mm_nt(wout[...], gal).astype(BF16)
     do_s = []
     for h in range(HEADS):
@@ -389,7 +673,15 @@
         dom[2 * p] = a
         dom[2 * p + 1] = b
 
-    def back_of(j, _):
+    def grad_copy(j):
+        return remote(dx.at[j], dx_in.at[own], (rs_send.at[j], rs_recv.at[own]), None, {"ctx": j // T, "tp": lax.rem(j, T)})
+
+    @pl.loop(0, own + 1)
+    def _(j):
+        @pl.when(j > 0)
+        def _():
+            grad_copy(j - 1).start()
+
         for p in range(HEADS // 2):
             c = slice(128 * p, 128 * p + 128)
             vp = vv[j, :, c]
@@ -406,40 +698,63 @@
             dv_acc[:, c] = dv.astype(BF16)
         dk = dk_acc[...]
         dv = dv_acc[...]
-        xj = xall[rows(j), :]
         dxj = mm_nt(dk, wk[...]) + mm_nt(dv, wv[...])
-        dx[rows(j), :] = dxj.astype(BF16)
+        dx[j] = dxj.astype(BF16)
         dx_own[...] = dxj
-        xt = jnp.transpose(xj)
+        xt = jnp.transpose(xall[j])
         dk_sum[...] += mm(xt, dk)
         dv_sum[...] += mm(xt, dv)
-        return 0
-
-    lax.fori_loop(0, own + 1, back_of, 0)
+
     dq = jnp.transpose((dqt[...] * 0.125).astype(BF16))
-    d_q[...] = mm_tn(xown, dq).astype(BF16)
-    d_k[...] = dk_sum[...].astype(BF16)
-    d_v[...] = dv_sum[...].astype(BF16)
-    dx[rows(own), :] = (dx_own[...] + mm_nt(dq, wq[...])).astype(BF16)
-
-
-def word_section(xall, start, cot, wq, wk, wv, wout, g2, wup, wdown):
-    blk, width = start.shape
-    nblk = xall.shape[0] // blk
+    d_w4[0] = mm_tn(xown, dq).astype(BF16)
+    d_w4[1] = dk_sum[...].astype(BF16)
+    d_w4[2] = dv_sum[...].astype(BF16)
+    dx_own[...] += mm_nt(dq, wq[...])
+
+    @pl.loop(own + 1, nblk)
+    def _(b):
+        remote(dx.at[own], dx_in.at[b], (rs_send.at[b], rs_recv.at[b]), None, {"ctx": 1 - at.c}).wait_recv()
+        dx_own[...] += dx_in[b].astype(F32)
+
+    gnf = dx_own[...]
+    grad = ga + ln_back(shat, sr, g1v, gnf)
+    words_grad[...] = grad
+    d_vec[...] = jnp.concatenate([jnp.sum(gnf * shat, axis=0, keepdims=True), d_g2, jnp.zeros((6, width), F32)], axis=0)
+    gproj = grad.astype(BF16)
+    d_proj[...] = mm_tn(pooled[...], gproj).astype(BF16)
+    gpool[...] = mm_nt(gproj, proj[...])
+
+    for k in range(1, T):
+
+        @pl.when((at.c == 0) | (at.t + k < T))
+        def _():
+            row_copy(k).wait_send()
+
+    @pl.when(at.c == 0)
+    def _():
+        for k in range(T):
+            side_copy(k).wait_send()
+
+    @pl.loop(0, own)
+    def _(j):
+        grad_copy(j).wait_send()
+
+
+def word_section(pooled, proj, words_in, cot, vec, w4, wup, wdown):
+    blk, width = words_in.shape
+    T = lax.axis_size("tp")
+    nblk = 2 * T
     ff = wup.shape[1]
-
-    def axes():
-        return lax.axis_index("ctx") * lax.axis_size("tp") + lax.axis_index("tp")
-
-    out_shapes = [((blk, width), BF16), ((8, blk), F32), ((blk, width), F32), ((nblk * blk, width), BF16)]
-    out_shapes += [((width, width), BF16)] * 4 + [((1, width), F32), ((width, ff), BF16), ((ff, width), BF16)]
+    out_shapes = [((blk, width), BF16), ((3, blk), F32), ((blk, width), F32), ((blk, pooled.shape[1]), F32), (proj.shape, BF16), ((8, width), F32)]
+    out_shapes += [(w4.shape, BF16), ((2, width, ff // 2), BF16), ((2, ff // 2, width), BF16)]
     vm = pl.BlockSpec(memory_space=pltpu.VMEM)
     return pl.pallas_call(
-        functools.partial(word_kernel, axes, nblk),
-        in_specs=[vm] * 10,
+        word_kernel,
+        in_specs=[vm] * 8,
         out_specs=[vm] * len(out_shapes),
         out_shape=[jax.ShapeDtypeStruct(s, d) for s, d in out_shapes],
         scratch_shapes=[
+            pltpu.VMEM((nblk, blk, width), BF16),
             pltpu.VMEM((nblk, blk, width), BF16),
             pltpu.VMEM((nblk, blk, width), BF16),
             pltpu.VMEM((nblk, width, blk), BF16),
@@ -454,16 +769,23 @@
             pltpu.VMEM((width, blk), F32),
             pltpu.VMEM((width, width), BF16),
             pltpu.VMEM((width, width), BF16),
+            pltpu.VMEM((width, width), BF16),
             pltpu.VMEM((blk, width), BF16),
             pltpu.VMEM((blk, width), BF16),
             pltpu.VMEM((HEADS, 8, blk), F32),
             pltpu.VMEM((width, width), F32),
             pltpu.VMEM((width, width), F32),
+            pltpu.VMEM((nblk, blk, width), BF16),
+            pltpu.VMEM((nblk, blk, width), BF16),
             pltpu.VMEM((blk, width), F32),
+            pltpu.SemaphoreType.DMA((2 * T,)),
+            pltpu.SemaphoreType.DMA((2 * T,)),
+            pltpu.SemaphoreType.DMA((nblk,)),
+            pltpu.SemaphoreType.DMA((nblk,)),
         ],
-        compiler_params=pltpu.CompilerParams(vmem_limit_bytes=VMEM_LIMIT),
+        compiler_params=pltpu.CompilerParams(vmem_limit_bytes=VMEM_LIMIT, collective_id=1, has_side_effects=True),
         name="word_section",
-    )(xall, start, cot, wq, wk, wv, wout, g2, wup, wdown)
+    )(pooled, proj, words_in, cot, vec, w4, wup, wdown)
 
 
 def gather(x, name, axis):
@@ -472,6 +794,10 @@
 
 def scatter(x, name, axis):
     return lax.psum_scatter(x, name, scatter_dimension=axis, tiled=True)
+
+
+def fits(rows):
+    return lax.axis_size("fsdp") == 4 and lax.axis_size("tp") == 4 and rows == 64
 
 
 def local(characters, counts, words_in, cotangent, char_prenorm, char_qkv, char_out, char_midnorm, char_up, char_down,
@@ -479,32 +805,30 @@
     words, slots, cdim = characters.shape
     x = characters.reshape(words * slots, cdim)
     cnt = jnp.repeat(counts.astype(F32), slots).reshape(words * slots // ROWS, ROWS // GROUP, GROUP)
-    names = (char_prenorm, char_qkv, char_out, char_midnorm, char_up, char_down, pool_query)
-    weights = [gather(w, "fsdp", 0) for w in names]
-    weights = [w.reshape(1, -1) if w.ndim == 1 else w for w in weights]
-    proj = gather(char_proj, "fsdp", 0)
-    g_word1 = gather(word_prenorm, "fsdp", 0).astype(F32)
-    g_word2 = gather(word_midnorm, "fsdp", 0).reshape(1, -1)
-    wqkv = gather(gather(jnp.moveaxis(word_qkv, 1, 0), "fsdp", 1), "tp", 2)
-    wout = gather(gather(word_out, "fsdp", 1), "tp", 0)
-    wup = gather(gather(word_up, "fsdp", 0), "tp", 1)
-    wdown = gather(gather(word_down, "fsdp", 1), "tp", 0)
-
-    *saved, pooled_low = char_forward(x, cnt, weights)
-    start = words_in.astype(F32) + mm(pooled_low, proj)
-    shat, sr = ln_parts(start)
-    normed_first = (shat * g_word1).astype(BF16)
-    xall = gather(normed_first, ("ctx", "tp"), 0)
-    (block_out, rms, gaa, dx, d_q, d_k, d_v, d_wout, d_g2w, d_wup, d_wdown) = word_section(
-        xall, start, cotangent, wqkv[0], wqkv[1], wqkv[2], wout, g_word2, wup, wdown
-    )
-    gnf = scatter(dx.astype(BF16), ("ctx", "tp"), 0).astype(F32)
-    words_grad = gaa + ln_back(shat, sr, g_word1, gnf)
-    d_g1w = jnp.sum(gnf * shat, axis=0)
-    gproj = words_grad.astype(BF16)
-    d_proj = mm_tn(pooled_low, gproj)
-    gpool = mm_nt(gproj, proj)
-    cg, d_g1, d_qkv, d_out, d_g2, d_up, d_down_t, d_pq = char_backward(x, cnt, saved, gpool, weights)
+    vectors_in = (char_prenorm, char_midnorm, pool_query, word_prenorm, word_midnorm)
+    qo = jnp.concatenate([char_qkv, char_out], axis=1)
+    w4 = jnp.concatenate([jnp.moveaxis(word_qkv, 1, 0), word_out.T[None]], axis=0)
+    direct = fits(char_prenorm.shape[0])
+    if direct:
+        pad = lambda v: jnp.pad(v.astype(F32), (0, 128 - v.shape[0]))
+        small = jnp.stack([pad(v) for v in vectors_in] + [jnp.zeros((128,), F32)] * 3)
+        *saved, pooled_low, qo, up, dn, proj, _, w4, wup, wdown, vec = gather_forward(x, cnt, [qo, char_up, char_down, char_proj, small, w4, word_up, word_down])
+        dn = dn.reshape(1024, 256)
+    else:
+        wide = [gather(v.astype(F32), "fsdp", 0) for v in vectors_in]
+        vec = jnp.stack([jnp.pad(v, (0, 512 - v.shape[0])) for v in wide] + [jnp.zeros((512,), F32)] * 3)
+        qo, up, dn, proj = (gather(w, "fsdp", 0) for w in (qo, char_up, char_down, char_proj))
+        w4 = gather(gather(w4, "fsdp", 1), "tp", 2)
+        wup = gather(gather(word_up, "fsdp", 0), "tp", 1)
+        wdown = gather(gather(word_down, "fsdp", 1), "tp", 0)
+        *saved, pooled_low = char_forward(x, cnt, vec, qo, up, dn)
+    (block_out, rms, words_grad, gpool, d_proj, d_vec, d_w4, d_wup, d_wdown) = word_section(pooled_low, proj, words_in, cotangent, vec, w4, wup, wdown)
+    cg, d_g1, d_qkv, d_out, d_g2, d_up, d_down_t, d_pq = char_backward(x, cnt, saved, gpool, [vec, qo, up, dn])
+    ff = word_up.shape[1] // 2
+    d_q, d_k, d_v, d_wout = d_w4[0], d_w4[1], d_w4[2], d_w4[3].T
+    d_wup = jnp.moveaxis(d_wup.reshape(2, 512, 4, ff), 0, 2).reshape(512, 2048)
+    d_wdown = jnp.moveaxis(d_wdown.reshape(2, 4, ff, 512), 0, 1).reshape(2048, 512)
+    d_g1w, d_g2w = d_vec[0], d_vec[1:2]
 
     def reduce_char(g):
         g = lax.psum(g.astype(BF16), ("ctx", "tp"))
@@ -520,7 +844,7 @@
         block_out,
         cg.reshape(words, slots, cdim),
         words_grad,
-        rms[:3],
+        rms,
         reduce_char(d_g1[0]),
         reduce_char(d_qkv),
         reduce_char(d_out),

time: 730 us -> 570 us (0.78)
  blocking collectives: 217 us -> 41.1 us
  Pallas kernels: 93.3 us -> 162 us
  waiting for transfers between devices: 351 us -> 283 us
  local copies, waits for them, and re-layouts: 23.2 us -> 41.3 us
    all_gather x12 -> x0, blocking collectives: 166 us -> none  [gather(): return lax.all_gather(x, name, axis=axis, tiled=True)]
    pallas_call x2, Pallas kernels: 49.2 us -> 118 us  [the longest x1 69 us: gather_forward(): pl.pallas_call(gather_fwd_kernel, grid=(tiles,), in_specs=[rows_spec(ROWS...]
    reduce_scatter x11 -> x10, waiting for transfers between devices: 237 us -> 190 us  [scatter(): return lax.psum_scatter(x, name, scatter_dimension=axis, tiled=True)]
    unnamed x23 -> x18, waiting for transfers between devices: 73.5 us -> 53.2 us
    unnamed x2 -> x1, blocking collectives: 18.5 us -> 8.69 us
    transpose x0 -> x3, local copies, waits for them, and re-layouts: none -> 8.66 us  [the longest x1 4.56 us: local(): d_wup = jnp.moveaxis(d_wup.reshape(2, 512, 4, ff), 0, 2).reshape(512, 2048)]
    unnamed x81 -> x42, local copies, waits for them, and re-layouts: 17.4 us -> 22 us
  transfers between devices with their start and end apart: 20 -> 15, of which waited for: 15 -> 14; matrix products, arithmetic and copies ran while one was open for 6% -> 8% of each run, Pallas kernels for 10% -> 8%
where the time goes in v2:
time: 570 us; the launch traced here: 569 us
  waiting for transfers between devices  283 us (50%)
  Pallas kernels  162 us (28%)
  local copies, waits for them, and re-layouts  41.3 us (7%)
  blocking collectives  41.1 us (7%)
  other arithmetic  24.3 us (4%)
  between operations  15.5 us (3%)
    reduce_scatter x10, waiting for transfers between devices, scatter(): return lax.psum_scatter(x, name, scatter_dimension=axis, tiled=True)  190 us
    pallas_call x1, Pallas kernels, gather_forward(): pl.pallas_call(gather_fwd_kernel, grid=(tiles,), in_specs=[rows_spec(ROWS...  69 us
    unnamed x18, waiting for transfers between devices  53.2 us
    pallas_call x1, Pallas kernels, word_section(): pl.pallas_call(word_kernel, in_specs=[vm] * 8, out_specs=[vm] * len(out_s...  49.1 us
    pallas_call x1, Pallas kernels, char_backward(): pl.pallas_call(char_bwd_kernel, grid=(tiles,), in_specs=[rows_spec(ROWS,...  44.3 us
    psum x1, blocking collectives, reduce_char(): g = lax.psum(g.astype(BF16), ('ctx', 'tp'))  28.4 us
    psum x1, waiting for transfers between devices, reduce_char(): g = lax.psum(g.astype(BF16), ('ctx', 'tp'))  24.8 us
    unnamed x42, local copies, waits for them, and re-layouts  22 us
  transfers between devices with their start and end apart: 15, of which 14 were waited for; matrix products, arithmetic and copies ran while one was open for 8% of the time, Pallas kernels for 8%

profile of v2, /device:TPU:0, one launch (start us, length us, event | category | flops | bytes accessed | tf_op | source)
XLA Modules:
  0.0 568.6 jit_solution(8912284059712108227)
XLA Ops:
  7.2 0.7 bitcast_convert_fusion.4
  7.9 0.7 convert_element_type.93
  8.8 0.7 broadcast_in_dim.12.refs_1_.cnt
  9.5 0.9 copy.41
  10.4 0.7 bitcast_convert_fusion
  11.0 0.7 bitcast_convert_fusion.2
  11.7 1.6 pad_maximum_fusion.1.refs_7_
  13.3 1.6 pad_maximum_fusion.refs_2_
  14.9 0.6 stack.49.refs_6_
  15.5 69.0 %gather_forward.1 = (bf16[4096,768]{1,0:T(8,128)(2,1)}, f32[512,512]{1,0:T(8,128)}, bf16[4096,256]{1,0:T(8,128)(2,1)}, f32[4096,256]{1,0:T(8,128)}, bf16[4096,10...) custom-call(bf16[4096,256]{1,0:T(8,128)(2,1)} %bitcast.45, ...), custom_call_target="tpu_custom_call" | custom-call | tf_op jit(solution)/shard_map/gather_forward/pallas_call | solution.py:493
  84.5 49.1 %word_section.1 = (bf16[256,512]{1,0:T(8,128)(2,1)}, f32[3,256]{1,0:T(4,128)}, f32[256,512]{1,0:T(8,128)}, f32[256,256]{1,0:T(8,128)}, bf16[256,512]{1,0:T(8,128...) custom-call(bf16[256,256]{1,0:T(8,128)(2,1)} %get-tuple-element.51.p, ...), custom_call_target="tpu_custom_call" | custom-call | tf_op jit(solution)/shard_map/word_section/pallas_call | solution.py:751
  133.6 3.0 copy.43
  136.7 1.5 copy-done
  138.2 1.2 slice.18
  139.5 3.2 copy.46
  142.7 1.7 copy.52
  144.4 3.3 reshape.67
  147.8 4.6 copy.42
  152.3 4.5 reshape.68
  156.9 0.5 reduce-scatter.32.cloned.1.call-update
  157.7 44.3 %char_backward.1 = (f32[4096,256]{1,0:T(8,128)}, f32[1,256]{1,0:T(1,128)}, f32[256,768]{1,0:T(8,128)}, f32[256,256]{1,0:T(8,128)}, f32[1,256]{1,0:T(1,128)}, /*i...) custom-call(bf16[4096,256]{1,0:T(8,128)(2,1)} %bitcast.46, f32[8,4,128]{2,1,0:T(4,128)} %broadcast_in_dim.12.refs_1_.cnt, ...), custom_call_target="tpu_custom_call" | custom-call | tf_op jit(solution)/shard_map/char_backward/pallas_call | solution.py:241
  202.0 2.0 convert_element_type.97
  204.1 2.1 convert_element_type.104
  206.3 0.9 convert_bitcast_fusion
  207.2 1.1 slice_bitcast_fusion
  208.3 1.0 copy.48
  209.4 2.2 copy.50
  211.7 5.7 reduce-scatter.40.cloned.1.call-done
  217.4 1.7 reshape.77
  219.0 1.1 copy.47
  220.2 35.6 %reduce-scatter.20.cloned.1.call-done = bf16[512,512]{1,0:T(8,128)(2,1)} async-done(((bf16[512,2048]{1,0:T(8,128)(2,1)}), bf16[512,512]{1,0:T(8,128)(2,1)}) %reduce-scatter.20.cloned.1.call-update) | async-done | bytes 524304 | tf_op jit(solution)/shard_map/reduce_scatter | solution.py:796
  255.9 0.7 convert_element_type.99
  256.6 20.9 %reduce-scatter.32.cloned.1.call-done = bf16[64,512]{1,0:T(8,128)(2,1)} async-done(((bf16[256,512]{1,0:T(8,128)(2,1)}), bf16[64,512]{1,0:T(8,128)(2,1)}) %reduce-scatter.32.cloned.1.call-update) | async-done | bytes 65552 | tf_op jit(solution)/shard_map/reduce_scatter | solution.py:796
  277.6 21.1 %reduce-scatter.24.cloned.1.call-done = bf16[64,768]{1,0:T(8,128)(2,1)} async-done(((bf16[256,768]{1,0:T(8,128)(2,1)}), bf16[64,768]{1,0:T(8,128)(2,1)}) %reduce-scatter.24.cloned.1.call-update) | async-done | bytes 98320 | tf_op jit(solution)/shard_map/reduce_scatter | solution.py:796
  298.7 22.1 %reduce-scatter.28.cloned.1.call-done = bf16[64,1024]{1,0:T(8,128)(2,1)} async-done(((bf16[256,1024]{1,0:T(8,128)(2,1)}), bf16[64,1024]{1,0:T(8,128)(2,1)}) %reduce-scatter.28.cloned.1.call-update) | async-done | bytes 131088 | tf_op jit(solution)/shard_map/reduce_scatter | solution.py:796
  320.8 22.8 %reduce-scatter.30.cloned.1.call-done = bf16[256,256]{0,1:T(8,128)(2,1)} async-done(((bf16[1024,256]{0,1:T(8,128)(2,1)}), bf16[256,256]{0,1:T(8,128)(2,1)}) %reduce-scatter.30.cloned.1.call-update) | async-done | bytes 131088 | tf_op jit(solution)/shard_map/reduce_scatter | solution.py:796
  343.7 25.8 %reduce-scatter.42.cloned.1.call-done = bf16[128,512]{1,0:T(8,128)(2,1)} async-done(((bf16[512,512]{1,0:T(8,128)(2,1)}), bf16[128,512]{1,0:T(8,128)(2,1)}) %reduce-scatter.42.cloned.1.call-update) | async-done | bytes 131088
  369.5 1.7 copy.49
  371.3 0.6 dynamic-slice
  372.5 20.9 %reduce-scatter.44.cloned.1.call-done = bf16[128,512]{1,0:T(8,128)(2,1)} async-done(((bf16[512,512]{1,0:T(8,128)(2,1)}), bf16[128,512]{1,0:T(8,128)(2,1)}) %reduce-scatter.44.cloned.1.call-update) | async-done | bytes 131088
  393.5 1.7 copy.51
  395.2 19.4 %reduce-scatter.34.cloned.1.call-done = bf16[3,128,128]{2,1,0:T(8,128)(2,1)} async-done(((bf16[3,512,128]{2,1,0:T(8,128)(2,1)}), bf16[3,128,128]{2,1,0:T(8,128)(2,1)}) %reduce-scatter.34.cloned.1.call-update) | async-done | bytes 98320 | tf_op jit(solution)/shard_map/reduce_scatter | solution.py:796
  414.6 22.3 %reduce-scatter.38.cloned.1.call-done = bf16[128,512]{1,0:T(8,128)(2,1)} async-done(((bf16[512,512]{1,0:T(8,128)(2,1)}), bf16[128,512]{1,0:T(8,128)(2,1)}) %reduce-scatter.38.cloned.1.call-update) | async-done | bytes 131088 | tf_op jit(solution)/shard_map/reduce_scatter | solution.py:796
  437.0 8.7 %all-reduce.10 = (bf16[256]{0:T(256)(128)(2,1)S(1)}, bf16[256]{0:T(256)(128)(2,1)S(1)}, bf16[256]{0:T(256)(128)(2,1)S(1)}, bf16[512]{0:T(512)(128)(2,1)S(1)}, bf16[512]{0:T(512)(128)(2,1)S(1)}) all-reduce(bf16[256]{0:T(256)(128)(2,1)S(1)} %convert_reduce_fusion.2, ...), channel_id=2, replica_groups=mesh['fsdp'=4,'ctx'=2,'tp'=4] {'fsdp'}, use_global_device_ids=true, to_apply=%region_1.2.clone | all-reduce | flops 1792 | bytes 7168
  446.7 10.3 %reduce-scatter.26.cloned.1.call-done = bf16[64,256]{1,0:T(8,128)(2,1)} async-done(((bf16[256,256]{1,0:T(8,128)(2,1)}), bf16[64,256]{1,0:T(8,128)(2,1)}) %reduce-scatter.26.cloned.1.call-update) | async-done | bytes 32784 | tf_op jit(solution)/shard_map/reduce_scatter | solution.py:796
  457.0 28.4 %all-reduce.8 = (bf16[64]{0:T(256)(128)(2,1)S(1)}, bf16[64,256]{1,0:T(8,128)(2,1)S(1)}, bf16[64]{0:T(256)(128)(2,1)S(1)}, bf16[64]{0:T(256)(128)(2,1)S(1)}, bf16...) all-reduce(bf16[64]{0:T(256)(128)(2,1)S(1)} %dynamic-slice.1, ...), channel_id=1, replica_groups=mesh['fsdp'=4,'ctx'=2,'tp'=4] {'ctx','tp'}, use_global_device_ids=true, to_apply=%region_0.1 | all-reduce | flops 16832 | bytes 67328 | tf_op jit(solution)/shard_map/psum | solution.py:834
  485.3 0.6 convert_element_type.100
  486.0 0.5 convert_element_type.103
  486.5 0.5 convert_element_type.111
  488.5 24.8 %all-reduce.15.cloned.1.call-done = (bf16[256,256]{0,1:T(8,128)(2,1)}, bf16[64,768]{1,0:T(8,128)(2,1)}, bf16[64,1024]{1,0:T(8,128)(2,1)}, bf16[64,512]{1,0:T(8,128)(2,1)}) async-done(((bf16[256,256]{0,1:T(8,128)(2,1)}, bf16[64,768]{1,0:T(8,128)(2,1)}, bf16[64,1024]{1,0:T(8,128)(2,1)}, bf16[64,512]{1,0:T(8,128)(2,1)}), (bf16[256,256]{0,1:T(8,128)(2,1)}, bf16[64,768]{1,0:T(8,128)(2,1)}, ...) | async-done | bytes 426000 | tf_op jit(solution)/shard_map/psum | solution.py:834
  513.3 1.6 convert_element_type.105
  515.0 1.7 copy.44
  516.7 1.6 convert_element_type.98
  518.3 1.5 convert_element_type.112
  519.8 15.6 %reduce-scatter.36.cloned.1.call-done = bf16[128,128]{0,1:T(8,128)(2,1)} async-done(((bf16[128,512]{0,1:T(8,128)(2,1)}), bf16[128,128]{0,1:T(8,128)(2,1)}) %reduce-scatter.36.cloned.1.call-update) | async-done | bytes 32784 | tf_op jit(solution)/shard_map/reduce_scatter | solution.py:796
  535.4 4.0 psum.122
  539.4 0.7 copy.45
  540.2 15.0 %all-reduce.17.cloned.1.call-done = (bf16[3,128,128]{2,1,0:T(8,128)(2,1)}, bf16[128,512]{1,0:T(8,128)(2,1)}, bf16[512,128]{1,0:T(8,128)(2,1)}) async-done(((bf16[3,128,128]{2,1,0:T(8,128)(2,1)}, bf16[128,512]{1,0:T(8,128)(2,1)}, bf16[512,128]{1,0:T(8,128)(2,1)}), (bf16[3,128,128]{2,1,0:T(8,128)(2,1)}, bf16[128,512]{1,0:T(8,128)(2,1)}, bf16[512,128]{1,0:T(8,128)(2,1)})) %all-reduce.17.cloned.1.call-update) | async-done | bytes 360464 | tf_op jit(solution)/shard_map/psum | solution.py:839
  555.1 1.6 convert_element_type.118
  556.8 1.6 convert_element_type.119
  558.4 1.6 convert_bitcast_fusion.1
  560.0 0.7 copy.63
  560.7 0.8 copy.64
  561.5 0.6 copy.65
  (68 shorter events, 3.3 us)
Async XLA Ops:
  7.2 202.2 %reduce-scatter.22.cloned.1.call-start = ((), (), s32[]{:S(2)}) async-start(), calls=%async_computation.14 | async-start | bytes 2621440 | tf_op jit(solution)/shard_map/reduce_scatter | solution.py:796
  136.6 1.6 copy-start
  136.6 80.7 %reduce-scatter.40.cloned.1.call-start = ((), (), s32[]{:S(2)}) async-start(), calls=%async_computation.23 | async-start | bytes 1966080
  144.4 111.4 %reduce-scatter.20.cloned.1.call-start = ((), (), s32[]{:S(2)}) async-start(), calls=%async_computation.13 | async-start | bytes 2621440 | tf_op jit(solution)/shard_map/reduce_scatter | solution.py:796
  156.9 120.7 %reduce-scatter.32.cloned.1.call-start = ((), (), s32[]{:S(2)}) async-start(), calls=%async_computation.19 | async-start | bytes 327680 | tf_op jit(solution)/shard_map/reduce_scatter | solution.py:796
  157.4 141.2 %reduce-scatter.24.cloned.1.call-start = ((), (), s32[]{:S(2)}) async-start(), calls=%async_computation.15 | async-start | bytes 491520 | tf_op jit(solution)/shard_map/reduce_scatter | solution.py:796
  202.0 4.3 copy-start.1
  204.0 116.8 %reduce-scatter.28.cloned.1.call-start = ((), (), s32[]{:S(2)}) async-start(), calls=%async_computation.17 | async-start | bytes 655360 | tf_op jit(solution)/shard_map/reduce_scatter | solution.py:796
  206.2 137.4 %reduce-scatter.30.cloned.1.call-start = ((), (), s32[]{:S(2)}) async-start(), calls=%async_computation.18 | async-start | bytes 655360 | tf_op jit(solution)/shard_map/reduce_scatter | solution.py:796
  207.2 162.3 %reduce-scatter.42.cloned.1.call-start = ((), (), s32[]{:S(2)}) async-start(), calls=%async_computation.24 | async-start | bytes 655360
  209.3 46.5 %copy-start.3 = (f32[256,256]{1,0:T(8,128)S(1)}, f32[256,256]{1,0:T(8,128)}, u32[]{:S(2)}) copy-start(f32[256,256]{1,0:T(8,128)} %get-tuple-element.74) | copy-start | bytes 786436
  209.3 184.1 %reduce-scatter.44.cloned.1.call-start = ((), (), s32[]{:S(2)}) async-start(), calls=%async_computation.25 | async-start | bytes 655360
  211.6 159.6 %copy-start.5 = (f32[8,512]{1,0:T(8,128)S(1)}, f32[8,512]{1,0:T(8,128)}, u32[]{:S(2)}) copy-start(f32[8,512]{1,0:T(8,128)} %get-tuple-element.80) | copy-start | bytes 49156
  211.6 159.7 %copy-start.10 = (u32[32]{0:T(128)S(1)}, u32[32]{0:T(128)}, u32[]{:S(2)}) copy-start(u32[32]{0:T(128)} %constant.15) | copy-start | bytes 388
  211.6 160.9 %copy-start.9 = (f32[1,256]{1,0:T(1,128)S(1)}, f32[1,256]{1,0:T(1,128)}, u32[]{:S(2)}) copy-start(f32[1,256]{1,0:T(1,128)} %get-tuple-element.78) | copy-start | bytes 3076
  211.6 202.9 %reduce-scatter.34.cloned.1.call-start = ((), (), s32[]{:S(2)}) async-start(), calls=%async_computation.20 | async-start | bytes 491520 | tf_op jit(solution)/shard_map/reduce_scatter | solution.py:796
  219.0 217.9 %copy-start.8 = (f32[1,256]{1,0:T(1,128)S(1)}, f32[1,256]{1,0:T(1,128)}, u32[]{:S(2)}) copy-start(f32[1,256]{1,0:T(1,128)} %get-tuple-element.75) | copy-start | bytes 3076
  219.0 217.9 %copy-start.7 = (f32[1,256]{1,0:T(1,128)S(1)}, f32[1,256]{1,0:T(1,128)}, u32[]{:S(2)}) copy-start(f32[1,256]{1,0:T(1,128)} %get-tuple-element.72) | copy-start | bytes 3076
  220.1 216.7 %reduce-scatter.38.cloned.1.call-start = ((), (), s32[]{:S(2)}) async-start(), calls=%async_computation.22 | async-start | bytes 655360 | tf_op jit(solution)/shard_map/reduce_scatter | solution.py:796
  255.8 201.2 %reduce-scatter.26.cloned.1.call-start = ((), (), s32[]{:S(2)}) async-start(), calls=%async_computation.16 | async-start | bytes 163840 | tf_op jit(solution)/shard_map/reduce_scatter | solution.py:796
  256.6 256.8 %all-reduce.15.cloned.1.call-start = ((), (), s32[]{:S(2)}) async-start(), calls=%async_computation.26 | async-start | bytes 851968 | tf_op jit(solution)/shard_map/psum | solution.py:834
  343.6 216.4 %copy-start.4 = (bf16[256,512]{1,0:T(8,128)(2,1)S(1)}, bf16[256,512]{1,0:T(8,128)(2,1)}, u32[]{:S(2)}) copy-start(bf16[256,512]{1,0:T(8,128)(2,1)} %get-tuple-element.162) | copy-start | bytes 786436
  343.6 191.8 %reduce-scatter.36.cloned.1.call-start = ((), (), s32[]{:S(2)}) async-start(), calls=%async_computation.21 | async-start | bytes 163840 | tf_op jit(solution)/shard_map/reduce_scatter | solution.py:796
  371.2 189.5 %copy-start.2 = (f32[256,512]{1,0:T(8,128)S(1)}, f32[256,512]{1,0:T(8,128)}, u32[]{:S(2)}) copy-start(f32[256,512]{1,0:T(8,128)} %get-tuple-element.164) | copy-start | bytes 1572868
  371.2 184.0 %all-reduce.17.cloned.1.call-start = ((), (), s32[]{:S(2)}) async-start(), calls=%async_computation.27 | async-start | bytes 720896 | tf_op jit(solution)/shard_map/psum | solution.py:839
  485.3 76.1 %copy-start.6 = (f32[3,256]{1,0:T(4,128)S(1)}, f32[3,256]{1,0:T(4,128)}, u32[]{:S(2)}) copy-start(f32[3,256]{1,0:T(4,128)} %get-tuple-element.165) | copy-start | bytes 9220
Sparse Core Ops, SparseCore 0:
  136.8 46.3 reduce-scatter.21
  186.4 30.9 reduce-scatter.39
  220.6 35.1 reduce-scatter.19
  257.9 19.6 reduce-scatter.31
  279.8 18.8 reduce-scatter.23
  300.8 19.9 reduce-scatter.27
  323.6 19.9 reduce-scatter.29
  346.4 23.0 reduce-scatter.41
  371.9 21.5 reduce-scatter.43
  395.7 18.8 reduce-scatter.33
  416.9 19.9 reduce-scatter.37
  439.5 17.3 reduce-scatter.25
  460.9 52.3 all-reduce.14
  516.1 19.2 reduce-scatter.35
  538.3 16.7 all-reduce.16

commit v3 on v2

--- a/solution.py
+++ b/solution.py
@@ -157,15 +157,12 @@
     return pl.BlockSpec((rows, width), lambda i: (i, 0))
 
 
-def char_bwd_tile(x, cnt, packed, probs, mixed, aa, upper, dgelu, am, gpool_ref, base, weights):
-    g1, wqkv, wout, g2, wup, wdown, pq = weights
-    rows = x.shape[0]
-    groups = rows // GROUP
+def char_mlp_back(cnt, aa, upper, dgelu, am, gpool_ref, base, weights):
+    _, _, _, g2, wup, wdown, pq = weights
+    rows = aa.shape[0]
     words = rows // 16
-    low = pair_masks(GROUP)
-    lw = word_of_lane(2 * GROUP)
-    cols = jnp.concatenate([count_column(cnt[g : g + 1, :]) for g in range(groups)], axis=0)
-    am3, w = pool_weights(am, pq, cols)
+    cols = jnp.concatenate([count_column(cnt[g : g + 1, :]) for g in range(rows // GROUP)], axis=0)
+    _, w = pool_weights(am, pq, cols)
     gp = jnp.concatenate(
         [jnp.broadcast_to(gpool_ref[pl.ds(base + i, 1), :], (16, 256)) for i in range(words)], axis=0
     )
@@ -182,6 +179,14 @@
     gmid = mm_nt(ghid, wup)
     gca = gm + ln_back(ahat, ar, g2, gmid)
     d_g2 = jnp.sum(gmid * ahat, axis=0, keepdims=True)
+    return gca, d_up, d_down_t, d_g2, d_pq
+
+
+def char_attn_back(x, packed, probs, mixed, gca, weights):
+    g1, wqkv, wout = weights[:3]
+    groups = x.shape[0] // GROUP
+    low = pair_masks(GROUP)
+    lw = word_of_lane(2 * GROUP)
     gcl = gca.astype(BF16)
     d_out = mm_tn(mixed, gcl)
     gcm = mm_nt(gcl, wout).astype(BF16)
@@ -205,48 +210,82 @@
             dq_g.append(jnp.where(low, o[:GROUP], o[GROUP:]) * 0.125)
         dqkv.append(jnp.concatenate(dq_g + dk_g + dv_g, axis=1))
     dqkv = jnp.concatenate(dqkv, axis=0).astype(BF16)
-    xf = x.astype(F32)
-    xhat, xr = ln_parts(xf)
+    xhat, xr = ln_parts(x.astype(F32))
     normed = (xhat * g1).astype(BF16)
     d_qkv = mm_tn(normed, dqkv)
     gn = mm_nt(dqkv, wqkv)
     d_g1 = jnp.sum(gn * xhat, axis=0, keepdims=True)
     cg = gca + ln_back(xhat, xr, g1, gn)
-    return cg, (d_g1, d_qkv, d_out, d_g2, d_up, d_down_t, d_pq)
-
-
-def char_bwd_kernel(x, cnt, packed, probs, mixed, aa, upper, dgelu, am, gpool, vec, qo, up, dn, cg, *accs):
+    return cg, d_qkv, d_out, d_g1
+
+
+def char_back_step(step, tiles, ins, cg, gca, accs):
+    x, cnt, packed, probs, mixed, aa, upper, dgelu, am, gpool, vec, qo, up, dn = ins
+    a_qo, a_up, a_dn, a_vec = accs
     weights = char_weights(vec, qo, up, dn)
-    step = pl.program_id(0)
 
     @pl.when(step == 0)
     def _():
         for acc in accs:
             acc[...] = jnp.zeros_like(acc)
 
-    out, sums = char_bwd_tile(
-        x[...], cnt[0], packed[...], probs[...], mixed[...], aa[...], upper[...], dgelu[...], am[...],
-        gpool, step * (ROWS // 16), weights,
-    )
-    cg[...] = out
-    for acc, val in zip(accs, sums):
-        acc[...] += val
-
-
-def char_backward(x, cnt, saved, gpool, weights):
+    @pl.when(step < tiles)
+    def _():
+        grad, d_up, d_dn, d_g2, d_pq = char_mlp_back(cnt[0], aa[...], upper[...], dgelu[...], am[...], gpool, step * (ROWS // 16), weights)
+        gca[span(step * ROWS, ROWS), :] = grad
+        a_vec[1:2, :256] += d_g2
+        a_vec[2:3, :256] += d_pq
+        for i in range(8):
+            t, c = i // 2, i % 2
+            a_up[c, :, 128 * t : 128 * t + 128] += d_up[:, 128 * i : 128 * i + 128]
+        for c in range(2):
+            a_dn[c] += d_dn[128 * c : 128 * c + 128, :]
+
+    @pl.when(step >= tiles)
+    def _():
+        grad, d_qkv, d_out, d_g1 = char_attn_back(x[...], packed[...], probs[...], mixed[...], gca[span((step - tiles) * ROWS, ROWS), :], weights)
+        cg[...] = grad
+        a_vec[0:1, :256] += d_g1
+        for i in range(8):
+            t, c = i // 2, i % 2
+            val = d_qkv[:, 128 * i : 128 * i + 128] if i < 6 else d_out[:, 128 * (i - 6) : 128 * (i - 6) + 128]
+            a_qo[c, :, 128 * t : 128 * t + 128] += val
+
+
+ACCS = [(2, 256, 512), (2, 256, 512), (2, 128, 1024), (8, 512)]
+
+
+def back_specs(tiles, gpool, weights):
+    one = lambda i: jnp.minimum(i, tiles - 1)
+    two = lambda i: jnp.maximum(i - tiles, 0)
+
+    def rows_at(where, r, w):
+        return pl.BlockSpec((r, w), lambda i: (where(i), 0))
+
+    once = lambda sh: pl.BlockSpec(sh, lambda i: (0,) * len(sh), pipeline_mode=pl.Buffered(1))
+    ins = [rows_at(two, ROWS, 256), pl.BlockSpec((1, ROWS // GROUP, GROUP), lambda i: (one(i), 0, 0))]
+    ins += [rows_at(two, ROWS, 768), rows_at(two, ROWS // 8, 512), rows_at(two, ROWS, 256)]
+    ins += [rows_at(one, ROWS, 256), rows_at(one, ROWS, 1024), rows_at(one, ROWS, 1024), rows_at(one, ROWS, 256)]
+    ins += [once(gpool.shape)] + [once(w.shape) for w in weights]
+    return ins, rows_at(two, ROWS, 256)
+
+
+def char_bwd_kernel(tiles, *refs):
+    ins, (cg, *accs), gca = refs[:14], refs[14:19], refs[19]
+    char_back_step(pl.program_id(0), tiles, ins, cg, gca, accs)
+
+
+def char_backward(x, cnt, saved, gpool, *weights):
     total = x.shape[0]
     tiles = total // ROWS
-    widths = [(ROWS, 768), (ROWS // 8, 512), (ROWS, 256), (ROWS, 256), (ROWS, 1024), (ROWS, 1024), (ROWS, 256)]
-    acc_shapes = [(1, 256), (256, 768), (256, 256), (1, 256), (256, 1024), (256, 1024), (1, 256)]
+    ins, out = back_specs(tiles, gpool, weights)
     return pl.pallas_call(
-        char_bwd_kernel,
-        grid=(tiles,),
-        in_specs=[rows_spec(ROWS, 256), pl.BlockSpec((1, ROWS // GROUP, GROUP), lambda i: (i, 0, 0))]
-        + [rows_spec(r, w) for r, w in widths]
-        + [full_spec(gpool.shape)]
-        + [full_spec(w.shape) for w in weights],
-        out_specs=[rows_spec(ROWS, 256)] + [full_spec(s) for s in acc_shapes],
-        out_shape=[jax.ShapeDtypeStruct((total, 256), F32)] + [jax.ShapeDtypeStruct(s, F32) for s in acc_shapes],
+        functools.partial(char_bwd_kernel, tiles),
+        grid=(2 * tiles,),
+        in_specs=ins,
+        out_specs=[out] + [full_spec(s) for s in ACCS],
+        out_shape=[jax.ShapeDtypeStruct((total, 256), F32)] + [jax.ShapeDtypeStruct(s, F32) for s in ACCS],
+        scratch_shapes=[pltpu.VMEM((total, 256), F32)],
         compiler_params=pltpu.CompilerParams(vmem_limit_bytes=VMEM_LIMIT, dimension_semantics=("arbitrary",)),
         name="char_backward",
     )(x, cnt, *saved, gpool, *weights)
@@ -658,7 +697,7 @@
     d_g2 = jnp.sum(gn2 * ahat, axis=0, keepdims=True)
     ga = cotv.astype(F32) + ln_back(ahat, ar, g2v, gn2)
     gal = ga.astype(BF16)
-    d_w4[3] = mm_tn(gal, mixed).astype(BF16)
+    d_w4[1, 1] = mm_tn(gal, mixed).astype(BF16)
     do_t = mm_nt(wout[...], gal).astype(BF16)
     do_s = []
     for h in range(HEADS):
@@ -706,9 +745,9 @@
         dv_sum[...] += mm(xt, dv)
 
     dq = jnp.transpose((dqt[...] * 0.125).astype(BF16))
-    d_w4[0] = mm_tn(xown, dq).astype(BF16)
-    d_w4[1] = dk_sum[...].astype(BF16)
-    d_w4[2] = dv_sum[...].astype(BF16)
+    d_w4[0, 0] = mm_tn(xown, dq).astype(BF16)
+    d_w4[0, 1] = dk_sum[...].astype(BF16)
+    d_w4[1, 0] = dv_sum[...].astype(BF16)
     dx_own[...] += mm_nt(dq, wq[...])
 
     @pl.loop(own + 1, nblk)
@@ -721,7 +760,11 @@
     words_grad[...] = grad
     d_vec[...] = jnp.concatenate([jnp.sum(gnf * shat, axis=0, keepdims=True), d_g2, jnp.zeros((6, width), F32)], axis=0)
     gproj = grad.astype(BF16)
-    d_proj[...] = mm_tn(pooled[...], gproj).astype(BF16)
+    gproj_w = mm_tn(pooled[...], gproj).astype(BF16)
+    hr = gproj_w.shape[0] // (2 * at.F)
+    for i in range(at.F):
+        for c in range(2):
+            d_proj[c, hr * i : hr * i + hr, :] = gproj_w[hr * (2 * i + c) : hr * (2 * i + c) + hr, :]
     gpool[...] = mm_nt(gproj, proj[...])
 
     for k in range(1, T):
@@ -745,8 +788,8 @@
     T = lax.axis_size("tp")
     nblk = 2 * T
     ff = wup.shape[1]
-    out_shapes = [((blk, width), BF16), ((3, blk), F32), ((blk, width), F32), ((blk, pooled.shape[1]), F32), (proj.shape, BF16), ((8, width), F32)]
-    out_shapes += [(w4.shape, BF16), ((2, width, ff // 2), BF16), ((2, ff // 2, width), BF16)]
+    out_shapes = [((blk, width), BF16), ((3, blk), F32), ((blk, width), F32), ((blk, pooled.shape[1]), F32), ((2, proj.shape[0] // 2, width), BF16), ((8, width), F32)]
+    out_shapes += [((2, 2) + w4.shape[1:], BF16), ((2, width, ff // 2), BF16), ((2, ff // 2, width), BF16)]
     vm = pl.BlockSpec(memory_space=pltpu.VMEM)
     return pl.pallas_call(
         word_kernel,
@@ -788,6 +831,277 @@
     )(pooled, proj, words_in, cot, vec, w4, wup, wdown)
 
 
+class Sum:
+    def __init__(self, at, source, bufs, tp_cut, fs_cut, sems, first, wide):
+        self.at, self.source, self.sems, self.first, self.wide = at, source, sems, first, wide
+        self.own, self.away, self.got, self.blocks, self.block, self.pieces, self.done = bufs
+        self.tp_cut, self.fs_cut = tp_cut, fs_cut
+
+    @staticmethod
+    def slots(F, T):
+        return 1 + (T - 1) + (F - 1) + (T - 1) + T
+
+    @staticmethod
+    def buffers(half, block, piece, F, T, wide):
+        shapes = [half, half, half, (T - 1,) + block, block, (F - 1,) + piece, ((2, T) if wide else (2,)) + piece]
+        return [pltpu.VMEM(sh, BF16) for sh in shapes]
+
+    def swap(self):
+        at = self.at
+        return remote(self.away, self.got, self.sems, self.first, {"ctx": 1 - at.c})
+
+    def to_tp(self, k):
+        return remote(self.own.at[self.tp_cut(self.at.tp(k))], self.blocks.at[k - 1], self.sems, self.first + k, {"tp": self.at.tp(k)})
+
+    def to_fs(self, k):
+        return remote(self.block.at[self.fs_cut(self.at.fs(k))], self.pieces.at[k - 1], self.sems, self.first + self.at.T - 1 + k, {"fsdp": self.at.fs(k)})
+
+    def spread(self, k, incoming=False):
+        at = self.at
+        r = self.done.at[at.c, at.tp(-k) if incoming else at.t]
+        return remote(r, r, self.sems, self.first + at.T + at.F - 2 + k, {"tp": at.tp(k)})
+
+    def side(self, k, incoming=False):
+        at = self.at
+        c = 1 - at.c if incoming else at.c
+        r = self.done.at[c, at.tp(-k)] if self.wide else self.done.at[c]
+        return remote(r, r, self.sems, self.first + 2 * at.T + at.F - 2 + k, {"ctx": 1 - at.c})
+
+    def local(self, i):
+        src = self.source.at[self.at.c if i == 0 else 1 - self.at.c]
+        return pltpu.make_async_copy(src, self.own if i == 0 else self.away, self.loc.at[i])
+
+    def fetch(self, loc):
+        self.loc = loc
+        for i in range(2):
+            self.local(i).start()
+
+    def begin_fetched(self):
+        for i in range(2):
+            self.local(i).wait()
+        self.swap().start()
+
+    def begin(self):
+        self.own[...] = self.source[self.at.c].astype(BF16)
+        self.away[...] = self.source[1 - self.at.c].astype(BF16)
+        self.swap().start()
+
+    def halves(self):
+        self.swap().wait_recv()
+        self.own[...] = (self.own[...].astype(F32) + self.got[...].astype(F32)).astype(BF16)
+        for k in range(1, self.at.T):
+            self.to_tp(k).start()
+
+    def over_tp(self):
+        total = self.own[self.tp_cut(self.at.t)].astype(F32)
+        for k in range(1, self.at.T):
+            self.to_tp(k).wait_recv()
+            total += self.blocks[k - 1].astype(F32)
+        self.block[...] = total.astype(BF16)
+        for k in range(1, self.at.F):
+            self.to_fs(k).start()
+
+    def over_fsdp(self):
+        at = self.at
+        total = self.block[self.fs_cut(at.f)].astype(F32)
+        for k in range(1, at.F):
+            self.to_fs(k).wait_recv()
+            total += self.pieces[k - 1].astype(F32)
+        if self.wide:
+            self.done[at.c, at.t] = total.astype(BF16)
+            for k in range(1, at.T):
+                self.spread(k).start()
+        else:
+            self.done[at.c] = total.astype(BF16)
+        self.side(0).start()
+
+    def pass_on(self):
+        if self.wide:
+            for k in range(1, self.at.T):
+                self.spread(k, True).wait_recv()
+                self.side(k).start()
+
+    def finish(self):
+        at = self.at
+        for k in range(at.T if self.wide else 1):
+            self.side(k, True).wait_recv()
+
+    def drain(self):
+        at = self.at
+        self.swap().wait_send()
+        for k in range(1, at.T):
+            self.to_tp(k).wait_send()
+        for k in range(1, at.F):
+            self.to_fs(k).wait_send()
+        if self.wide:
+            for k in range(1, at.T):
+                self.spread(k).wait_send()
+        for k in range(at.T if self.wide else 1):
+            self.side(k).wait_send()
+
+
+SUMS = [
+    ((2, 512, 512), (2, 512, 128), (2, 128, 128), 2, 1, False),
+    ((512, 1024), (512, 256), (128, 256), 1, 0, False),
+    ((1024, 512), (256, 512), (256, 128), 0, 1, False),
+    ((128, 512), (128, 128), (32, 128), 1, 0, True),
+    ((256, 512), (256, 128), (64, 128), 1, 0, True),
+    ((128, 1024), (32, 1024), (32, 256), 0, 1, True),
+    ((256, 512), (256, 128), (64, 128), 1, 0, True),
+]
+
+
+def cutter(shape, axis, size):
+    def cut(i):
+        return tuple(span(i * size, size) if d == axis else ALL for d in range(len(shape)))
+
+    return cut
+
+
+RESULTS = [(3, 128, 128), (128, 128), (128, 512), (512, 128), (64, 512), (64, 1024), (256, 256), (64, 768), (64, 256), (8, 128)]
+
+
+def reduce_bwd_kernel(tiles, *refs):
+    ins = refs[:14]
+    sources = refs[14:18]
+    d_vec = refs[18]
+    cg = refs[19]
+    results = refs[20 : 20 + len(RESULTS)]
+    rest = list(refs[20 + len(RESULTS) :])
+    gca = rest.pop(0)
+    accs = [rest.pop(0) for _ in ACCS]
+    at = Place()
+    bufs = [[rest.pop(0) for _ in range(7)] for _ in SUMS]
+    vec_in, send, recv, vsend, vrecv, local_sems = rest
+    slots = Sum.slots(at.F, at.T)
+    a_qo, a_up, a_dn, a_vec = accs
+    origin = list(sources) + [a_up, a_dn, a_qo]
+    sums = []
+    for i, (half, block, piece, ta, fa, wide) in enumerate(SUMS):
+        sums.append(Sum(at, origin[i], bufs[i], cutter(half, ta, block[ta]), cutter(block, fa, piece[fa]), (send, recv), i * slots, wide))
+        sums[i].loc = local_sems.at[i]
+    w4, wup, wdn, pj, up, dn, qo = sums
+    step = pl.program_id(0)
+    last = 2 * tiles - 1
+
+    def when(i, *acts):
+        @pl.when(step == i)
+        def _():
+            for act in acts:
+                act()
+
+    def open_():
+        for s in (w4, wup, wdn, pj):
+            s.fetch(s.loc)
+        greet(at.peers())
+        for s in (w4, wup, wdn, pj):
+            s.begin_fetched()
+
+    when(0, open_)
+    when(1, w4.halves)
+    when(2, wup.halves)
+    when(3, wdn.halves, pj.halves)
+    when(6, w4.over_tp)
+    when(8, up.begin, dn.begin)
+    when(10, up.halves, dn.halves, w4.over_fsdp, wup.over_tp)
+    when(13, wup.over_fsdp, wdn.over_tp, pj.over_tp)
+    char_back_step(step, tiles, ins, cg, gca, accs)
+
+    @pl.when(step == last)
+    def _():
+        qo.begin()
+        a_vec[3:5, :] = d_vec[0:2, :]
+
+        def vec_copy(i, where):
+            return remote(a_vec, vec_in.at[i], (vsend, vrecv), i, where)
+
+        vec_copy(0, {"ctx": 1 - at.c}).start()
+        wdn.over_fsdp()
+        pj.over_fsdp()
+        up.over_tp()
+        dn.over_tp()
+        qo.halves()
+        vec_copy(0, {"ctx": 1 - at.c}).wait()
+        a_vec[...] += vec_in[0]
+        for k in range(1, at.T):
+            vec_copy(k, {"tp": at.tp(k)}).start()
+        up.over_fsdp()
+        dn.over_fsdp()
+        pj.pass_on()
+        for k in range(1, at.T):
+            vec_copy(k, {"tp": at.tp(k)}).wait()
+        a_vec[...] += vec_in[1] + vec_in[2] + vec_in[3]
+        for k in range(1, at.F):
+            vec_copy(at.T - 1 + k, {"fsdp": at.fs(k)}).start()
+        qo.over_tp()
+        up.pass_on()
+        dn.pass_on()
+        for k in range(1, at.F):
+            vec_copy(at.T - 1 + k, {"fsdp": at.fs(k)}).wait()
+        total = a_vec[...] + (vec_in[4] + vec_in[5] + vec_in[6])
+        rows = []
+        for i, n in ((0, 64), (1, 64), (2, 64), (3, 128), (4, 128)):
+            v = jnp.zeros((1, n), F32)
+            for f in range(4):
+                v = jnp.where(at.f == f, total[i : i + 1, f * n : f * n + n], v)
+            rows.append(v if n == 128 else jnp.concatenate([v, jnp.zeros((1, n), F32)], axis=1))
+        results[9][...] = jnp.concatenate(rows + [jnp.zeros((3, 128), F32)], axis=0)
+        for s in (w4, wup, wdn):
+            s.finish()
+        o4, o_out, o_wup, o_wdn, o_pj, o_up, o_dn, o_qkv, o_cout = results[:9]
+        for c in range(2):
+            o_wup[:, 256 * c : 256 * c + 256] = wup.done[c].astype(F32)
+            o_wdn[256 * c : 256 * c + 256, :] = wdn.done[c].astype(F32)
+        o4[0] = w4.done[0, 0].astype(F32)
+        o4[1] = w4.done[0, 1].astype(F32)
+        o4[2] = w4.done[1, 0].astype(F32)
+        o_out[...] = jnp.transpose(w4.done[1, 1].astype(F32))
+        qo.over_fsdp()
+        for s in (pj, up, dn):
+            s.finish()
+        for t in range(at.T):
+            for c in range(2):
+                lanes = slice(256 * t + 128 * c, 256 * t + 128 * c + 128)
+                o_pj[32 * c : 32 * c + 32, 128 * t : 128 * t + 128] = pj.done[c, t].astype(F32)
+                o_up[:, lanes] = up.done[c, t].astype(F32)
+        o_dn[...] = jnp.transpose(dn.done[...].astype(F32).reshape(256, 256))
+        qo.pass_on()
+        qo.finish()
+        for t in range(at.T):
+            for c in range(2):
+                i = 2 * t + c
+                ref = o_qkv if i < 6 else o_cout
+                i = i % 6
+                ref[:, 128 * i : 128 * i + 128] = qo.done[c, t].astype(F32)
+        for s in sums:
+            s.drain()
+
+
+def reduce_backward(x, cnt, saved, gpool, weights, sources, d_vec):
+    total = x.shape[0]
+    tiles = total // ROWS
+    F, T = lax.axis_size("fsdp"), lax.axis_size("tp")
+    ins, out = back_specs(tiles, gpool, weights)
+    any_ = pl.BlockSpec(memory_space=pl.ANY)
+    scratch = [pltpu.VMEM((total, 256), F32)] + [pltpu.VMEM(s, F32) for s in ACCS]
+    for half, block, piece, _, _, wide in SUMS:
+        scratch += Sum.buffers(half, block, piece, F, T, wide)
+    count = len(SUMS) * Sum.slots(F, T)
+    vecs = 1 + (T - 1) + (F - 1)
+    scratch += [pltpu.VMEM((vecs, 8, 512), F32)]
+    scratch += [pltpu.SemaphoreType.DMA((n,)) for n in (count, count, vecs, vecs)] + [pltpu.SemaphoreType.DMA((len(SUMS), 2))]
+    return pl.pallas_call(
+        functools.partial(reduce_bwd_kernel, tiles),
+        grid=(2 * tiles,),
+        in_specs=ins + [any_] * len(sources) + [full_spec((8, 512))],
+        out_specs=[out] + [full_spec(s) for s in RESULTS],
+        out_shape=[jax.ShapeDtypeStruct((total, 256), F32)] + [jax.ShapeDtypeStruct(s, F32) for s in RESULTS],
+        scratch_shapes=scratch,
+        compiler_params=pltpu.CompilerParams(vmem_limit_bytes=VMEM_LIMIT, collective_id=2, has_side_effects=True, dimension_semantics=("arbitrary",)),
+        name="reduce_backward",
+    )(x, cnt, *saved, gpool, *weights, *sources, d_vec)
+
+
 def gather(x, name, axis):
     return lax.all_gather(x, name, axis=axis, tiled=True)
 
@@ -823,42 +1137,55 @@
         wdown = gather(gather(word_down, "fsdp", 1), "tp", 0)
         *saved, pooled_low = char_forward(x, cnt, vec, qo, up, dn)
     (block_out, rms, words_grad, gpool, d_proj, d_vec, d_w4, d_wup, d_wdown) = word_section(pooled_low, proj, words_in, cotangent, vec, w4, wup, wdown)
-    cg, d_g1, d_qkv, d_out, d_g2, d_up, d_down_t, d_pq = char_backward(x, cnt, saved, gpool, [vec, qo, up, dn])
-    ff = word_up.shape[1] // 2
-    d_q, d_k, d_v, d_wout = d_w4[0], d_w4[1], d_w4[2], d_w4[3].T
-    d_wup = jnp.moveaxis(d_wup.reshape(2, 512, 4, ff), 0, 2).reshape(512, 2048)
-    d_wdown = jnp.moveaxis(d_wdown.reshape(2, 4, ff, 512), 0, 1).reshape(2048, 512)
-    d_g1w, d_g2w = d_vec[0], d_vec[1:2]
-
-    def reduce_char(g):
-        g = lax.psum(g.astype(BF16), ("ctx", "tp"))
-        return scatter(g, "fsdp", 0).astype(F32)
-
-    def reduce_word(g, tp_axis, fsdp_axis):
-        g = scatter(g.astype(BF16), "tp", tp_axis)
-        g = lax.psum(g, "ctx")
-        return scatter(g, "fsdp", fsdp_axis).astype(F32)
-
-    d_wqkv = reduce_word(jnp.stack([d_q, d_k, d_v], axis=0), 2, 1)
+    if direct:
+        cg, g_qkv4, g_wout, g_wup, g_wdown, g_proj, g_up, g_down, g_qkv, g_out, g_vec = reduce_backward(
+            x, cnt, saved, gpool, [vec, qo, up, dn], [d_w4, d_wup, d_wdown, d_proj], d_vec
+        )
+        vecs = [g_vec[i, :n] for i, n in ((0, 64), (1, 64), (2, 64), (3, 128), (4, 128))]
+    else:
+        cg, a_qo, a_up, a_dn, a_vec = char_backward(x, cnt, saved, gpool, vec, qo, up, dn)
+
+        def reduce_char(g):
+            g = lax.psum(g.astype(BF16), ("ctx", "tp"))
+            return scatter(g, "fsdp", 0).astype(F32)
+
+        def reduce_word(g, tp_axis, fsdp_axis):
+            g = scatter(g, "tp", tp_axis)
+            g = lax.psum(g, "ctx")
+            return scatter(g, "fsdp", fsdp_axis).astype(F32)
+
+        lanes = lambda g, n: jnp.moveaxis(g.reshape(2, g.shape[1], -1, n), 0, 2).reshape(g.shape[1], -1)
+        hr = char_proj.shape[0] // 2
+        ff = word_up.shape[1] // 2
+        g_qo = reduce_char(lanes(a_qo, 128))
+        g_qkv, g_out = g_qo[:, :768], g_qo[:, 768:]
+        g_up = reduce_char(lanes(a_up, 128))
+        g_down = reduce_char(a_dn.reshape(256, 1024).T)
+        g_proj = reduce_char(jnp.moveaxis(d_proj.reshape(2, -1, hr, 512), 0, 1).reshape(256, 512))
+        g_w4 = reduce_word(d_w4.reshape(4, 512, 512), 2, 1)
+        g_qkv4, g_wout = g_w4[:3], g_w4[3].T
+        g_wup = reduce_word(lanes(d_wup, ff), 1, 0)
+        g_wdown = reduce_word(jnp.moveaxis(d_wdown.reshape(2, -1, ff, 512), 0, 1).reshape(2048, 512), 0, 1)
+        vecs = [reduce_char(v) for v in (a_vec[0, :256], a_vec[1, :256], a_vec[2, :256], d_vec[0], d_vec[1])]
     return (
         block_out,
         cg.reshape(words, slots, cdim),
         words_grad,
         rms,
-        reduce_char(d_g1[0]),
-        reduce_char(d_qkv),
-        reduce_char(d_out),
-        reduce_char(d_g2[0]),
-        reduce_char(d_up),
-        reduce_char(d_down_t.T),
-        reduce_char(d_pq[0]),
-        reduce_char(d_proj),
-        reduce_char(d_g1w),
-        jnp.moveaxis(d_wqkv, 0, 1),
-        reduce_word(d_wout, 0, 1),
-        reduce_char(d_g2w[0]),
-        reduce_word(d_wup, 1, 0),
-        reduce_word(d_wdown, 0, 1),
+        vecs[0],
+        g_qkv,
+        g_out,
+        vecs[1],
+        g_up,
+        g_down,
+        vecs[2],
+        g_proj,
+        vecs[3],
+        jnp.moveaxis(g_qkv4, 0, 1),
+        g_wout,
+        vecs[4],
+        g_wup,
+        g_wdown,
     )
 
 

time: 570 us -> 231 us (0.41)
  waiting for transfers between devices: 283 us -> 0 us
  Pallas kernels: 162 us -> 206 us
  blocking collectives: 41.1 us -> 0 us
  local copies, waits for them, and re-layouts: 41.3 us -> 17.9 us
  other arithmetic: 24.3 us -> 5.84 us
  between operations: 15.5 us -> 0.77 us
    reduce_scatter x10 -> x0, waiting for transfers between devices: 190 us -> none  [scatter(): return lax.psum_scatter(x, name, scatter_dimension=axis, tiled=True)]
    unnamed x18 -> x0, waiting for transfers between devices: 53.2 us -> none
    pallas_call x1, Pallas kernels: 44.3 us -> 87.3 us  [reduce_backward(): pl.pallas_call(functools.partial(reduce_bwd_kernel, tiles), grid=(2 * til...]
    psum x2 -> x0, waiting for transfers between devices: 39.8 us -> none  [the longest x1 24.8 us: reduce_char(): g = lax.psum(g.astype(BF16), ('ctx', 'tp'))]
    psum x2 -> x0, blocking collectives: 32.4 us -> none  [the longest x1 28.4 us: reduce_char(): g = lax.psum(g.astype(BF16), ('ctx', 'tp'))]
    convert_element_type x18 -> x0, other arithmetic: 16.9 us -> none  [the longest x9 7.9 us: reduce_char(): return scatter(g, 'fsdp', 0).astype(F32)]
    unnamed x1 -> x0, blocking collectives: 8.69 us -> none
    transpose x3 -> x0, local copies, waits for them, and re-layouts: 8.66 us -> none  [the longest x1 4.56 us: local(): d_wup = jnp.moveaxis(d_wup.reshape(2, 512, 4, ff), 0, 2).reshape(512, 2048)]
  transfers between devices with their start and end apart: 15 -> 0, of which waited for: 14 -> 0; matrix products, arithmetic and copies ran while one was open for 8% -> 0% of each run, Pallas kernels for 8% -> 0%
where the time goes in v3:
time: 231 us; the launch traced here: 230 us
  Pallas kernels  206 us (89%)
  local copies, waits for them, and re-layouts  17.9 us (8%)
  other arithmetic  5.84 us (3%)
    pallas_call x1, Pallas kernels, reduce_backward(): pl.pallas_call(functools.partial(reduce_bwd_kernel, tiles), grid=(2 * til...  87.3 us
    pallas_call x1, Pallas kernels, gather_forward(): pl.pallas_call(gather_fwd_kernel, grid=(tiles,), in_specs=[rows_spec(ROWS...  69.1 us
    pallas_call x1, Pallas kernels, word_section(): pl.pallas_call(word_kernel, in_specs=[vm] * 8, out_specs=[vm] * len(out_s...  49.2 us
    unnamed x38, local copies, waits for them, and re-layouts  13.8 us

profile of v3, /device:TPU:0, one launch (start us, length us, event | category | flops | bytes accessed | tf_op | source)
XLA Modules:
  0.0 230.1 jit_solution(3872287656478448247)
XLA Ops:
  0.7 0.7 bitcast_convert_fusion.4
  1.3 0.7 convert_element_type.6
  2.0 0.7 bitcast_convert_fusion.2
  2.7 0.7 bitcast_convert_fusion
  3.3 0.6 stack.47.refs_6_
  4.0 0.1 broadcast_in_dim.10
  4.1 0.9 copy.36
  4.9 1.6 pad_maximum_fusion.1.refs_7_
  6.5 0.1 broadcast_in_dim.11
  6.6 0.7 broadcast_in_dim.12.refs_1_
  7.3 1.6 pad_maximum_fusion.refs_2_
  8.9 69.1 %gather_forward.1 = (bf16[4096,768]{1,0:T(8,128)(2,1)}, f32[512,512]{1,0:T(8,128)}, bf16[4096,256]{1,0:T(8,128)(2,1)}, f32[4096,256]{1,0:T(8,128)}, bf16[4096,10...) custom-call(bf16[4096,256]{1,0:T(8,128)(2,1)} %bitcast.35, ...), custom_call_target="tpu_custom_call" | custom-call | tf_op jit(solution)/shard_map/gather_forward/pallas_call | solution.py:532
  78.0 49.2 %word_section.1 = (bf16[256,512]{1,0:T(8,128)(2,1)}, f32[3,256]{1,0:T(4,128)}, f32[256,512]{1,0:T(8,128)}, f32[256,256]{1,0:T(8,128)}, bf16[2,128,512]{2,1,0:T(8...) custom-call(bf16[256,256]{1,0:T(8,128)(2,1)} %get-tuple-element.54.p, ...), custom_call_target="tpu_custom_call" | custom-call | tf_op jit(solution)/shard_map/word_section/pallas_call | solution.py:794
  127.2 0.0 copy-start.3
  127.2 87.3 %reduce_backward.1 = (f32[4096,256]{1,0:T(8,128)}, f32[3,128,128]{2,1,0:T(8,128)}, f32[128,128]{1,0:T(8,128)}, f32[128,512]{1,0:T(8,128)}, f32[512,128]{1,0:T(8,...) custom-call(bf16[4096,256]{1,0:T(8,128)(2,1)} %bitcast.36, ...), custom_call_target="tpu_custom_call" | custom-call | tf_op jit(solution)/shard_map/reduce_backward/pallas_call | solution.py:1093
  214.5 1.3 slice_bitcast_fusion
  215.8 1.3 slice_bitcast_fusion.2
  217.1 0.0 copy-done.3
  217.1 0.7 copy.50
  217.8 0.0 copy-start
  217.8 0.0 copy-start.11
  217.8 0.0 copy-start.7
  217.8 0.0 copy-start.10
  217.8 0.0 copy-start.5
  217.8 4.7 %copy.51 = f32[256,16,256]{2,1,0:T(8,128)} copy(f32[256,16,256]{2,1,0:T(8,128)} %bitcast.37) | data formatting | bytes 8388608
  222.6 0.0 copy-done
  222.6 0.0 copy-start.4
  222.6 0.0 copy-start.8
  222.6 0.0 copy-start.6
  222.6 0.0 copy-start.9
  222.6 0.0 copy-start.2
  222.6 0.0 copy-start.1
  222.6 0.8 copy.52
  223.4 0.0 copy-done.11
  223.4 0.6 copy.53
  224.0 0.0 copy-done.7
  224.0 0.7 copy.54
  224.7 0.0 copy-done.10
  224.7 0.6 copy.55
  225.3 0.0 copy-done.5
  225.3 0.7 copy.56
  226.0 0.0 copy-done.4
  226.0 0.7 copy.57
  226.7 0.0 copy-done.8
  226.7 0.7 copy.58
  227.4 0.0 copy-done.6
  227.4 0.7 copy.59
  228.1 0.0 copy-done.9
  228.1 0.6 copy.60
  228.7 0.0 copy-done.2
  228.7 0.7 copy.61
  229.4 0.0 copy-done.1
  229.4 0.7 copy.62
  (2 shorter events, 0.0 us)
Async XLA Ops:
  127.2 89.9 %copy-start.3 = (bf16[256,512]{1,0:T(8,128)(2,1)S(1)}, bf16[256,512]{1,0:T(8,128)(2,1)}, u32[]{:S(2)}) copy-start(bf16[256,512]{1,0:T(8,128)(2,1)} %get-tuple-element.117) | copy-start | bytes 786436
  217.8 4.7 %copy-start = (f32[256,512]{1,0:T(8,128)S(1)}, f32[256,512]{1,0:T(8,128)}, u32[]{:S(2)}) copy-start(f32[256,512]{1,0:T(8,128)} %get-tuple-element.119) | copy-start | bytes 1572868
  217.8 5.6 %copy-start.11 = (f32[3,256]{1,0:T(4,128)S(1)}, f32[3,256]{1,0:T(4,128)}, u32[]{:S(2)}) copy-start(f32[3,256]{1,0:T(4,128)} %get-tuple-element.120) | copy-start | bytes 9220
  217.8 6.2 %copy-start.7 = (f32[64,768]{1,0:T(8,128)S(1)}, f32[64,768]{1,0:T(8,128)}, u32[]{:S(2)}) copy-start(f32[64,768]{1,0:T(8,128)} %get-tuple-element.122) | copy-start | bytes 589828
  217.8 6.9 %copy-start.10 = (f32[64,256]{1,0:T(8,128)S(1)}, f32[64,256]{1,0:T(8,128)}, u32[]{:S(2)}) copy-start(f32[64,256]{1,0:T(8,128)} %get-tuple-element.123) | copy-start | bytes 196612
  217.8 7.5 %copy-start.5 = (f32[64,1024]{1,0:T(8,128)S(1)}, f32[64,1024]{1,0:T(8,128)}, u32[]{:S(2)}) copy-start(f32[64,1024]{1,0:T(8,128)} %get-tuple-element.125) | copy-start | bytes 786436
  222.6 3.5 %copy-start.4 = (f32[256,256]{1,0:T(8,128)S(1)}, f32[256,256]{1,0:T(8,128)}, u32[]{:S(2)}) copy-start(f32[256,256]{1,0:T(8,128)} %get-tuple-element.126) | copy-start | bytes 786436
  222.6 4.2 %copy-start.8 = (f32[64,512]{1,0:T(8,128)S(1)}, f32[64,512]{1,0:T(8,128)}, u32[]{:S(2)}) copy-start(f32[64,512]{1,0:T(8,128)} %get-tuple-element.128) | copy-start | bytes 393220
  222.6 4.8 %copy-start.6 = (f32[3,128,128]{2,1,0:T(8,128)S(1)}, f32[3,128,128]{2,1,0:T(8,128)}, u32[]{:S(2)}) copy-start(f32[3,128,128]{2,1,0:T(8,128)} %get-tuple-element.86) | copy-start | bytes 589828
  222.6 5.5 %copy-start.9 = (f32[128,128]{1,0:T(8,128)S(1)}, f32[128,128]{1,0:T(8,128)}, u32[]{:S(2)}) copy-start(f32[128,128]{1,0:T(8,128)} %get-tuple-element.131) | copy-start | bytes 196612
  222.6 6.1 %copy-start.2 = (f32[128,512]{1,0:T(8,128)S(1)}, f32[128,512]{1,0:T(8,128)}, u32[]{:S(2)}) copy-start(f32[128,512]{1,0:T(8,128)} %get-tuple-element.133) | copy-start | bytes 786436
  222.6 6.8 %copy-start.1 = (f32[512,128]{1,0:T(8,128)S(1)}, f32[512,128]{1,0:T(8,128)}, u32[]{:S(2)}) copy-start(f32[512,128]{1,0:T(8,128)} %get-tuple-element.134) | copy-start | bytes 786436

commit v4 on v3

v4 whole, which is shorter than its diff:
```python
import functools

import jax
import jax.numpy as jnp
from jax import lax
from jax.experimental import pallas as pl
from jax.experimental.pallas import tpu as pltpu
from jax.sharding import PartitionSpec as P

CHEADS = 4
HEADS = 8
HEAD = 64
EPSILON = 1e-05
MASKED = -1e30
CGELU = 0.7978845608028654
AGELU = 0.044715
ROWS = 512
GROUP = 128
F32 = jnp.float32
BF16 = jnp.bfloat16
VMEM_LIMIT = 66_000_000


def mm(a, b):
    return lax.dot_general(a, b, (((1,), (0,)), ((), ())), preferred_element_type=F32)


def mm_nt(a, b):
    return lax.dot_general(a, b, (((1,), (1,)), ((), ())), preferred_element_type=F32)


def mm_tn(a, b):
    return lax.dot_general(a, b, (((0,), (0,)), ((), ())), preferred_element_type=F32)


def ln_parts(x):
    c = x - jnp.mean(x, axis=-1, keepdims=True)
    r = lax.rsqrt(jnp.mean(c * c, axis=-1, keepdims=True) + EPSILON)
    return c * r, r


def ln_back(xhat, r, gain, g):
    gg = g * gain
    a = jnp.mean(gg, axis=-1, keepdims=True)
    b = jnp.mean(gg * xhat, axis=-1, keepdims=True)
    return r * (gg - a - xhat * b)


def gelu_both(x):
    x2 = x * x
    y = (CGELU * AGELU) * x2 + CGELU
    hp = 0.5 * jnp.tanh(x * y) + 0.5
    g = x * hp
    d = hp + (g - g * hp) * (6.0 * y - 4.0 * CGELU)
    return g, d


def pair_masks(rows):
    lane = lax.broadcasted_iota(jnp.int32, (rows, 128), 1)
    return lane < HEAD


def split_heads(x, low_lanes):
    zero = jnp.zeros_like(x)
    return jnp.where(low_lanes, x, zero), jnp.where(low_lanes, zero, x)


def stack_heads(x, low_lanes):
    a, b = split_heads(x, low_lanes)
    return jnp.concatenate([a, b], axis=0)


def word_of_lane(width):
    return (lax.broadcasted_iota(jnp.int32, (16, width), 1) % GROUP) // 16


def compress(blocks, lane_word):
    out = blocks[0:16, :]
    for w in range(1, GROUP // 16):
        out = jnp.where(lane_word == w, blocks[16 * w : 16 * w + 16, :], out)
    return out


def expand(dense, lane_word):
    zero = jnp.zeros_like(dense)
    return jnp.concatenate(
        [jnp.where(lane_word == w, dense, zero) for w in range(GROUP // 16)], axis=0
    )


def pool_weights(am, q_row, cnt_col):
    words = am.shape[0] // 16
    am3 = am.reshape(words, 16, am.shape[1])
    logits = jnp.sum(am * q_row, axis=-1, keepdims=True)
    slot = (lax.broadcasted_iota(jnp.int32, (am.shape[0], 1), 0) % 16).astype(F32)
    logits = jnp.where(slot < cnt_col, logits, MASKED).reshape(words, 16, 1)
    e = jnp.exp(logits - jnp.max(logits, axis=1, keepdims=True))
    w = e / jnp.sum(e, axis=1, keepdims=True)
    return am3, w


def count_column(cnt_row):
    return jnp.transpose(jnp.broadcast_to(cnt_row, (GROUP, GROUP)))[:, 0:1]


def char_attn_tile(x, cnt, weights):
    g1, wqkv, wout = weights[:3]
    groups = x.shape[0] // GROUP
    xf = x.astype(F32)
    xhat, _ = ln_parts(xf)
    normed = (xhat * g1).astype(BF16)
    packed = mm(normed, wqkv).astype(BF16)
    low = pair_masks(GROUP)
    lw = word_of_lane(2 * GROUP)
    slot = lax.broadcasted_iota(jnp.int32, (16, 2 * GROUP), 0).astype(F32)
    raw, values, scores = [], [], []
    for g in range(groups):
        r = slice(g * GROUP, (g + 1) * GROUP)
        for p in range(CHEADS // 2):
            q = packed[r, 128 * p : 128 * p + 128] * BF16(0.125)
            values.append(packed[r, 512 + 128 * p : 640 + 128 * p])
            raw.append(mm_nt(packed[r, 256 + 128 * p : 384 + 128 * p], stack_heads(q, low)))
    pairs = len(raw)
    for i, st in enumerate(raw):
        cnt_row = cnt[i // 2 : i // 2 + 1, :]
        scores.append(jnp.where(slot < jnp.concatenate([cnt_row, cnt_row], axis=1), compress(st, lw), MASKED))
    scores = jnp.concatenate(scores, axis=0).reshape(pairs, 16, 2 * GROUP)
    e = jnp.exp(scores - jnp.max(scores, axis=1, keepdims=True))
    probs = e / jnp.sum(e, axis=1, keepdims=True)
    low_probs = probs.astype(BF16)
    spread = [expand(low_probs[i], lw) for i in range(pairs)]
    mixed = [mm_tn(pt, v) for pt, v in zip(spread, values)]
    mixed = [jnp.where(low, o[:GROUP], o[GROUP:]) for o in mixed]
    probs = jnp.concatenate([jnp.concatenate([probs[2 * g], probs[2 * g + 1]], axis=1) for g in range(groups)], axis=0)
    mixed = jnp.concatenate([jnp.concatenate(mixed[2 * g : 2 * g + 2], axis=1) for g in range(groups)], axis=0).astype(BF16)
    return packed, probs, mixed, xf + mm(mixed, wout)


def char_mlp_tile(aa, cnt, weights):
    _, _, _, g2, wup, wdown, pq = weights
    ahat, _ = ln_parts(aa)
    middle = (ahat * g2).astype(BF16)
    upper, dgelu = gelu_both(mm(middle, wup))
    upper = upper.astype(BF16)
    am = aa + mm(upper, wdown)
    cols = jnp.concatenate([count_column(cnt[g : g + 1, :]) for g in range(aa.shape[0] // GROUP)], axis=0)
    am3, w = pool_weights(am, pq, cols)
    pooled = jnp.sum(w * am3, axis=1)
    return upper, dgelu.astype(BF16), am, pooled.astype(BF16)


def count_lanes(counts):
    take = GROUP // 16
    w = lax.broadcasted_iota(jnp.int32, (128, GROUP), 0)
    l = lax.broadcasted_iota(jnp.int32, (128, GROUP), 1)
    spread = (lax.rem(w, take) == l // 16).astype(BF16)
    g = lax.broadcasted_iota(jnp.int32, (128 // take, 128), 0)
    lane = lax.broadcasted_iota(jnp.int32, (128 // take, 128), 1)
    rows = []
    for r in range(counts.shape[0]):
        one = jnp.where(lane // take == g, counts[r : r + 1, :].astype(F32), 0.0).astype(BF16)
        rows.append(mm(one, spread))
    return jnp.concatenate(rows, axis=0)


def full_spec(shape):
    return pl.BlockSpec(shape, lambda i: (0,) * len(shape))


def rows_spec(rows, width):
    return pl.BlockSpec((rows, width), lambda i: (i, 0))


def char_mlp_back(cnt, aa, upper, dgelu, am, gpool_ref, base, weights):
    _, _, _, g2, wup, wdown, pq = weights
    rows = aa.shape[0]
    words = rows // 16
    cols = jnp.concatenate([count_column(cnt[g : g + 1, :]) for g in range(rows // GROUP)], axis=0)
    _, w = pool_weights(am, pq, cols)
    gp = jnp.concatenate(
        [jnp.broadcast_to(gpool_ref[pl.ds(base + i, 1), :], (16, 256)) for i in range(words)], axis=0
    )
    dw = jnp.sum(gp * am, axis=-1, keepdims=True).reshape(words, 16, 1)
    dlog = (w * (dw - jnp.sum(w * dw, axis=1, keepdims=True))).reshape(rows, 1)
    gm = w.reshape(rows, 1) * gp + dlog * pq
    d_pq = jnp.sum(dlog * am, axis=0, keepdims=True)
    gdl = gm.astype(BF16)
    d_down_t = mm_tn(gdl, upper)
    ghid = (dgelu.astype(F32) * mm_nt(gdl, wdown)).astype(BF16)
    ahat, ar = ln_parts(aa)
    middle = (ahat * g2).astype(BF16)
    d_up = mm_tn(middle, ghid)
    gmid = mm_nt(ghid, wup)
    gca = gm + ln_back(ahat, ar, g2, gmid)
    d_g2 = jnp.sum(gmid * ahat, axis=0, keepdims=True)
    return gca, d_up, d_down_t, d_g2, d_pq


def char_attn_back(x, packed, probs, mixed, gca, weights):
    g1, wqkv, wout = weights[:3]
    groups = x.shape[0] // GROUP
    low = pair_masks(GROUP)
    lw = word_of_lane(2 * GROUP)
    gcl = gca.astype(BF16)
    d_out = mm_tn(mixed, gcl)
    gcm = mm_nt(gcl, wout).astype(BF16)
    keys, queries, grads, raw, prs = [], [], [], [], []
    for g in range(groups):
        r = slice(g * GROUP, (g + 1) * GROUP)
        for p in range(CHEADS // 2):
            queries.append(stack_heads(packed[r, 128 * p : 128 * p + 128] * BF16(0.125), low))
            keys.append(packed[r, 256 + 128 * p : 384 + 128 * p])
            grads.append(stack_heads(gcm[r, 128 * p : 128 * p + 128], low))
            raw.append(mm_nt(packed[r, 512 + 128 * p : 640 + 128 * p], grads[-1]))
            prs.append(probs[16 * g : 16 * g + 16, 256 * p : 256 * p + 256])
    pairs = len(raw)
    dp = jnp.concatenate([compress(v, lw) for v in raw], axis=0).reshape(pairs, 16, 2 * GROUP)
    pr = jnp.concatenate(prs, axis=0).reshape(pairs, 16, 2 * GROUP)
    ds = (pr * (dp - jnp.sum(pr * dp, axis=1, keepdims=True))).astype(BF16)
    pr = pr.astype(BF16)
    dst = [expand(ds[i], lw) for i in range(pairs)]
    pt = [expand(pr[i], lw) for i in range(pairs)]
    dq = [mm_tn(dst[i], keys[i]) for i in range(pairs)]
    dq = [jnp.where(low, o[:GROUP], o[GROUP:]) * 0.125 for o in dq]
    dk = [mm(dst[i], queries[i]) for i in range(pairs)]
    dv = [mm(pt[i], grads[i]) for i in range(pairs)]
    dqkv = [jnp.concatenate([v[2 * g + p] for v in (dq, dk, dv) for p in range(2)], axis=1) for g in range(groups)]
    dqkv = jnp.concatenate(dqkv, axis=0).astype(BF16)
    xhat, xr = ln_parts(x.astype(F32))
    normed = (xhat * g1).astype(BF16)
    gn = mm_nt(dqkv, wqkv)
    grad = gca + ln_back(xhat, xr, g1, gn)
    return grad, mm_tn(normed, dqkv), d_out, gn * xhat


def char_back_step(step, tiles, ins, cg, gca, accs, gains):
    x, cnt, packed, probs, mixed, aa, upper, dgelu, am, gpool, vec, qo, up, dn = ins
    a_qo, a_up, a_dn, a_vec = accs
    weights = char_weights(vec, qo, up, dn)

    @pl.when(step == 0)
    def _():
        for acc in accs:
            acc[...] = jnp.zeros_like(acc)

    @pl.when(step < tiles)
    def _():
        grad, d_up, d_dn, d_g2, d_pq = char_mlp_back(cnt[0], aa[...], upper[...], dgelu[...], am[...], gpool, step * (ROWS // 16), weights)
        gca[span(step * ROWS, ROWS), :] = grad
        if gains:
            a_vec[1:2, :256] += d_g2
        a_vec[2:3, :256] += d_pq
        for i in range(8):
            t, c = i // 2, i % 2
            a_up[c, :, 128 * t : 128 * t + 128] += d_up[:, 128 * i : 128 * i + 128]
        for c in range(2):
            a_dn[c] += d_dn[128 * c : 128 * c + 128, :]

    @pl.when(step >= tiles)
    def _():
        r = span((step - tiles) * ROWS, ROWS)
        grad, d_qkv, d_out, terms = char_attn_back(x[...], packed[...], probs[...], mixed[...], gca[r, :], weights)
        cg[...] = grad
        if gains:
            a_vec[0:1, :256] += jnp.sum(terms, axis=0, keepdims=True)
        for i in range(8):
            t, c = i // 2, i % 2
            val = d_qkv[:, 128 * i : 128 * i + 128] if i < 6 else d_out[:, 128 * (i - 6) : 128 * (i - 6) + 128]
            a_qo[c, :, 128 * t : 128 * t + 128] += val


ACCS = [(2, 256, 512), (2, 256, 512), (2, 128, 1024), (8, 512)]


def back_specs(tiles, gpool, weights):
    one = lambda i: jnp.minimum(i, tiles - 1)
    two = lambda i: jnp.maximum(i - tiles, 0)

    def rows_at(where, r, w):
        return pl.BlockSpec((r, w), lambda i: (where(i), 0))

    once = lambda sh: pl.BlockSpec(sh, lambda i: (0,) * len(sh), pipeline_mode=pl.Buffered(1))
    ins = [rows_at(two, ROWS, 256), pl.BlockSpec((1, ROWS // GROUP, GROUP), lambda i: (one(i), 0, 0))]
    ins += [rows_at(two, ROWS, 768), rows_at(two, ROWS // 8, 512), rows_at(two, ROWS, 256)]
    ins += [rows_at(one, ROWS, 256), rows_at(one, ROWS, 1024), rows_at(one, ROWS, 1024), rows_at(one, ROWS, 256)]
    ins += [once(gpool.shape)] + [once(w.shape) for w in weights]
    return ins, rows_at(two, ROWS, 256)


def char_bwd_kernel(tiles, *refs):
    ins, (cg, *accs), gca = refs[:14], refs[14:19], refs[19]
    char_back_step(pl.program_id(0), tiles, ins, cg, gca, accs, True)


def char_backward(x, cnt, saved, gpool, *weights):
    total = x.shape[0]
    tiles = total // ROWS
    ins, out = back_specs(tiles, gpool, weights)
    return pl.pallas_call(
        functools.partial(char_bwd_kernel, tiles),
        grid=(2 * tiles,),
        in_specs=ins,
        out_specs=[out] + [full_spec(s) for s in ACCS],
        out_shape=[jax.ShapeDtypeStruct((total, 256), F32)] + [jax.ShapeDtypeStruct(s, F32) for s in ACCS],
        scratch_shapes=[pltpu.VMEM((total, 256), F32)],
        compiler_params=pltpu.CompilerParams(vmem_limit_bytes=VMEM_LIMIT, dimension_semantics=("arbitrary",)),
        name="char_backward",
    )(x, cnt, *saved, gpool, *weights)


MESH = pl.DeviceIdType.MESH


def remote(src, dst, sems, index, where):
    return pltpu.make_async_remote_copy(
        src_ref=src, dst_ref=dst,
        send_sem=sems[0] if index is None else sems[0].at[index],
        recv_sem=sems[1] if index is None else sems[1].at[index],
        device_id=where, device_id_type=MESH,
    )


def span(start, size):
    return pl.ds(pl.multiple_of(start, size), size)


class Place:
    def __init__(self):
        self.f, self.c, self.t = lax.axis_index("fsdp"), lax.axis_index("ctx"), lax.axis_index("tp")
        self.F, self.T = lax.axis_size("fsdp"), lax.axis_size("tp")

    def fs(self, k):
        return lax.rem(self.f + k + self.F, self.F)

    def tp(self, k):
        return lax.rem(self.t + k + self.T, self.T)

    def peers(self):
        out = [{"fsdp": self.fs(k)} for k in range(1, self.F)]
        out += [{"tp": self.tp(k)} for k in range(1, self.T)]
        out += [{"ctx": 1 - self.c, "tp": self.tp(k)} for k in range(1, self.T)]
        return out + [{"ctx": 1 - self.c}]


def call(peers):
    for where in peers:
        pl.semaphore_signal(pltpu.get_barrier_semaphore(), inc=1, device_id=where, device_id_type=MESH)


def meet(peers):
    pl.semaphore_wait(pltpu.get_barrier_semaphore(), len(peers))


def greet(peers):
    call(peers)
    meet(peers)


class Piece:
    def __init__(self, at, shard, whole, mine, landing, region, sems, local_sem, first, side=True, core=None, source=None):
        self.at, self.shard, self.whole = at, shard, whole
        self.mine, self.landing, self.region = mine, landing, region
        self.sems, self.local_sem, self.first = sems, local_sem, first
        self.cores, self.core, self.source = side, core, source

    @staticmethod
    def slots(F, T):
        return (F - 1) + (T - 1) + T

    def held(self, act, other=False):
        if self.core is None:
            act()
        else:
            pl.when(self.at.c == (1 - self.core if other else self.core))(act)

    def local(self, src):
        at = self.at
        return pltpu.make_async_copy(src, self.whole.at[self.landing(at.f, at.c, at.t)], self.local_sem)

    def z(self, k, src=None):
        at = self.at
        f = at.fs(-k) if src is None else at.f
        dst = self.whole.at[self.landing(f, at.c, at.t)]
        return remote(dst if src is None else src, dst, self.sems, self.first + k - 1, {"fsdp": at.fs(k)})

    def plane(self, k, incoming=False):
        at = self.at
        r = self.whole.at[self.region(at.c, at.tp(-k) if incoming else at.t)]
        return remote(r, r, self.sems, self.first + at.F - 1 + k - 1, {"tp": at.tp(k)})

    def side(self, k, incoming=False):
        at = self.at
        c = at.c if self.core is not None else (1 - at.c if incoming else at.c)
        r = self.whole.at[self.region(c, at.tp(-k))]
        return remote(r, r, self.sems, self.first + at.F + at.T - 2 + k, {"ctx": 1 - at.c})

    def begin(self):
        at = self.at

        def go(src):
            self.local(src).start()
            for k in range(1, at.F):
                self.z(k, src).start()

        if self.source is not None:
            for cond, src in self.source:
                pl.when(cond)(functools.partial(go, src))
        else:
            self.held(lambda: go(self.shard.at[self.mine(at.c, at.t)]))

    def landed(self):
        at = self.at
        dst = self.whole.at[self.landing(at.f, at.c, at.t)]
        pltpu.make_async_copy(dst, dst, self.local_sem).wait()
        for k in range(1, at.F):
            self.z(k).wait_recv()

    def spread(self):
        def go():
            self.landed()
            if self.region is not None:
                for k in range(1, self.at.T):
                    self.plane(k).start()
                if self.cores:
                    self.side(0).start()

        self.held(go)

    def pass_on(self):
        def go():
            for k in range(1, self.at.T):
                self.plane(k, True).wait_recv()
                if self.cores:
                    self.side(k).start()

        if self.region is not None:
            self.held(go)

    def arrive(self):
        def go():
            for k in range(self.at.T):
                self.side(k, True).wait_recv()

        if self.region is not None and self.cores:
            self.held(go, True)

    def drain(self):
        def go():
            for k in range(1, self.at.F):
                self.z(k).wait_send()
            if self.region is not None:
                for k in range(1, self.at.T):
                    self.plane(k).wait_send()
                if self.cores:
                    for k in range(self.at.T):
                        self.side(k).wait_send()

        self.held(go)


ALL = slice(None)
GATHERED = [((256, 1024), BF16), ((256, 1024), BF16), ((4, 256, 256), BF16), ((256, 512), BF16), ((4, 8, 128), F32), ((3, 512, 512), BF16), ((512, 512), BF16), ((512, 256), BF16), ((256, 512), BF16)]


def gather_pieces(at, shards, wholes, sems, local_sems):
    F, T = at.F, at.T
    qkv, out, up, dn, pj, sm, w3, wo, wu, wd = shards
    rq, rd, rw = up.shape[0], dn.shape[0], w3.shape[1]
    cu = wu.shape[1] // 2
    lanes = lambda c, t: span(256 * t + 128 * c, 128)
    cols = (lambda c, t: (ALL, lanes(c, t)), lambda f, c, t: (span(f * rq, rq), lanes(c, t)), lambda c, t: (ALL, lanes(c, t)))
    n = qkv.shape[1] // 256
    inside = lax.rem(at.t, n)
    qo_source = [(at.t < n, qkv.at[:, span(256 * inside + 128 * at.c, 128)]), (at.t == n, out.at[:, span(128 * at.c, 128)])]
    quarter = rd // T
    slots = Piece.slots(F, T)
    specs = [
        (None, wholes[0], *cols, dict(source=qo_source)),
        (up, wholes[1], *cols, {}),
        (dn, wholes[2], lambda c, t: (span(quarter * t, quarter), span(128 * c, 128)), lambda f, c, t: (f, span(quarter * t, quarter), span(128 * c, 128)), lambda c, t: (ALL, span(quarter * t, quarter), span(128 * c, 128)), {}),
        (pj, wholes[3], lambda c, t: (ALL, span(128 * t, 128)), lambda f, c, t: (span(f * rq, rq), span(128 * t, 128)), lambda c, t: (ALL, span(128 * t, 128)), dict(side=False)),
        (sm, wholes[4], lambda c, t: (ALL, ALL), lambda f, c, t: (f,), None, dict(side=False)),
        (w3, wholes[5], lambda c, t: (span(0, 2),), lambda f, c, t: (span(0, 2), span(f * rw, rw), span(128 * t, 128)), lambda c, t: (span(0, 2), ALL, span(128 * t, 128)), dict(core=0)),
        (w3, wholes[5], lambda c, t: (pl.ds(2, 1),), lambda f, c, t: (pl.ds(2, 1), span(f * rw, rw), span(128 * t, 128)), lambda c, t: (pl.ds(2, 1), ALL, span(128 * t, 128)), dict(core=1)),
        (wo, wholes[6], lambda c, t: (ALL, ALL), lambda f, c, t: (span(t * rw, rw), span(128 * f, 128)), lambda c, t: (span(t * rw, rw), ALL), dict(core=1)),
        (wu, wholes[7], lambda c, t: (ALL, span(cu * c, cu)), lambda f, c, t: (span(f * rw, rw), ALL), None, {}),
        (wd, wholes[8], lambda c, t: (span(cu * c, cu), ALL), lambda f, c, t: (ALL, span(f * rw, rw)), None, {}),
    ]
    return [
        Piece(at, shard, whole, mine, landing, region, sems, local_sems.at[i], i * slots, **more)
        for i, (shard, whole, mine, landing, region, more) in enumerate(specs)
    ]


PIECES = 10


FWD_OUTS = [(ROWS, 768, BF16), (ROWS // 8, 512, F32), (ROWS, 256, BF16), (ROWS, 256, F32), (ROWS, 1024, BF16), (ROWS, 1024, BF16), (ROWS, 256, F32), (ROWS // 16, 256, BF16)]


def char_weights(vec, qo, up, dn):
    return (vec[0:1, :256], qo[:, :768], qo[:, 768:], vec[1:2, :256], up[...], dn[...], vec[2:3, :256])


def char_fwd_kernel(x, cnt, vec, qo, up, dn, *outs):
    w = char_weights(vec, qo, up, dn)
    first = char_attn_tile(x[...], cnt[0], w)
    for ref, val in zip(outs, first + char_mlp_tile(first[3], cnt[0], w)):
        ref[...] = val


def char_forward(x, cnt, *weights):
    tiles = x.shape[0] // ROWS
    return pl.pallas_call(
        char_fwd_kernel,
        grid=(tiles,),
        in_specs=[rows_spec(ROWS, 256), pl.BlockSpec((1, ROWS // GROUP, GROUP), lambda i: (i, 0, 0))] + [full_spec(w.shape) for w in weights],
        out_specs=[rows_spec(r, w) for r, w, _ in FWD_OUTS],
        out_shape=[jax.ShapeDtypeStruct((r * tiles, w), d) for r, w, d in FWD_OUTS],
        compiler_params=pltpu.CompilerParams(vmem_limit_bytes=VMEM_LIMIT, dimension_semantics=("arbitrary",)),
        name="char_forward",
    )(x, cnt, *weights)


def vectors(sm):
    rows = []
    for i, n in enumerate((64, 64, 64, 128, 128)):
        v = jnp.concatenate([sm[f, i : i + 1, :n] for f in range(sm.shape[0])], axis=1)
        rows.append(v if n == 128 else jnp.concatenate([v, jnp.zeros_like(v)], axis=1))
    return jnp.concatenate(rows + [jnp.zeros((3, 512), F32)], axis=0)


CHUNKS = ((0, 4), (4, 6), (6, 8))
LAG = 5


def gather_fwd_kernel(*refs):
    refs = list(refs)
    take = lambda n: [refs.pop(0) for _ in range(n)]
    x, counts, words_in = take(3)
    small_in = take(5)
    shards = take(PIECES - 1)
    outs = take(len(FWD_OUTS))
    full_out = take(len(GATHERED))
    vec_out, cnt_out, xall = take(3)
    wholes = take(len(GATHERED))
    vec, cnt, xown, pool, kept, small, send, recv, xsend, xrecv, local_sems = refs
    shards.insert(5, small)
    at = Place()
    T = at.T
    own = at.c * T + at.t
    part = ROWS // 16
    pieces = gather_pieces(at, shards, wholes, (send, recv), local_sems)
    qo, up, dn, pj, sm, wa, wb, wo, zu, zd = pieces
    step = pl.program_id(0)
    last = pl.num_programs(0) - 1

    def out(i):
        return pltpu.make_async_copy(wholes[i], full_out[i], local_sems.at[PIECES + i])

    def chunk(i):
        lo, hi = CHUNKS[i]
        return span(lo * part, (hi - lo) * part) if lo % (hi - lo) == 0 else pl.ds(lo * part, (hi - lo) * part)

    def row_copy(i, k, incoming=False):
        dst = xall.at[at.c * T + (at.tp(-k) if incoming else at.t), chunk(i)]
        return remote(dst if incoming else xown.at[chunk(i)], dst, (xsend, xrecv), i * 2 * T + k - 1, {"tp": at.tp(k)})

    def side_copy(i, k):
        dst = xall.at[at.tp(-k), chunk(i)]
        return remote(xown.at[chunk(i)] if k == 0 else dst, dst, (xsend, xrecv), i * 2 * T + T - 1 + k, {"ctx": 1 - at.c})

    def keep(i):
        return pltpu.make_async_copy(xown.at[chunk(i)], xall.at[own, chunk(i)], local_sems.at[PIECES + len(GATHERED) + i])

    def cross_copy(k):
        dst = xall.at[own, chunk(1)]
        return remote(xown.at[chunk(1)], dst, (xsend, xrecv), 2 * T + T - 1 + k, {"ctx": 1, "tp": at.tp(k)})

    def crossed(k):
        dst = xall.at[at.tp(-k), chunk(1)]
        return remote(dst, dst, (xsend, xrecv), 2 * T + T - 1 + k, {"ctx": 1 - at.c})

    def send_rows(i):
        keep(i).start()
        for k in range(1, T):
            pl.when(((at.c == 0) & (i == 0)) | (at.t + k < T))(lambda k=k: row_copy(i, k).start())

        @pl.when(at.c == 0)
        def _():
            for k in range(T if i else 1):
                (cross_copy(k) if i else side_copy(0, 0)).start()

    def pass_rows(i):
        @pl.when(at.c == 0)
        def _():
            for k in range(1, T):
                row_copy(i, k, True).wait_recv()
                side_copy(i, k).start()

    def take_rows(i):
        for k in range(T):
            pl.when(at.c == 1)(lambda k=k: (crossed(k) if i else side_copy(i, k)).wait_recv())
        for k in range(1, T):
            pl.when((at.t >= k) & ((at.c == 1) | (i == 1)))(lambda k=k: row_copy(i, k, True).wait_recv())

    def drain_rows(i):
        keep(i).wait()
        for k in range(1, T):
            pl.when(((at.c == 0) & (i == 0)) | (at.t + k < T))(lambda k=k: row_copy(i, k).wait_send())

        @pl.when(at.c == 0)
        def _():
            for k in range(T):
                (cross_copy(k) if i else side_copy(0, k)).wait_send()

    tiles = pl.num_programs(0) - LAG

    def when(i, *acts):
        @pl.when(step == i)
        def _():
            for act in acts:
                act()

    def open_():
        small[...] = jnp.zeros_like(small)
        for i, v in enumerate(small_in):
            small[i : i + 1, : v.shape[1]] = v[...].astype(F32)
        greet(at.peers())
        for p in (qo, sm):
            p.begin()
        cnt[...] = count_lanes(counts[...])
        cnt_out[...] = cnt[...]
        qo.spread()
        for p in (up, dn):
            p.begin()
        sm.spread()
        vec[...] = vectors(wholes[4])
        vec_out[...] = vec[...]
        qo.pass_on()
        qo.arrive()
        for p in (up, dn):
            p.spread()
        for p in (pj, wa, wb, wo):
            p.begin()

    def copy_out(*which):
        for i in which:
            out(i).start()

    groups = ROWS // GROUP

    def count_rows(i):
        return jnp.concatenate([cnt[pl.ds(i * groups + g, 1), :] for g in range(groups)], axis=0)

    def rows_of(i):
        r = chunk(i)
        start = words_in[r, :].astype(F32) + mm(pool[r, :], wholes[3][...])
        xown[r, :] = (ln_parts(start)[0] * vec[3:4, :]).astype(BF16)

    when(0, open_)
    when(6, *[p.spread for p in (pj, wa, wb, wo)])
    when(7, zu.begin, zd.begin)
    when(8, pj.pass_on, lambda: copy_out(0, 1, 2))
    when(9, lambda: send_rows(0))
    when(11, wa.pass_on, wb.pass_on, wo.pass_on, lambda: send_rows(1), lambda: copy_out(3))
    when(12, lambda: pass_rows(0), wa.arrive, wb.arrive, wo.arrive, lambda: copy_out(5, 6), zu.spread, zd.spread, lambda: copy_out(7, 8))

    @pl.when(step < tiles)
    def _():
        first = char_attn_tile(x[...], count_rows(step), (vec[0:1, :256], wholes[0][:, :768], wholes[0][:, 768:]))
        for ref, val in zip(outs[:4], first):
            ref[...] = val
        kept[lax.rem(step, LAG + 1)] = first[3]

    when(LAG, *[p.pass_on for p in (up, dn)], *[p.arrive for p in (up, dn)])

    @pl.when(step >= LAG)
    def _():
        i = step - LAG
        second = char_mlp_tile(kept[lax.rem(i, LAG + 1)], count_rows(i), (None, None, None, vec[1:2, :256], wholes[1][...], wholes[2][...].reshape(1024, 256), vec[2:3, :256]))
        for ref, val in zip(outs[4:], second):
            ref[...] = val
        pool[span(i * part, part), :] = second[3]

    when(3 + LAG, lambda: rows_of(0))
    when(5 + LAG, lambda: rows_of(1))

    @pl.when(step == last)
    def _():
        rows_of(2)
        keep(2).start()
        for p in pieces:
            p.drain()
        for i in (0, 1, 2, 3, 5, 6, 7, 8):
            out(i).wait()
        for i in range(2):
            take_rows(i)
            drain_rows(i)
        keep(2).wait()


def gather_forward(x, counts, words_in, small, shards):
    tiles = x.shape[0] // ROWS
    F, T = lax.axis_size("fsdp"), lax.axis_size("tp")
    any_ = pl.BlockSpec(memory_space=pl.ANY)
    count = PIECES * Piece.slots(F, T)
    words, width = words_in.shape
    nchunk = len(CHUNKS) * 2 * T

    def early(r, w):
        return pl.BlockSpec((r, w), lambda i: (jnp.minimum(i, tiles - 1), 0))

    def late(r, w):
        return pl.BlockSpec((r, w), lambda i: (jnp.maximum(i - LAG, 0), 0))

    return pl.pallas_call(
        gather_fwd_kernel,
        grid=(tiles + LAG,),
        in_specs=[early(ROWS, 256), full_spec(counts.shape), full_spec(words_in.shape)] + [full_spec(v.shape) for v in small] + [any_] * len(shards),
        out_specs=[early(r, w) for r, w, _ in FWD_OUTS[:4]] + [late(r, w) for r, w, _ in FWD_OUTS[4:]] + [any_] * len(GATHERED) + [full_spec((8, 512)), full_spec((x.shape[0] // GROUP, GROUP)), any_],
        out_shape=[jax.ShapeDtypeStruct((r * tiles, w), d) for r, w, d in FWD_OUTS]
        + [jax.ShapeDtypeStruct(sh, d) for sh, d in GATHERED]
        + [jax.ShapeDtypeStruct((8, 512), F32), jax.ShapeDtypeStruct((x.shape[0] // GROUP, GROUP), F32), jax.ShapeDtypeStruct((2 * T, words, width), BF16)],
        scratch_shapes=[pltpu.VMEM(sh, d) for sh, d in GATHERED]
        + [pltpu.VMEM((8, 512), F32), pltpu.VMEM((x.shape[0] // GROUP, GROUP), F32), pltpu.VMEM((words, width), BF16), pltpu.VMEM((words, 256), BF16), pltpu.VMEM((LAG + 1, ROWS, 256), F32), pltpu.VMEM((8, 128), F32)]
        + [pltpu.SemaphoreType.DMA((n,)) for n in (count, count, nchunk, nchunk, PIECES + len(GATHERED) + len(CHUNKS))],
        compiler_params=pltpu.CompilerParams(vmem_limit_bytes=VMEM_LIMIT, collective_id=0, has_side_effects=True, dimension_semantics=("arbitrary",)),
        name="gather_forward",
    )(x, counts, words_in, *small, *shards)


def word_kernel(
    pooled, proj, words_in, cot, vec, xin, w3_in, wo_in, zu, zd,
    block_out, rms, words_grad, gpool, d_proj, d_vec, h_w4, h_up, h_down,
    xall, kk, vv, kt, vt, ss, ee, qm, dom, mx, ll, ot, dqt, wkt, wvt, w3, wout, wup, wdown, dk_acc, dv_acc, dlt, dk_sum, dv_sum,
    dx_in, dx_own, g_up, g_down, g_w4, in_up, in_down, in_w4,
    xlast, w_send, w_recv, g_send, g_recv, rs_send, rs_recv, x_send, x_recv, local_sems,
):
    at = Place()
    T = at.T
    own = at.c * T + at.t
    nblk, blk, width = xall.shape
    dx = kk
    half = HEADS // 2
    low = pair_masks(blk)
    first, second = range(half), range(half, HEADS)
    cu = zu.shape[1]
    loads = [pltpu.make_async_copy(src, dst, local_sems.at[i]) for i, (src, dst) in enumerate(((w3_in, w3), (xin, xall), (wo_in, wout)))]
    for load in loads:
        load.start()

    near = (at.t + 1 - 2 * lax.rem(at.t, 2), lax.rem(at.t + 2, T))
    far = T - 1 - at.t

    def area(c, t, i, part=None):
        r = span(2 * cu * t + cu * c, cu)
        if part is None:
            return wup.at[:, r] if i == 0 else wdown.at[r, :]
        if i == 0:
            return wup.at[pl.ds(part * width // 2, width // 2), r]
        return wdown.at[span(2 * cu * t + cu * c + part * (cu // 2), cu // 2), :]

    def wide(n, i, incoming=False):
        dst = area(at.c, near[n] if incoming else at.t, i)
        return remote(dst if incoming else (zu, zd)[i], dst, (w_send, w_recv), 2 * n + i, {"tp": near[n]})

    def onward(n, i, incoming=False):
        dst = area(at.c, far if incoming else near[1 - n], i, n)
        return remote(dst, dst, (w_send, w_recv), 4 + 2 * n + i, {"tp": near[n]})

    def side(k, i, incoming=False):
        t = (at.t, near[0], near[1], far)[k]
        dst = area(1 - at.c if incoming else at.c, t, i)
        return remote((zu, zd)[i] if k == 0 and not incoming else dst, dst, (w_send, w_recv), 8 + 2 * k + i, {"ctx": 1 - at.c})

    def mine(i):
        return pltpu.make_async_copy((zu, zd)[i], area(at.c, at.t, i), local_sems.at[3 + i])

    plane = [{"ctx": i, "tp": at.tp(k)} for i in (at.c, 1 - at.c) for k in range(T) if k > 0] + [{"ctx": 1 - at.c}]
    call(plane)
    tail = xlast.shape[1]
    lead = blk - tail

    start = words_in[...].astype(F32) + mm(pooled[...], proj[...])
    shat, sr = ln_parts(start)
    g1v = vec[3:4, :]
    wq, wk, wv = w3.at[0], w3.at[1], w3.at[2]
    loads[0].wait()
    wkt[...] = jnp.transpose(wk[...])
    wvt[...] = jnp.transpose(wv[...])
    loads[1].wait()
    xown = xall[own]
    q = mm(xown, wq[...]).astype(BF16) * BF16(0.125)
    for p in range(HEADS // 2):
        a, b = split_heads(q[:, 128 * p : 128 * p + 128], low)
        qm[2 * p] = a
        qm[2 * p + 1] = b
    mx[...] = jnp.full(mx.shape, MASKED, F32)
    ll[...] = jnp.zeros(ll.shape, F32)
    ot[...] = jnp.zeros(ot.shape, F32)
    dqt[...] = jnp.zeros(dqt.shape, F32)
    dk_sum[...] = jnp.zeros(dk_sum.shape, F32)
    dv_sum[...] = jnp.zeros(dv_sum.shape, F32)

    def scores_of(j, heads):
        for h in heads:
            p = h // 2
            s = mm_nt(kk[j, :, 128 * p : 128 * p + 128], qm[h])
            ss[j, h % half] = s
            mx[h] = jnp.maximum(mx[h], jnp.max(s.reshape(blk // 8, 8, blk), axis=0))

    def mix_of(j, heads):
        for h in heads:
            e = jnp.exp(ss[j, h % half] - mx[h, 0:1, :])
            ll[h] += jnp.sum(e.reshape(blk // 8, 8, blk), axis=0)
            eb = e.astype(BF16)
            ee[j, h] = eb
            ot[64 * h : 64 * h + 64, :] += mm(vt[j, 64 * h : 64 * h + 64, :], eb)

    def top_of(heads):
        for h in heads:
            mx[h] = jnp.broadcast_to(jnp.max(mx[h], axis=0, keepdims=True), (8, blk))

    meet(plane)

    def got_rows(j, sem):
        pltpu.make_async_remote_copy(
            src_ref=xlast.at[j], dst_ref=xlast.at[j], send_sem=x_send.at[0], recv_sem=x_recv.at[sem],
            device_id={"ctx": 1 - at.c}, device_id_type=MESH,
        ).wait_recv()
        xall[j, lead:, :] = xlast[j]

    for k in range(T):

        @pl.when((at.c == 0) & (at.t + k < T) & (k > 0))
        def _():
            if k:
                remote(xin.at[own, pl.ds(lead, tail)], xlast.at[own], (x_send.at[2 * k], x_recv.at[2 * k]), None, {"ctx": 0, "tp": at.tp(k)}).start()

        @pl.when((at.c == 0) | ((at.t + k < T) & (k > 0)))
        def _():
            remote(xin.at[own, pl.ds(lead, tail)], xlast.at[own], (x_send.at[2 * k + 1], x_recv.at[2 * k + 1 + 2 * T * at.c]), None, {"ctx": 1, "tp": at.tp(k)}).start()


    def others():
        for k in range(T):
            pl.when((at.c == 0) & (at.t >= k) & (k > 0))(lambda k=k: got_rows(at.t - k, 2 * k))
            pl.when(at.c == 1)(lambda k=k: got_rows(at.tp(-k), 2 * k + 1))
            pl.when((at.c == 1) & (at.t >= k) & (k > 0))(lambda k=k: got_rows(T + at.t - k, 2 * k + 1 + 2 * T))
        for i in range(2):
            for n in range(2):
                wide(n, i).start()
            side(0, i).start()
            mine(i).start()

    pl.when(own == 0)(others)

    @pl.loop(0, own + 1)
    def _(m):
        pl.when(m == 1)(others)
        j = own - m
        xj = xall[j]
        kk[j] = mm(xj, wk[...]).astype(BF16)
        vv[j] = mm(xj, wv[...]).astype(BF16)
        kt[j] = mm_nt(wkt[...], xj).astype(BF16)
        vt[j] = mm_nt(wvt[...], xj).astype(BF16)
        scores_of(j, first)

    top_of(first)

    @pl.loop(0, own + 1)
    def _(j):
        mix_of(j, first)
        scores_of(j, second)

    top_of(second)
    for i in range(2):
        for n in range(2):
            wide(n, i, True).wait_recv()
        for n in range(2):
            onward(n, i).start()
            side(1 + n, i).start()

    @pl.loop(0, own + 1)
    def _(j):
        mix_of(j, second)

    for h in range(HEADS):
        linv = 1.0 / jnp.sum(ll[h], axis=0, keepdims=True)
        ll[h] = jnp.broadcast_to(linv, (8, blk))
        ot[64 * h : 64 * h + 64, :] = ot[64 * h : 64 * h + 64, :] * linv
    mixed_t = ot[...].astype(BF16)
    mixed = jnp.transpose(mixed_t)
    loads[2].wait()
    attn = mm(mixed, wout[...])
    awa = start + attn
    ahat, ar = ln_parts(awa)
    g2v = vec[4:5, :]
    n2 = (ahat * g2v).astype(BF16)
    for i in range(2):
        for n in range(2):
            onward(n, i, True).wait_recv()
        side(3, i).start()
    for i in range(2):
        mine(i).wait()
        for k in range(4):
            side(k, i, True).wait_recv()
    upper, dgelu = gelu_both(mm(n2, wup[...]))
    upper = upper.astype(BF16)
    mlp = mm(upper, wdown[...])
    final = awa + mlp
    block_out[...] = final.astype(BF16)
    lane = lax.broadcasted_iota(jnp.int32, (blk, 128), 1)
    cols = [jnp.sqrt(jnp.mean(v * v, axis=-1, keepdims=True)) for v in (attn, mlp, final)]
    rms[...] = jnp.transpose(jnp.where(lane == 0, cols[0], jnp.where(lane == 1, cols[1], cols[2])))[0:3, :]
    cotv = cot[...]
    gdown = mm_tn(upper, cotv).astype(BF16)
    ghid = (dgelu * mm_nt(cotv, wdown[...])).astype(BF16)
    gup = mm_tn(n2, ghid).astype(BF16)
    for c in range(2):
        for t in range(T):
            g_down[c, cu * t : cu * t + cu, :] = gdown[cu * (2 * t + c) : cu * (2 * t + c) + cu, :]
            g_up[c, :, cu * t : cu * t + cu] = gup[:, cu * (2 * t + c) : cu * (2 * t + c) + cu]
    grads = ((g_down, in_down, h_down), (g_up, in_up, h_up), (g_w4, in_w4, h_w4))

    def swap(i):
        return remote(grads[i][0].at[1 - at.c], grads[i][1], (g_send, g_recv), i, {"ctx": 1 - at.c})

    def store(i):
        return pltpu.make_async_copy(grads[i][0].at[at.c], grads[i][2], local_sems.at[5 + i])

    def add_halves(i):
        g, other, _ = grads[i]
        swap(i).wait_recv()
        g[at.c] = (g[at.c].astype(F32) + other[...].astype(F32)).astype(BF16)
        store(i).start()

    gn2 = mm_nt(ghid, wup[...])
    d_g2 = jnp.sum(gn2 * ahat, axis=0, keepdims=True)
    ga = cotv.astype(F32) + ln_back(ahat, ar, g2v, gn2)
    gal = ga.astype(BF16)
    g_w4[1, 1] = mm_tn(gal, mixed).astype(BF16)
    swap(0).start()
    swap(1).start()
    do_t = mm_nt(wout[...], gal).astype(BF16)
    do_s = []
    for h in range(HEADS):
        r = slice(64 * h, 64 * h + 64)
        d = do_t[r, :].astype(F32)
        linv = ll[h, 0:1, :]
        dlt[h] = jnp.broadcast_to(jnp.sum(d * ot[r, :], axis=0, keepdims=True) * linv, (8, blk))
        do_s.append((d * linv).astype(BF16))
    do = jnp.transpose(jnp.concatenate(do_s, axis=0))
    for p in range(HEADS // 2):
        a, b = split_heads(do[:, 128 * p : 128 * p + 128], low)
        dom[2 * p] = a
        dom[2 * p + 1] = b

    add_halves(0)
    add_halves(1)

    def grad_copy(j):
        return remote(dx.at[j], dx_in.at[own], (rs_send.at[j], rs_recv.at[own]), None, {"ctx": j // T, "tp": lax.rem(j, T)})

    @pl.loop(0, own + 1)
    def _(j):
        @pl.when(j > 0)
        def _():
            grad_copy(j - 1).start()

        for p in range(HEADS // 2):
            c = slice(128 * p, 128 * p + 128)
            vp = vv[j, :, c]
            dk = None
            for h in (2 * p, 2 * p + 1):
                e = ee[j, h]
                dp = mm_nt(vp, dom[h])
                ds = (e.astype(F32) * (dp - dlt[h, 0:1, :])).astype(BF16)
                dvh = mm(e, dom[h])
                dkh = mm(ds, qm[h])
                dk, dv = (dkh, dvh) if dk is None else (dk + dkh, dv + dvh)
                dqt[64 * h : 64 * h + 64, :] += mm(kt[j, 64 * h : 64 * h + 64, :], ds)
            dk_acc[:, c] = dk.astype(BF16)
            dv_acc[:, c] = dv.astype(BF16)
        dk = dk_acc[...]
        dv = dv_acc[...]
        dxj = mm_nt(dk, wk[...]) + mm_nt(dv, wv[...])
        dx[j] = dxj.astype(BF16)
        dx_own[...] = dxj
        xt = jnp.transpose(xall[j])
        dk_sum[...] += mm(xt, dk)
        dv_sum[...] += mm(xt, dv)

    dq = jnp.transpose((dqt[...] * 0.125).astype(BF16))
    g_w4[0, 0] = mm_tn(xown, dq).astype(BF16)
    g_w4[0, 1] = dk_sum[...].astype(BF16)
    g_w4[1, 0] = dv_sum[...].astype(BF16)
    swap(2).start()
    dx_own[...] += mm_nt(dq, wq[...])

    @pl.loop(own + 1, nblk)
    def _(b):
        remote(dx.at[own], dx_in.at[b], (rs_send.at[b], rs_recv.at[b]), None, {"ctx": 1 - at.c}).wait_recv()
        dx_own[...] += dx_in[b].astype(F32)

    gnf = dx_own[...]
    grad = ga + ln_back(shat, sr, g1v, gnf)
    words_grad[...] = grad
    d_vec[...] = jnp.concatenate([jnp.sum(gnf * shat, axis=0, keepdims=True), d_g2, jnp.zeros((6, width), F32)], axis=0)
    gproj = grad.astype(BF16)
    gproj_w = mm_tn(pooled[...], gproj).astype(BF16)
    hr = gproj_w.shape[0] // (2 * at.F)
    for i in range(at.F):
        for c in range(2):
            d_proj[c, hr * i : hr * i + hr, :] = gproj_w[hr * (2 * i + c) : hr * (2 * i + c) + hr, :]
    gpool[...] = mm_nt(gproj, proj[...])

    add_halves(2)
    for k in range(T):
        pl.when((at.c == 0) & (at.t + k < T) & (k > 0))(lambda k=k: remote(xin.at[own, pl.ds(lead, tail)], xlast.at[own], (x_send.at[2 * k], x_recv.at[2 * k]), None, {"ctx": 0, "tp": at.tp(k)}).wait_send() if k else None)
        pl.when((at.c == 0) | ((at.t + k < T) & (k > 0)))(lambda k=k: remote(xin.at[own, pl.ds(lead, tail)], xlast.at[own], (x_send.at[2 * k + 1], x_recv.at[2 * k + 1]), None, {"ctx": 1 - at.c}).wait_send())
    for i in range(2):
        for n in range(2):
            wide(n, i).wait_send()
            onward(n, i).wait_send()
        for k in range(4):
            side(k, i).wait_send()
    for i in range(3):
        swap(i).wait_send()
        store(i).wait()

    @pl.loop(0, own)
    def _(j):
        grad_copy(j).wait_send()


def word_section(pooled, proj, words_in, cot, vec, xall, w3, wo, zu, zd):
    blk, width = words_in.shape
    T = lax.axis_size("tp")
    nblk = 2 * T
    cu = zu.shape[1]
    ff = 2 * T * cu
    vm = pl.BlockSpec(memory_space=pltpu.VMEM)
    any_ = pl.BlockSpec(memory_space=pl.ANY)
    out_shapes = [((blk, width), BF16), ((3, blk), F32), ((blk, width), F32), ((blk, pooled.shape[1]), F32), ((2, proj.shape[0] // 2, width), BF16), ((8, width), F32)]
    halves = [((2, width, width), BF16), ((width, ff // 2), BF16), ((ff // 2, width), BF16)]
    bufs = [
        ((nblk, blk, width), BF16), ((nblk, blk, width), BF16), ((nblk, blk, width), BF16), ((nblk, width, blk), BF16), ((nblk, width, blk), BF16),
        ((nblk, HEADS // 2, blk, blk), F32), ((nblk, HEADS, blk, blk), BF16), ((HEADS, blk, 128), BF16), ((HEADS, blk, 128), BF16),
        ((HEADS, 8, blk), F32), ((HEADS, 8, blk), F32), ((width, blk), F32), ((width, blk), F32), ((width, width), BF16), ((width, width), BF16),
        ((3, width, width), BF16), ((width, width), BF16), ((width, ff), BF16), ((ff, width), BF16), ((blk, width), BF16), ((blk, width), BF16), ((HEADS, 8, blk), F32),
        ((width, width), F32), ((width, width), F32), ((nblk, blk, width), BF16), ((blk, width), F32),
        ((2, width, ff // 2), BF16), ((2, ff // 2, width), BF16), ((2, 2, width, width), BF16), ((width, ff // 2), BF16), ((ff // 2, width), BF16), ((2, width, width), BF16),
    ]
    nw = 16
    rows = (CHUNKS[-1][1] - CHUNKS[-1][0]) * (ROWS // 16)
    return pl.pallas_call(
        word_kernel,
        in_specs=[vm] * 5 + [any_] * 5,
        out_specs=[vm] * len(out_shapes) + [any_] * len(halves),
        out_shape=[jax.ShapeDtypeStruct(s, d) for s, d in out_shapes + halves],
        scratch_shapes=[pltpu.VMEM(s, d) for s, d in bufs] + [pltpu.VMEM((nblk, rows, width), BF16)] + [pltpu.SemaphoreType.DMA((n,)) for n in (nw, nw, 3, 3, nblk, nblk, 2 * T, 4 * T, 8)],
        compiler_params=pltpu.CompilerParams(vmem_limit_bytes=VMEM_LIMIT, collective_id=1, has_side_effects=True),
        name="word_section",
    )(pooled, proj, words_in, cot, vec, xall, w3, wo, zu, zd)


class Sum:
    def __init__(self, at, source, bufs, tp_cut, fs_cut, sems, first, wide, halved):
        self.at, self.source, self.sems, self.first, self.wide, self.halved = at, source, sems, first, wide, halved
        self.own, self.away, self.got, self.blocks, self.block, self.pieces, self.done = bufs
        self.hold, self.came = self.away, self.got
        self.near = (at.t + 1 - 2 * lax.rem(at.t, 2), lax.rem(at.t + 2, at.T))
        self.far = at.T - 1 - at.t
        self.fs_base = 5 if halved else at.T - 1
        self.tp_cut, self.fs_cut = tp_cut, fs_cut

    @staticmethod
    def slots(F, T):
        return 6 + (F - 1) + 2 * T

    @staticmethod
    def buffers(half, block, piece, F, T, wide, halved):
        quarter = (block[0] // 2,) + block[1:]
        first = [block, (4,) + quarter, (6,) + quarter, (1, 8, 128)] if halved else [half, half, half, (T - 1,) + block]
        shapes = first + [block, (F - 1,) + piece, ((2, T) if wide else (2,)) + piece]
        return [pltpu.VMEM(sh, BF16) for sh in shapes]

    def swap(self):
        at = self.at
        return remote(self.away, self.got, self.sems, self.first, {"ctx": 1 - at.c})

    def to_tp(self, k):
        src = self.source if self.halved else self.own
        return remote(src.at[self.tp_cut(self.at.tp(k))], self.blocks.at[k - 1], self.sems, self.first + k, {"tp": self.at.tp(k)})

    def to_fs(self, k):
        return remote(self.block.at[self.fs_cut(self.at.fs(k))], self.pieces.at[k - 1], self.sems, self.first + self.fs_base + k, {"fsdp": self.at.fs(k)})

    def share(self, k, x, incoming=False):
        at = self.at
        there = 1 - at.c if x else at.c
        c = there if incoming else at.c
        r = self.done.at[c, at.tp(-k) if incoming else at.t] if self.wide else self.done.at[c]
        return remote(r, r, self.sems, self.first + self.fs_base + at.F + 2 * k + x, {"ctx": there, "tp": at.tp(k)} if k else {"ctx": there})

    def shares(self):
        if not self.wide:
            return [(0, 1)]
        return [(k, x) for k in range(self.at.T) for x in range(2) if k or x]

    def local(self, i):
        src = self.source.at[self.at.c if i == 0 else 1 - self.at.c]
        return pltpu.make_async_copy(src, self.own if i == 0 else self.away, self.loc.at[i])

    def fetch(self, loc):
        self.loc = loc
        for i in range(2):
            self.local(i).start()

    def begin_fetched(self):
        for i in range(2):
            self.local(i).wait()
        self.swap().start()

    def begin(self):
        self.own[...] = self.source[self.at.c].astype(BF16)
        self.away[...] = self.source[1 - self.at.c].astype(BF16)
        self.swap().start()

    def halves(self):
        self.swap().wait_recv()
        self.own[...] = (self.own[...].astype(F32) + self.got[...].astype(F32)).astype(BF16)
        for k in range(1, self.at.T):
            self.to_tp(k).start()

    def part(self, t, i):
        cut = list(self.tp_cut(t))
        n = self.own.shape[0] // 2
        if cut[0] == ALL:
            cut[0] = pl.ds(i * n, n)
        else:
            cut[0] = span(t * 2 * n + i * n, n)
        return self.source.at[tuple(cut)]

    def mine(self, i):
        t, j = ((self.at.t, 0), (self.at.t, 1), (self.near[1], 0), (self.near[0], 1))[i]
        return pltpu.make_async_copy(self.part(t, j), self.hold.at[i], self.loc.at[i])

    def near_send(self, n, far):
        at = self.at
        src = self.part(self.far if far else self.near[n], n)
        return remote(src, self.came.at[2 * n + far], self.sems, self.first + 2 * n + far, {"tp": self.near[n]})

    def onward(self, n):
        return remote(self.hold.at[2 + n], self.came.at[4 + n], self.sems, self.first + 4 + n, {"tp": self.near[1 - n]})

    def begin_halved(self):
        for i in range(4):
            self.mine(i).start()
        for n in range(2):
            for far in (1, 0):
                self.near_send(n, far).start()

    def pass_halved(self):
        for i in range(4):
            self.mine(i).wait()
        for n in range(2):
            self.near_send(n, 1).wait_recv()
            self.hold[2 + n] = (self.hold[2 + n].astype(F32) + self.came[2 * n + 1].astype(F32)).astype(BF16)
        for n in range(2):
            self.onward(n).start()

    def over_near(self):
        n = self.own.shape[0] // 2
        for i in range(2):
            self.near_send(i, 0).wait_recv()
            self.onward(i).wait_recv()
            total = self.hold[i].astype(F32) + self.came[2 * i].astype(F32) + self.came[4 + i].astype(F32)
            self.block[i * n : i * n + n] = total.astype(BF16)
        for k in range(1, self.at.F):
            self.to_fs(k).start()

    def over_tp(self):
        total = self.own[self.tp_cut(self.at.t)].astype(F32)
        for k in range(1, self.at.T):
            self.to_tp(k).wait_recv()
            total += self.blocks[k - 1].astype(F32)
        self.block[...] = total.astype(BF16)
        for k in range(1, self.at.F):
            self.to_fs(k).start()

    def over_fsdp(self):
        at = self.at
        total = self.block[self.fs_cut(at.f)].astype(F32)
        for k in range(1, at.F):
            self.to_fs(k).wait_recv()
            total += self.pieces[k - 1].astype(F32)
        if self.wide:
            self.done[at.c, at.t] = total.astype(BF16)
        else:
            self.done[at.c] = total.astype(BF16)
        for k, x in self.shares():
            self.share(k, x).start()

    def finish(self):
        for k, x in self.shares():
            self.share(k, x, True).wait_recv()

    def drain(self):
        at = self.at
        if self.halved:
            for n in range(2):
                for far in range(2):
                    self.near_send(n, far).wait_send()
                self.onward(n).wait_send()
        else:
            self.swap().wait_send()
            for k in range(1, at.T):
                self.to_tp(k).wait_send()
        for k in range(1, at.F):
            self.to_fs(k).wait_send()
        for k, x in self.shares():
            self.share(k, x).wait_send()


SUMS = [
    ((2, 512, 512), (2, 512, 128), (2, 128, 128), 2, 1, False, True),
    ((512, 1024), (512, 256), (128, 256), 1, 0, False, True),
    ((1024, 512), (256, 512), (256, 128), 0, 1, False, True),
    ((128, 512), (128, 128), (32, 128), 1, 0, True, False),
    ((256, 512), (256, 128), (64, 128), 1, 0, True, False),
    ((128, 1024), (32, 1024), (32, 256), 0, 1, True, False),
    ((256, 512), (256, 128), (64, 128), 1, 0, True, False),
]


def cutter(shape, axis, size):
    def cut(i):
        return tuple(span(i * size, size) if d == axis else ALL for d in range(len(shape)))

    return cut


def reduce_bwd_kernel(tiles, *refs):
    refs = list(refs)
    take = lambda n: [refs.pop(0) for _ in range(n)]
    ins = take(14)
    sources = take(4)
    (d_vec,) = take(1)
    (cg,) = take(1)
    results = take(len(SUMS))
    (vec_out,) = take(1)
    (gca,) = take(1)
    accs = take(len(ACCS))
    at = Place()
    bufs = [take(7) for _ in SUMS]
    vec_in, send, recv, vsend, vrecv, local_sems = refs
    slots = Sum.slots(at.F, at.T)
    a_qo, a_up, a_dn, a_vec = accs
    origin = list(sources) + [a_up, a_dn, a_qo]
    sums = []
    for i, (half, block, piece, ta, fa, wide, halved) in enumerate(SUMS):
        sums.append(Sum(at, origin[i], bufs[i], cutter(half, ta, block[ta]), cutter(block, fa, piece[fa]), (send, recv), i * slots, wide, halved))
        sums[i].loc = local_sems.at[i]
    w4, wup, wdn, pj, up, dn, qo = sums
    step = pl.program_id(0)
    last = 2 * tiles - 1

    def when(i, *acts):
        @pl.when(step == i)
        def _():
            for act in acts:
                act()

    def open_():
        meet(at.peers())
        w4.begin_halved()
        wup.begin_halved()
        pj.begin_fetched()

    when(0, lambda: call(at.peers()), lambda: pj.fetch(pj.loc))
    when(1, open_)
    when(3, pj.halves)
    when(6, w4.pass_halved, wup.pass_halved, wdn.begin_halved)
    when(8, up.begin, dn.begin, pj.over_tp)
    when(11, w4.over_near, wup.over_near, wdn.pass_halved, up.halves, dn.halves, pj.over_fsdp)
    when(15, wdn.over_near, up.over_tp, dn.over_tp)
    def vec_copy(i, where):
        return remote(a_vec, vec_in.at[i], (vsend, vrecv), i, where)

    def vec_begin():
        a_vec[3:5, :] = d_vec[0:2, :]
        vec_copy(0, {"ctx": 1 - at.c}).start()

    def vec_plane():
        vec_copy(0, {"ctx": 1 - at.c}).wait()
        a_vec[...] += vec_in[0]
        for k in range(1, at.T):
            vec_copy(k, {"tp": at.tp(k)}).start()

    def vec_depth():
        for k in range(1, at.T):
            vec_copy(k, {"tp": at.tp(k)}).wait()
        a_vec[...] += vec_in[1] + vec_in[2] + vec_in[3]
        for k in range(1, at.F):
            vec_copy(at.T - 1 + k, {"fsdp": at.fs(k)}).start()

    def vec_end():
        for k in range(1, at.F):
            vec_copy(at.T - 1 + k, {"fsdp": at.fs(k)}).wait()
        total = a_vec[...] + (vec_in[4] + vec_in[5] + vec_in[6])
        rows = [jnp.zeros((2, 128), F32)]
        for i, n in ((2, 64), (3, 128), (4, 128)):
            v = jnp.zeros((1, n), F32)
            for f in range(at.F):
                v = jnp.where(at.f == f, total[i : i + 1, f * n : f * n + n], v)
            rows.append(v if n == 128 else jnp.concatenate([v, jnp.zeros((1, n), F32)], axis=1))
        vec_out[...] = jnp.concatenate(rows + [jnp.zeros((3, 128), F32)], axis=0)

    when(8, vec_begin)
    when(10, vec_plane)
    when(12, vec_depth)
    when(14, vec_end)
    char_back_step(step, tiles, ins, cg, gca, accs, False)

    @pl.when(step == last)
    def _():
        qo.begin()
        w4.over_fsdp()
        wup.over_fsdp()
        qo.halves()

        def keep(*which):
            for i in which:
                sums[i].finish()
                results[i][...] = sums[i].done[...]

        keep(0, 1, 3)
        qo.over_tp()
        up.over_fsdp()
        dn.over_fsdp()
        wdn.over_fsdp()
        qo.over_fsdp()
        keep(4, 5, 2)
        for s in sums[:6]:
            s.drain()
        keep(6)
        qo.drain()


def reduce_backward(x, cnt, saved, gpool, weights, sources, d_vec):
    total = x.shape[0]
    tiles = total // ROWS
    F, T = lax.axis_size("fsdp"), lax.axis_size("tp")
    ins, out = back_specs(tiles, gpool, weights)
    any_ = pl.BlockSpec(memory_space=pl.ANY)
    scratch = [pltpu.VMEM((total, 256), F32)] + [pltpu.VMEM(s, F32) for s in ACCS]
    results = []
    for half, block, piece, _, _, wide, halved in SUMS:
        scratch += Sum.buffers(half, block, piece, F, T, wide, halved)
        results.append(((2, T) if wide else (2,)) + piece)
    count = len(SUMS) * Sum.slots(F, T)
    vecs = 1 + (T - 1) + (F - 1)
    scratch += [pltpu.VMEM((vecs, 8, 512), F32)]
    scratch += [pltpu.SemaphoreType.DMA((n,)) for n in (count, count, vecs, vecs)] + [pltpu.SemaphoreType.DMA((len(SUMS), 4))]
    return pl.pallas_call(
        functools.partial(reduce_bwd_kernel, tiles),
        grid=(2 * tiles,),
        in_specs=ins + [any_] * len(sources) + [full_spec((8, 512))],
        out_specs=[out] + [full_spec(s) for s in results] + [full_spec((8, 128))],
        out_shape=[jax.ShapeDtypeStruct((total, 256), F32)] + [jax.ShapeDtypeStruct(s, BF16) for s in results] + [jax.ShapeDtypeStruct((8, 128), F32)],
        scratch_shapes=scratch,
        compiler_params=pltpu.CompilerParams(vmem_limit_bytes=VMEM_LIMIT, collective_id=2, has_side_effects=True, dimension_semantics=("arbitrary",)),
        name="reduce_backward",
    )(x, cnt, *saved, gpool, *weights, *sources, d_vec)


FINAL = [(3, 128, 128), (128, 128), (128, 512), (512, 128), (64, 512), (64, 1024), (256, 256), (64, 768), (64, 256), (1, 64), (1, 64), (1, 64), (1, 128), (1, 128)]


def final_kernel(cg, block, grad, rms, w4, wup, wdn, pj, up, dn, qo, vec, w_qkv, w_up, g1, g2, cg_out, block_out, grad_out, rms_out, *outs):
    cg_out[...] = cg[...]

    @pl.when(pl.program_id(0) == 0)
    def _():
        block_out[...] = block[...]
        grad_out[...] = grad[...]
        rms_out[...] = rms[...]
        o3, o_out, o_wup, o_wdn, o_pj, o_up, o_dn, o_qkv, o_cout = outs[:9]
        o3[0] = w4[0, 0].astype(F32)
        o3[1] = w4[0, 1].astype(F32)
        o3[2] = w4[1, 0].astype(F32)
        o_out[...] = jnp.transpose(w4[1, 1].astype(F32))
        for c in range(2):
            o_wup[:, 256 * c : 256 * c + 256] = wup[c].astype(F32)
            o_wdn[256 * c : 256 * c + 256, :] = wdn[c].astype(F32)
            for t in range(pj.shape[1]):
                i = 2 * t + c
                o_pj[32 * c : 32 * c + 32, 128 * t : 128 * t + 128] = pj[c, t].astype(F32)
                o_up[:, 128 * i : 128 * i + 128] = up[c, t].astype(F32)
                ref, i = (o_qkv, i) if i < 6 else (o_cout, i - 6)
                ref[:, 128 * i : 128 * i + 128] = qo[c, t].astype(F32)
        o_dn[...] = jnp.transpose(dn[...].astype(F32).reshape(256, 256))
        for i, n in enumerate((64, 64, 64, 128, 128)):
            if i > 1:
                outs[9 + i][...] = vec[i : i + 1, :n]
        for i, (w, d, gain) in enumerate(((w_qkv, o_qkv, g1), (w_up, o_up, g2))):
            col = jnp.sum(w[...].astype(F32) * d[...], axis=-1, keepdims=True)
            row = jnp.transpose(jnp.broadcast_to(col, (64, 128)))[0:1, :]
            outs[9 + i][...] = row / gain[...].astype(F32)


def finish(cg, block, grad, rms, parts):
    tiles = 4
    rows = cg.shape[0] // tiles
    small = [block, grad, rms] + list(parts)
    return pl.pallas_call(
        final_kernel,
        grid=(tiles,),
        in_specs=[rows_spec(rows, cg.shape[1])] + [full_spec(v.shape) for v in small],
        out_specs=[rows_spec(rows, cg.shape[1])] + [full_spec(v.shape) for v in small[:3]] + [full_spec(v) for v in FINAL],
        out_shape=[jax.ShapeDtypeStruct(v.shape, v.dtype) for v in [cg] + small[:3]] + [jax.ShapeDtypeStruct(v, F32) for v in FINAL],
        compiler_params=pltpu.CompilerParams(vmem_limit_bytes=VMEM_LIMIT, dimension_semantics=("arbitrary",)),
        name="finish",
    )(cg, block, grad, rms, *parts)


def gather(x, name, axis):
    return lax.all_gather(x, name, axis=axis, tiled=True)


def scatter(x, name, axis):
    return lax.psum_scatter(x, name, scatter_dimension=axis, tiled=True)


def fits(rows):
    return lax.axis_size("fsdp") == 4 and lax.axis_size("tp") == 4 and rows == 64


def local(characters, counts, words_in, cotangent, char_prenorm, char_qkv, char_out, char_midnorm, char_up, char_down,
          pool_query, char_proj, word_prenorm, word_qkv, word_out, word_midnorm, word_up, word_down):
    words, slots, cdim = characters.shape
    x = characters.reshape(words * slots, cdim)
    vectors_in = (char_prenorm, char_midnorm, pool_query, word_prenorm, word_midnorm)
    w3 = jnp.moveaxis(word_qkv, 1, 0)
    direct = fits(char_prenorm.shape[0])
    group_rows = (words * slots // ROWS, ROWS // GROUP, GROUP)
    if direct:
        shards = [char_qkv, char_out, char_up, char_down, char_proj, w3, word_out, word_up, word_down]
        *saved, pooled_low, qo, up, dn, proj, _, w3, wo, zu, zd, vec, cnt, xall = gather_forward(x, counts.reshape(words // 128, 128), words_in, [v.reshape(1, -1) for v in vectors_in], shards)
        dn = dn.reshape(1024, 256)
        cnt = cnt.reshape(group_rows)
    else:
        cnt = jnp.repeat(counts.astype(F32), slots).reshape(group_rows)
        wide = [gather(v.astype(F32), "fsdp", 0) for v in vectors_in]
        vec = jnp.stack([jnp.pad(v, (0, 512 - v.shape[0])) for v in wide] + [jnp.zeros((512,), F32)] * 3)
        qo = jnp.concatenate([gather(char_qkv, "fsdp", 0), gather(char_out, "fsdp", 0)], axis=1)
        up, dn, proj = (gather(w, "fsdp", 0) for w in (char_up, char_down, char_proj))
        w3 = gather(gather(w3, "fsdp", 1), "tp", 2)
        wo = gather(gather(word_out, "fsdp", 1), "tp", 0)
        cu = word_up.shape[1] // 2
        zu = lax.dynamic_slice_in_dim(gather(word_up, "fsdp", 0), lax.axis_index("ctx") * cu, cu, 1)
        zd = lax.dynamic_slice_in_dim(gather(word_down, "fsdp", 1), lax.axis_index("ctx") * cu, cu, 0)
        *saved, pooled_low = char_forward(x, cnt, vec, qo, up, dn)
        start, _ = ln_parts(words_in.astype(F32) + mm(pooled_low, proj))
        xall = gather((start * vec[3:4]).astype(BF16), ("ctx", "tp"), 0).reshape(-1, words, words_in.shape[1])
    (block_out, rms, words_grad, gpool, d_proj, d_vec, h_w4, h_up, h_down) = word_section(pooled_low, proj, words_in, cotangent, vec, xall, w3, wo, zu, zd)
    if direct:
        cg, *parts = reduce_backward(x, cnt, saved, gpool, [vec, qo, up, dn], [h_w4, h_up, h_down, d_proj], d_vec)
        cg, block_out, words_grad, rms, g_qkv4, g_wout, g_wup, g_wdown, g_proj, g_up, g_down, g_qkv, g_out, *vecs = finish(cg, block_out, words_grad, rms, parts + [char_qkv, char_up, char_prenorm.reshape(1, -1), char_midnorm.reshape(1, -1)])
        vecs = [v.reshape(-1) for v in vecs]
    else:
        cg, a_qo, a_up, a_dn, a_vec = char_backward(x, cnt, saved, gpool, vec, qo, up, dn)

        def reduce_char(g):
            g = lax.psum(g.astype(BF16), ("ctx", "tp"))
            return scatter(g, "fsdp", 0).astype(F32)

        def reduce_word(g, tp_axis, fsdp_axis, ctx_axis):
            g = scatter(scatter(g, "tp", tp_axis), "fsdp", fsdp_axis)
            return gather(g, "ctx", ctx_axis).astype(F32)

        lanes = lambda g, n: jnp.moveaxis(g.reshape(2, g.shape[1], -1, n), 0, 2).reshape(g.shape[1], -1)
        hr = char_proj.shape[0] // 2
        g_qo = reduce_char(lanes(a_qo, 128))
        g_qkv, g_out = g_qo[:, :768], g_qo[:, 768:]
        g_up = reduce_char(lanes(a_up, 128))
        g_down = reduce_char(a_dn.reshape(256, 1024).T)
        g_proj = reduce_char(jnp.moveaxis(d_proj.reshape(2, -1, hr, 512), 0, 1).reshape(256, 512))
        g_w4 = reduce_word(h_w4, 2, 1, 0)
        g_qkv4, g_wout = g_w4[:3], g_w4[3].T
        g_wup = reduce_word(h_up, 1, 0, 1)
        g_wdown = reduce_word(h_down, 0, 1, 0)
        vecs = [reduce_char(v) for v in (a_vec[0, :256], a_vec[1, :256], a_vec[2, :256], d_vec[0], d_vec[1])]
    return (
        block_out,
        cg.reshape(words, slots, cdim),
        words_grad,
        rms,
        vecs[0],
        g_qkv,
        g_out,
        vecs[1],
        g_up,
        g_down,
        vecs[2],
        g_proj,
        vecs[3],
        jnp.moveaxis(g_qkv4, 0, 1),
        g_wout,
        vecs[4],
        g_wup,
        g_wdown,
    )


def solution(mesh):
    rows = ("fsdp", "ctx", "tp")
    v, m = P("fsdp"), P("fsdp", None)
    return jax.shard_map(
        local,
        mesh=mesh,
        in_specs=(
            P(rows, None, None), P(rows), P(rows, None), P(rows, None),
            v, m, m, v, m, m, v, m, v, P("fsdp", None, "tp"), P("tp", "fsdp"), v, P("fsdp", "tp"), P("tp", "fsdp"),
        ),
        out_specs=(
            P(rows, None), P(rows, None, None), P(rows, None), P(None, rows),
            v, m, m, v, m, m, v, m, v, P("fsdp", None, "tp"), P("tp", "fsdp"), v, P("fsdp", "tp"), P("tp", "fsdp"),
        ),
        check_vma=False,
    )
```

time: 231 us -> 197 us (0.85)
  local copies, waits for them, and re-layouts: 17.9 us -> 0 us
  Pallas kernels: 206 us -> 196 us
  other arithmetic: 5.84 us -> 0 us
    pallas_call x1, Pallas kernels: 87.3 us -> 73.1 us  [reduce_backward(): pl.pallas_call(functools.partial(reduce_bwd_kernel, tiles), grid=(2 * til...]
    unnamed x38 -> x0, local copies, waits for them, and re-layouts: 13.8 us -> none
    pallas_call x2 -> x3, Pallas kernels: 118 us -> 123 us  [the longest x1 60.7 us: word_section(): pl.pallas_call(word_kernel, in_specs=[vm] * 5 + [any_] * 5, out_specs=[vm...]
    concatenate x2 -> x0, other arithmetic: 3.15 us -> none  [the longest x1 1.58 us: local(): qo = jnp.concatenate([char_qkv, char_out], axis=1)]
    squeeze x2 -> x0, local copies, waits for them, and re-layouts: 2.57 us -> none  [local(): g_vec[i, :n]]
where the time goes in v4:
time: 197 us
  Pallas kernels  196 us (99%)
    pallas_call x1, Pallas kernels, reduce_backward(): pl.pallas_call(functools.partial(reduce_bwd_kernel, tiles), grid=(2 * til...  73.1 us
    pallas_call x1, Pallas kernels, word_section(): pl.pallas_call(word_kernel, in_specs=[vm] * 5 + [any_] * 5, out_specs=[vm...  60.7 us
    pallas_call x1, Pallas kernels, gather_forward(): pl.pallas_call(gather_fwd_kernel, grid=(tiles + LAG,), in_specs=[early(RO...  55.5 us
    pallas_call x1, Pallas kernels, finish(): pl.pallas_call(final_kernel, grid=(tiles,), in_specs=[rows_spec(rows, cg....  6.41 us

profile of v4, /device:TPU:0, one launch (start us, length us, event | category | flops | bytes accessed | tf_op | source)
XLA Modules:
  0.0 196.6 jit_solution(3199642984276169325)
XLA Ops:
  0.7 55.5 %gather_forward.1 = (bf16[4096,768]{1,0:T(8,128)(2,1)}, f32[512,512]{1,0:T(8,128)}, bf16[4096,256]{1,0:T(8,128)(2,1)}, f32[4096,256]{1,0:T(8,128)}, bf16[4096,10...) custom-call(bf16[4096,256]{1,0:T(8,128)(2,1)} %bitcast.17, ...), custom_call_target="tpu_custom_call" | custom-call | tf_op jit(solution)/shard_map/gather_forward/pallas_call | solution.py:717
  56.2 60.7 %word_section.1 = (bf16[256,512]{1,0:T(8,128)(2,1)}, f32[3,256]{1,0:T(4,128)}, f32[256,512]{1,0:T(8,128)}, f32[256,256]{1,0:T(8,128)}, bf16[2,128,512]{2,1,0:T(8...) custom-call(bf16[256,256]{1,0:T(8,128)(2,1)} %get-tuple-element.81.p, ...), custom_call_target="tpu_custom_call" | custom-call | tf_op jit(solution)/shard_map/word_section/pallas_call | solution.py:1058
  116.9 73.1 %reduce_backward.1 = (f32[4096,256]{1,0:T(8,128)}, bf16[2,2,128,128]{3,2,1,0:T(8,128)(2,1)}, bf16[2,128,256]{2,1,0:T(8,128)(2,1)}, bf16[2,256,128]{2,1,0:T(8,128...) custom-call(bf16[4096,256]{1,0:T(8,128)(2,1)} %bitcast.18, ...), custom_call_target="tpu_custom_call" | custom-call | tf_op jit(solution)/shard_map/reduce_backward/pallas_call | solution.py:1368
  190.0 6.4 %finish.1 = (f32[4096,256]{1,0:T(8,128)}, bf16[256,512]{1,0:T(8,128)(2,1)}, f32[256,512]{1,0:T(8,128)}, f32[3,256]{1,0:T(4,128)}, f32[3,128,128]{2,1,0:T(8,128)}...) custom-call(f32[4096,256]{1,0:T(8,128)} %get-tuple-element.98.cg, ...), custom_call_target="tpu_custom_call" | custom-call | tf_op jit(solution)/shard_map/finish/pallas_call | solution.py:1419

commit v5 on v4

--- a/solution.py
+++ b/solution.py
@@ -531,7 +531,7 @@
 
 
 CHUNKS = ((0, 4), (4, 6), (6, 8))
-LAG = 5
+LAG = 6
 
 
 def gather_fwd_kernel(*refs):
@@ -661,10 +661,10 @@
     when(0, open_)
     when(6, *[p.spread for p in (pj, wa, wb, wo)])
     when(7, zu.begin, zd.begin)
-    when(8, pj.pass_on, lambda: copy_out(0, 1, 2))
-    when(9, lambda: send_rows(0))
-    when(11, wa.pass_on, wb.pass_on, wo.pass_on, lambda: send_rows(1), lambda: copy_out(3))
-    when(12, lambda: pass_rows(0), wa.arrive, wb.arrive, wo.arrive, lambda: copy_out(5, 6), zu.spread, zd.spread, lambda: copy_out(7, 8))
+    when(9, pj.pass_on, lambda: copy_out(0, 1, 2))
+    when(10, lambda: send_rows(0))
+    when(12, wa.pass_on, wb.pass_on, wo.pass_on, lambda: send_rows(1), lambda: copy_out(3))
+    when(13, lambda: pass_rows(0), wa.arrive, wb.arrive, wo.arrive, lambda: copy_out(5, 6), zu.spread, zd.spread, lambda: copy_out(7, 8))
 
     @pl.when(step < tiles)
     def _():
@@ -733,7 +733,7 @@
 def word_kernel(
     pooled, proj, words_in, cot, vec, xin, w3_in, wo_in, zu, zd,
     block_out, rms, words_grad, gpool, d_proj, d_vec, h_w4, h_up, h_down,
-    xall, kk, vv, kt, vt, ss, ee, qm, dom, mx, ll, ot, dqt, wkt, wvt, w3, wout, wup, wdown, dk_acc, dv_acc, dlt, dk_sum, dv_sum,
+    xall, kk, vv, kt, vt, ss, ee, qm, dom, mx, ll, ot, dqt, w3, wout, wup, wdown, dk_acc, dv_acc, dlt, dk_sum, dv_sum,
     dx_in, dx_own, g_up, g_down, g_w4, in_up, in_down, in_w4,
     xlast, w_send, w_recv, g_send, g_recv, rs_send, rs_recv, x_send, x_recv, local_sems,
 ):
@@ -787,8 +787,6 @@
     g1v = vec[3:4, :]
     wq, wk, wv = w3.at[0], w3.at[1], w3.at[2]
     loads[0].wait()
-    wkt[...] = jnp.transpose(wk[...])
-    wvt[...] = jnp.transpose(wv[...])
     loads[1].wait()
     xown = xall[own]
     q = mm(xown, wq[...]).astype(BF16) * BF16(0.125)
@@ -843,44 +841,45 @@
             remote(xin.at[own, pl.ds(lead, tail)], xlast.at[own], (x_send.at[2 * k + 1], x_recv.at[2 * k + 1 + 2 * T * at.c]), None, {"ctx": 1, "tp": at.tp(k)}).start()
 
 
+    for i in range(2):
+        for n in range(2):
+            wide(n, i).start()
+        side(0, i).start()
+        mine(i).start()
+
     def others():
         for k in range(T):
             pl.when((at.c == 0) & (at.t >= k) & (k > 0))(lambda k=k: got_rows(at.t - k, 2 * k))
             pl.when(at.c == 1)(lambda k=k: got_rows(at.tp(-k), 2 * k + 1))
             pl.when((at.c == 1) & (at.t >= k) & (k > 0))(lambda k=k: got_rows(T + at.t - k, 2 * k + 1 + 2 * T))
-        for i in range(2):
-            for n in range(2):
-                wide(n, i).start()
-            side(0, i).start()
-            mine(i).start()
-
-    pl.when(own == 0)(others)
 
     @pl.loop(0, own + 1)
     def _(m):
         pl.when(m == 1)(others)
         j = own - m
         xj = xall[j]
-        kk[j] = mm(xj, wk[...]).astype(BF16)
-        vv[j] = mm(xj, wv[...]).astype(BF16)
-        kt[j] = mm_nt(wkt[...], xj).astype(BF16)
-        vt[j] = mm_nt(wvt[...], xj).astype(BF16)
+        kj = mm(xj, wk[...]).astype(BF16)
+        vj = mm(xj, wv[...]).astype(BF16)
+        kk[j] = kj
+        vv[j] = vj
+        kt[j] = jnp.transpose(kj)
+        vt[j] = jnp.transpose(vj)
         scores_of(j, first)
 
     top_of(first)
-
-    @pl.loop(0, own + 1)
-    def _(j):
-        mix_of(j, first)
-        scores_of(j, second)
-
-    top_of(second)
     for i in range(2):
         for n in range(2):
             wide(n, i, True).wait_recv()
         for n in range(2):
             onward(n, i).start()
             side(1 + n, i).start()
+
+    @pl.loop(0, own + 1)
+    def _(j):
+        mix_of(j, first)
+        scores_of(j, second)
+
+    top_of(second)
 
     @pl.loop(0, own + 1)
     def _(j):
@@ -1048,7 +1047,7 @@
     bufs = [
         ((nblk, blk, width), BF16), ((nblk, blk, width), BF16), ((nblk, blk, width), BF16), ((nblk, width, blk), BF16), ((nblk, width, blk), BF16),
         ((nblk, HEADS // 2, blk, blk), F32), ((nblk, HEADS, blk, blk), BF16), ((HEADS, blk, 128), BF16), ((HEADS, blk, 128), BF16),
-        ((HEADS, 8, blk), F32), ((HEADS, 8, blk), F32), ((width, blk), F32), ((width, blk), F32), ((width, width), BF16), ((width, width), BF16),
+        ((HEADS, 8, blk), F32), ((HEADS, 8, blk), F32), ((width, blk), F32), ((width, blk), F32),
         ((3, width, width), BF16), ((width, width), BF16), ((width, ff), BF16), ((ff, width), BF16), ((blk, width), BF16), ((blk, width), BF16), ((HEADS, 8, blk), F32),
         ((width, width), F32), ((width, width), F32), ((nblk, blk, width), BF16), ((blk, width), F32),
         ((2, width, ff // 2), BF16), ((2, ff // 2, width), BF16), ((2, 2, width, width), BF16), ((width, ff // 2), BF16), ((ff // 2, width), BF16), ((2, width, width), BF16),
@@ -1066,6 +1065,14 @@
     )(pooled, proj, words_in, cot, vec, xall, w3, wo, zu, zd)
 
 
+def sweep(shape, act, rows=32):
+    rows = min(rows, shape[-2])
+
+    @pl.loop(0, shape[-2] // rows)
+    def _(i):
+        act((ALL,) * (len(shape) - 2) + (span(i * rows, rows), ALL))
+
+
 class Sum:
     def __init__(self, at, source, bufs, tp_cut, fs_cut, sems, first, wide, halved):
         self.at, self.source, self.sems, self.first, self.wide, self.halved = at, source, sems, first, wide, halved
@@ -1125,13 +1132,22 @@
         self.swap().start()
 
     def begin(self):
-        self.own[...] = self.source[self.at.c].astype(BF16)
-        self.away[...] = self.source[1 - self.at.c].astype(BF16)
+        near, there = self.source.at[self.at.c], self.source.at[1 - self.at.c]
+
+        def act(r):
+            self.own[r] = near[r].astype(BF16)
+            self.away[r] = there[r].astype(BF16)
+
+        sweep(self.own.shape, act)
         self.swap().start()
 
     def halves(self):
         self.swap().wait_recv()
-        self.own[...] = (self.own[...].astype(F32) + self.got[...].astype(F32)).astype(BF16)
+
+        def act(r):
+            self.own[r] = (self.own[r].astype(F32) + self.got[r].astype(F32)).astype(BF16)
+
+        sweep(self.own.shape, act)
         for k in range(1, self.at.T):
             self.to_tp(k).start()
 
@@ -1168,7 +1184,12 @@
             self.mine(i).wait()
         for n in range(2):
             self.near_send(n, 1).wait_recv()
-            self.hold[2 + n] = (self.hold[2 + n].astype(F32) + self.came[2 * n + 1].astype(F32)).astype(BF16)
+            mine, came = self.hold.at[2 + n], self.came.at[2 * n + 1]
+
+            def act(r, mine=mine, came=came):
+                mine[r] = (mine[r].astype(F32) + came[r].astype(F32)).astype(BF16)
+
+            sweep(mine.shape, act)
         for n in range(2):
             self.onward(n).start()
 
@@ -1177,30 +1198,40 @@
         for i in range(2):
             self.near_send(i, 0).wait_recv()
             self.onward(i).wait_recv()
-            total = self.hold[i].astype(F32) + self.came[2 * i].astype(F32) + self.came[4 + i].astype(F32)
-            self.block[i * n : i * n + n] = total.astype(BF16)
+            terms = (self.hold.at[i], self.came.at[2 * i], self.came.at[4 + i])
+            block = self.block.at[pl.ds(i * n, n)]
+
+            def act(r, terms=terms, block=block):
+                block[r] = sum(v[r].astype(F32) for v in terms).astype(BF16)
+
+            sweep(block.shape, act)
         for k in range(1, self.at.F):
             self.to_fs(k).start()
 
     def over_tp(self):
-        total = self.own[self.tp_cut(self.at.t)].astype(F32)
+        own = self.own.at[self.tp_cut(self.at.t)]
         for k in range(1, self.at.T):
             self.to_tp(k).wait_recv()
-            total += self.blocks[k - 1].astype(F32)
-        self.block[...] = total.astype(BF16)
+        terms = [own] + [self.blocks.at[k - 1] for k in range(1, self.at.T)]
+
+        def act(r):
+            self.block[r] = sum(v[r].astype(F32) for v in terms).astype(BF16)
+
+        sweep(self.block.shape, act)
         for k in range(1, self.at.F):
             self.to_fs(k).start()
 
     def over_fsdp(self):
         at = self.at
-        total = self.block[self.fs_cut(at.f)].astype(F32)
         for k in range(1, at.F):
             self.to_fs(k).wait_recv()
-            total += self.pieces[k - 1].astype(F32)
-        if self.wide:
-            self.done[at.c, at.t] = total.astype(BF16)
-        else:
-            self.done[at.c] = total.astype(BF16)
+        terms = [self.block.at[self.fs_cut(at.f)]] + [self.pieces.at[k - 1] for k in range(1, at.F)]
+        done = self.done.at[at.c, at.t] if self.wide else self.done.at[at.c]
+
+        def act(r):
+            done[r] = sum(v[r].astype(F32) for v in terms).astype(BF16)
+
+        sweep(done.shape, act)
         for k, x in self.shares():
             self.share(k, x).start()
 
@@ -1268,11 +1299,10 @@
     step = pl.program_id(0)
     last = 2 * tiles - 1
 
+    plan = {}
+
     def when(i, *acts):
-        @pl.when(step == i)
-        def _():
-            for act in acts:
-                act()
+        plan.setdefault(i, []).extend(acts)
 
     def open_():
         meet(at.peers())
@@ -1284,9 +1314,14 @@
     when(1, open_)
     when(3, pj.halves)
     when(6, w4.pass_halved, wup.pass_halved, wdn.begin_halved)
-    when(8, up.begin, dn.begin, pj.over_tp)
-    when(11, w4.over_near, wup.over_near, wdn.pass_halved, up.halves, dn.halves, pj.over_fsdp)
-    when(15, wdn.over_near, up.over_tp, dn.over_tp)
+    when(8, lambda: vec_begin(), up.begin, dn.begin, pj.over_tp, w4.over_near)
+    when(9, lambda: vec_plane(), wup.over_near)
+    when(10, wdn.pass_halved, up.halves, dn.halves, pj.over_fsdp)
+    when(11, lambda: vec_depth())
+    when(13, w4.over_fsdp)
+    when(13, wdn.over_near)
+    when(14, up.over_tp, dn.over_tp, wup.over_fsdp)
+
     def vec_copy(i, where):
         return remote(a_vec, vec_in.at[i], (vsend, vrecv), i, where)
 
@@ -1319,24 +1354,33 @@
             rows.append(v if n == 128 else jnp.concatenate([v, jnp.zeros((1, n), F32)], axis=1))
         vec_out[...] = jnp.concatenate(rows + [jnp.zeros((3, 128), F32)], axis=0)
 
-    when(8, vec_begin)
-    when(10, vec_plane)
-    when(12, vec_depth)
-    when(14, vec_end)
+    busy = functools.reduce(lambda a, b: a | b, [step == i for i in plan])
+
+    @pl.when(busy)
+    def _():
+        for i, acts in plan.items():
+
+            @pl.when(step == i)
+            def _():
+                for act in acts:
+                    act()
+
     char_back_step(step, tiles, ins, cg, gca, accs, False)
 
     @pl.when(step == last)
     def _():
         qo.begin()
-        w4.over_fsdp()
-        wup.over_fsdp()
         qo.halves()
+
+        def result(i):
+            return pltpu.make_async_copy(sums[i].done, results[i], local_sems.at[i, 0])
 
         def keep(*which):
             for i in which:
                 sums[i].finish()
-                results[i][...] = sums[i].done[...]
-
+                result(i).start()
+
+        vec_end()
         keep(0, 1, 3)
         qo.over_tp()
         up.over_fsdp()
@@ -1348,6 +1392,8 @@
             s.drain()
         keep(6)
         qo.drain()
+        for i in range(len(sums)):
+            result(i).wait()
 
 
 def reduce_backward(x, cnt, saved, gpool, weights, sources, d_vec):
@@ -1369,7 +1415,7 @@
         functools.partial(reduce_bwd_kernel, tiles),
         grid=(2 * tiles,),
         in_specs=ins + [any_] * len(sources) + [full_spec((8, 512))],
-        out_specs=[out] + [full_spec(s) for s in results] + [full_spec((8, 128))],
+        out_specs=[out] + [any_] * len(results) + [full_spec((8, 128))],
         out_shape=[jax.ShapeDtypeStruct((total, 256), F32)] + [jax.ShapeDtypeStruct(s, BF16) for s in results] + [jax.ShapeDtypeStruct((8, 128), F32)],
         scratch_shapes=scratch,
         compiler_params=pltpu.CompilerParams(vmem_limit_bytes=VMEM_LIMIT, collective_id=2, has_side_effects=True, dimension_semantics=("arbitrary",)),
@@ -1413,7 +1459,7 @@
 
 
 def finish(cg, block, grad, rms, parts):
-    tiles = 4
+    tiles = 2
     rows = cg.shape[0] // tiles
     small = [block, grad, rms] + list(parts)
     return pl.pallas_call(

time: 197 us -> 188 us (0.954)
  Pallas kernels: 196 us -> 186 us
    pallas_call x1, Pallas kernels: 60.7 us -> 57.7 us  [word_section(): pl.pallas_call(word_kernel, in_specs=[vm] * 5 + [any_] * 5, out_specs=[vm...]
    pallas_call x1, Pallas kernels: 55.5 us -> 52.7 us  [gather_forward(): pl.pallas_call(gather_fwd_kernel, grid=(tiles + LAG,), in_specs=[early(RO...]
    pallas_call x1, Pallas kernels: 73.1 us -> 70.7 us  [reduce_backward(): pl.pallas_call(functools.partial(reduce_bwd_kernel, tiles), grid=(2 * til...]
where the time goes in v5:
time: 188 us; the launch traced here: 187 us
  Pallas kernels  186 us (99%)
    pallas_call x1, Pallas kernels, reduce_backward(): pl.pallas_call(functools.partial(reduce_bwd_kernel, tiles), grid=(2 * til...  70.7 us
    pallas_call x1, Pallas kernels, word_section(): pl.pallas_call(word_kernel, in_specs=[vm] * 5 + [any_] * 5, out_specs=[vm...  57.7 us
    pallas_call x1, Pallas kernels, gather_forward(): pl.pallas_call(gather_fwd_kernel, grid=(tiles + LAG,), in_specs=[early(RO...  52.7 us
    pallas_call x1, Pallas kernels, finish(): pl.pallas_call(final_kernel, grid=(tiles,), in_specs=[rows_spec(rows, cg....  5.38 us

profile of v5, /device:TPU:0, one launch (start us, length us, event | category | flops | bytes accessed | tf_op | source)
XLA Modules:
  0.0 187.4 jit_solution(7411641629283380605)
XLA Ops:
  0.7 52.7 %gather_forward.1 = (bf16[4096,768]{1,0:T(8,128)(2,1)}, f32[512,512]{1,0:T(8,128)}, bf16[4096,256]{1,0:T(8,128)(2,1)}, f32[4096,256]{1,0:T(8,128)}, bf16[4096,10...) custom-call(bf16[4096,256]{1,0:T(8,128)(2,1)} %bitcast.17, ...), custom_call_target="tpu_custom_call" | custom-call | tf_op jit(solution)/shard_map/gather_forward/pallas_call | solution.py:717
  53.3 57.7 %word_section.1 = (bf16[256,512]{1,0:T(8,128)(2,1)}, f32[3,256]{1,0:T(4,128)}, f32[256,512]{1,0:T(8,128)}, f32[256,256]{1,0:T(8,128)}, bf16[2,128,512]{2,1,0:T(8...) custom-call(bf16[256,256]{1,0:T(8,128)(2,1)} %get-tuple-element.81.p, ...), custom_call_target="tpu_custom_call" | custom-call | tf_op jit(solution)/shard_map/word_section/pallas_call | solution.py:1057
  111.0 70.7 %reduce_backward.1 = (f32[4096,256]{1,0:T(8,128)}, bf16[2,2,128,128]{3,2,1,0:T(8,128)(2,1)}, bf16[2,128,256]{2,1,0:T(8,128)(2,1)}, bf16[2,256,128]{2,1,0:T(8,128...) custom-call(bf16[4096,256]{1,0:T(8,128)(2,1)} %bitcast.18, ...), custom_call_target="tpu_custom_call" | custom-call | tf_op jit(solution)/shard_map/reduce_backward/pallas_call | solution.py:1414
  181.8 5.4 %finish.1 = (f32[4096,256]{1,0:T(8,128)}, bf16[256,512]{1,0:T(8,128)(2,1)}, f32[256,512]{1,0:T(8,128)}, f32[3,256]{1,0:T(4,128)}, f32[3,128,128]{2,1,0:T(8,128)}...) custom-call(f32[4096,256]{1,0:T(8,128)} %get-tuple-element.98.cg, ...), custom_call_target="tpu_custom_call" | custom-call | tf_op jit(solution)/shard_map/finish/pallas_call | solution.py:1465

commit v6 on v5

--- a/solution.py
+++ b/solution.py
@@ -478,7 +478,7 @@
         (None, wholes[0], *cols, dict(source=qo_source)),
         (up, wholes[1], *cols, {}),
         (dn, wholes[2], lambda c, t: (span(quarter * t, quarter), span(128 * c, 128)), lambda f, c, t: (f, span(quarter * t, quarter), span(128 * c, 128)), lambda c, t: (ALL, span(quarter * t, quarter), span(128 * c, 128)), {}),
-        (pj, wholes[3], lambda c, t: (ALL, span(128 * t, 128)), lambda f, c, t: (span(f * rq, rq), span(128 * t, 128)), lambda c, t: (ALL, span(128 * t, 128)), dict(side=False)),
+        (pj, wholes[3], lambda c, t: (ALL, span(128 * t, 128)), lambda f, c, t: (span(f * rq, rq), span(128 * t, 128)), lambda c, t: (ALL, span(128 * t, 128)), dict(core=0)),
         (sm, wholes[4], lambda c, t: (ALL, ALL), lambda f, c, t: (f,), None, dict(side=False)),
         (w3, wholes[5], lambda c, t: (span(0, 2),), lambda f, c, t: (span(0, 2), span(f * rw, rw), span(128 * t, 128)), lambda c, t: (span(0, 2), ALL, span(128 * t, 128)), dict(core=0)),
         (w3, wholes[5], lambda c, t: (pl.ds(2, 1),), lambda f, c, t: (pl.ds(2, 1), span(f * rw, rw), span(128 * t, 128)), lambda c, t: (pl.ds(2, 1), ALL, span(128 * t, 128)), dict(core=1)),
@@ -661,7 +661,8 @@
     when(0, open_)
     when(6, *[p.spread for p in (pj, wa, wb, wo)])
     when(7, zu.begin, zd.begin)
-    when(9, pj.pass_on, lambda: copy_out(0, 1, 2))
+    when(8, pj.pass_on)
+    when(9, pj.arrive, lambda: copy_out(0, 1, 2))
     when(10, lambda: send_rows(0))
     when(12, wa.pass_on, wb.pass_on, wo.pass_on, lambda: send_rows(1), lambda: copy_out(3))
     when(13, lambda: pass_rows(0), wa.arrive, wb.arrive, wo.arrive, lambda: copy_out(5, 6), zu.spread, zd.spread, lambda: copy_out(7, 8))

time: 188 us -> 187 us (level)
  no operation moved by 1% of the time
where the time goes in v6:
time: 187 us
  Pallas kernels  186 us (99%)
    pallas_call x1, Pallas kernels, reduce_backward(): pl.pallas_call(functools.partial(reduce_bwd_kernel, tiles), grid=(2 * til...  70.9 us
    pallas_call x1, Pallas kernels, word_section(): pl.pallas_call(word_kernel, in_specs=[vm] * 5 + [any_] * 5, out_specs=[vm...  58.7 us
    pallas_call x1, Pallas kernels, gather_forward(): pl.pallas_call(gather_fwd_kernel, grid=(tiles + LAG,), in_specs=[early(RO...  51.2 us
    pallas_call x1, Pallas kernels, finish(): pl.pallas_call(final_kernel, grid=(tiles,), in_specs=[rows_spec(rows, cg....  5.38 us

profile of v6, /device:TPU:0, one launch (start us, length us, event | category | flops | bytes accessed | tf_op | source)
XLA Modules:
  0.0 187.0 jit_solution(15294699770271788707)
XLA Ops:
  0.7 51.2 %gather_forward.1 = (bf16[4096,768]{1,0:T(8,128)(2,1)}, f32[512,512]{1,0:T(8,128)}, bf16[4096,256]{1,0:T(8,128)(2,1)}, f32[4096,256]{1,0:T(8,128)}, bf16[4096,10...) custom-call(bf16[4096,256]{1,0:T(8,128)(2,1)} %bitcast.17, ...), custom_call_target="tpu_custom_call" | custom-call | tf_op jit(solution)/shard_map/gather_forward/pallas_call | solution.py:718
  51.8 58.7 %word_section.1 = (bf16[256,512]{1,0:T(8,128)(2,1)}, f32[3,256]{1,0:T(4,128)}, f32[256,512]{1,0:T(8,128)}, f32[256,256]{1,0:T(8,128)}, bf16[2,128,512]{2,1,0:T(8...) custom-call(bf16[256,256]{1,0:T(8,128)(2,1)} %get-tuple-element.81.p, ...), custom_call_target="tpu_custom_call" | custom-call | tf_op jit(solution)/shard_map/word_section/pallas_call | solution.py:1058
  110.5 70.9 %reduce_backward.1 = (f32[4096,256]{1,0:T(8,128)}, bf16[2,2,128,128]{3,2,1,0:T(8,128)(2,1)}, bf16[2,128,256]{2,1,0:T(8,128)(2,1)}, bf16[2,256,128]{2,1,0:T(8,128...) custom-call(bf16[4096,256]{1,0:T(8,128)(2,1)} %bitcast.18, ...), custom_call_target="tpu_custom_call" | custom-call | tf_op jit(solution)/shard_map/reduce_backward/pallas_call | solution.py:1415
  181.4 5.4 %finish.1 = (f32[4096,256]{1,0:T(8,128)}, bf16[256,512]{1,0:T(8,128)(2,1)}, f32[256,512]{1,0:T(8,128)}, f32[3,256]{1,0:T(4,128)}, f32[3,128,128]{2,1,0:T(8,128)}...) custom-call(f32[4096,256]{1,0:T(8,128)} %get-tuple-element.98.cg, ...), custom_call_target="tpu_custom_call" | custom-call | tf_op jit(solution)/shard_map/finish/pallas_call | solution.py:1466
